TPU v7x, 32 devices: a whole 2x2x4 slice. The times are simulated.
32 devices in a mesh: dp: 8 (over z, y), cp: 4 (over x, core).
Axes of the slice: x: 2, y: 2, z: 4, core: 2. Of those that a mesh axis runs over, the one named last changes fastest.
Arguments:
- x_in: bfloat16 [8, 4096, 1024], P('dp', 'cp')
- d_out: bfloat16 [8, 4096, 1024], P('dp', 'cp')
- w_q: bfloat16 [1024, 16, 64], replicated
- w_k: bfloat16 [1024, 16, 64], replicated
- w_v: bfloat16 [1024, 16, 64], replicated
- w_o: bfloat16 [16, 64, 1024], replicated
- w_up: bfloat16 [1024, 4096], replicated
- w_down: bfloat16 [4096, 1024], replicated
Outputs:
- output 1: bfloat16 [8, 4096, 1024], P('dp', 'cp')
- output 2: float32 [1024, 16, 64], replicated
- output 3: float32 [1024, 16, 64], replicated
- output 4: float32 [1024, 16, 64], replicated
- output 5: float32 [16, 64, 1024], replicated
- output 6: float32 [1024, 4096], replicated
- output 7: float32 [4096, 1024], replicated
All inputs are finite; a program needn't handle non-finite values.
Results may differ from a plain program's by a relative error of at most 0.0176615.
Values are sent between devices in bfloat16 or wider.
A program may use at most 1 GiB of HBM per device.

v0:
```python
import functools
import jax
import jax.numpy as jnp
from jax import lax
from jax.sharding import PartitionSpec as P

NEG_BIG = -1e30


def causal_keep(size_len):
    offsets = jnp.arange(size_len)
    return offsets[:, None] >= offsets[None, :]


def block_forward(carry_state, q_rows, key_blk, val_blk, causal):
    row_max, row_sum, acc_out = carry_state
    score_scale = q_rows.shape[-1] ** -0.5
    scores = jnp.einsum('bqhe,bkhe->bhqk', q_rows, key_blk, preferred_element_type=jnp.float32) * score_scale
    if causal:
        scores = jnp.where(causal_keep(q_rows.shape[1]), scores, NEG_BIG)
    new_max = jnp.maximum(row_max, jnp.max(scores, axis=-1))
    factor = jnp.exp(row_max - new_max)
    prob_f = jnp.exp(scores - new_max[..., None])
    row_sum = row_sum * factor + jnp.sum(prob_f, axis=-1)
    acc_out = acc_out * factor[..., None] + jnp.einsum('bhqk,bkhe->bhqe', prob_f.astype(jnp.bfloat16), val_blk, preferred_element_type=jnp.float32)
    return new_max, row_sum, acc_out


def block_backward(q_rows, grad_rows, lse_rows, dot_rows, key_blk, val_blk, causal):
    score_scale = q_rows.shape[-1] ** -0.5
    scores = jnp.einsum('bqhe,bkhe->bhqk', q_rows, key_blk, preferred_element_type=jnp.float32) * score_scale
    if causal:
        scores = jnp.where(causal_keep(q_rows.shape[1]), scores, NEG_BIG)
    prob_f = jnp.exp(scores - lse_rows[..., None])
    grad_val = jnp.einsum('bhqk,bhqe->bkhe', prob_f.astype(jnp.bfloat16), grad_rows, preferred_element_type=jnp.float32)
    grad_prob = jnp.einsum('bhqe,bkhe->bhqk', grad_rows, val_blk, preferred_element_type=jnp.float32).astype(jnp.bfloat16)
    grad_score = (prob_f * (grad_prob.astype(jnp.float32) - dot_rows[..., None]) * score_scale).astype(jnp.bfloat16)
    grad_query = jnp.einsum('bhqk,bkhe->bhqe', grad_score, key_blk, preferred_element_type=jnp.float32)
    grad_key = jnp.einsum('bhqk,bqhe->bkhe', grad_score, q_rows, preferred_element_type=jnp.float32)
    return grad_query, grad_key, grad_val


def solution(mesh):
    cp_size = mesh.shape['cp']
    n_total = mesh.shape['dp'] * cp_size
    shift_pairs = [(rank_id, (rank_id + 1) % cp_size) for rank_id in range(cp_size)]

    def rotate(tree):
        return jax.tree.map(lambda tensor: lax.ppermute(tensor, 'cp', shift_pairs), tree)

    def per_device(x_in, d_out, w_q, w_k, w_v, w_o, w_up, w_down):
        my_rank = lax.axis_index('cp')
        batch_local, seq_local, d_model = x_in.shape
        half_len = seq_local // 2
        n_heads, head_dim = w_q.shape[1], w_q.shape[2]
        q_proj = jnp.einsum('bsd,dhe->bshe', x_in, w_q, preferred_element_type=jnp.float32).astype(jnp.bfloat16)
        k_proj = jnp.einsum('bsd,dhe->bshe', x_in, w_k, preferred_element_type=jnp.float32).astype(jnp.bfloat16)
        v_proj = jnp.einsum('bsd,dhe->bshe', x_in, w_v, preferred_element_type=jnp.float32).astype(jnp.bfloat16)
        q_low, q_high = q_proj[:, :half_len], q_proj[:, half_len:]
        key_own_a, key_own_b = k_proj[:, :half_len], k_proj[:, half_len:]
        val_own_a, val_own_b = v_proj[:, :half_len], v_proj[:, half_len:]

        def fresh_state():
            return (jnp.full((batch_local, n_heads, half_len), NEG_BIG, jnp.float32),
                    jnp.zeros((batch_local, n_heads, half_len), jnp.float32),
                    jnp.zeros((batch_local, n_heads, half_len, head_dim), jnp.float32))

        state_low = block_forward(fresh_state(), q_low, key_own_a, val_own_a, True)
        state_high = block_forward(fresh_state(), q_high, key_own_a, val_own_a, False)
        state_high = block_forward(state_high, q_high, key_own_b, val_own_b, True)

        def forward_step(step_idx, loop_carry):
            key_val, state_low, state_high = loop_carry
            key_val = rotate(key_val)
            key_all, val_all = key_val
            key_first, key_second = key_all[:, :half_len], key_all[:, half_len:]
            val_first, val_second = val_all[:, :half_len], val_all[:, half_len:]
            src_rank = (my_rank - step_idx) % cp_size

            def from_lower(states):
                return (block_forward(states[0], q_low, key_first, val_first, False),
                        block_forward(states[1], q_high, key_first, val_first, False))

            def from_higher(states):
                mid_state = block_forward(states[1], q_high, key_first, val_first, False)
                return (states[0], block_forward(mid_state, q_high, key_second, val_second, False))

            state_low, state_high = lax.cond(src_rank < my_rank, from_lower, from_higher, (state_low, state_high))
            return key_val, state_low, state_high

        fwd_result = lax.fori_loop(1, cp_size, forward_step, ((k_proj, v_proj), state_low, state_high))
        state_low, state_high = fwd_result[1], fwd_result[2]
        attn_out = jnp.concatenate([state_low[2] / state_low[1][..., None],
                                    state_high[2] / state_high[1][..., None]], axis=2).astype(jnp.bfloat16)
        lse_low = state_low[0] + jnp.log(state_low[1])
        lse_high = state_high[0] + jnp.log(state_high[1])

        hidden = (x_in.astype(jnp.float32) + jnp.einsum('bhse,hed->bsd', attn_out, w_o, preferred_element_type=jnp.float32)).astype(jnp.bfloat16)
        up_pre = jnp.einsum('bsd,df->bsf', hidden, w_up, preferred_element_type=jnp.float32).astype(jnp.bfloat16)
        act_val, gelu_pull = jax.vjp(functools.partial(jax.nn.gelu, approximate=True), up_pre.astype(jnp.float32))
        act_b = act_val.astype(jnp.bfloat16)
        grad_down = jnp.einsum('bsf,bsd->fd', act_b, d_out, preferred_element_type=jnp.float32)
        grad_act = jnp.einsum('bsd,fd->bsf', d_out, w_down, preferred_element_type=jnp.float32).astype(jnp.bfloat16)
        grad_pre = gelu_pull(grad_act.astype(jnp.float32))[0].astype(jnp.bfloat16)
        grad_up = jnp.einsum('bsd,bsf->df', hidden, grad_pre, preferred_element_type=jnp.float32)
        grad_hidden = (d_out.astype(jnp.float32) + jnp.einsum('bsf,df->bsd', grad_pre, w_up, preferred_element_type=jnp.float32)).astype(jnp.bfloat16)
        grad_o = jnp.einsum('bhse,bsd->hed', attn_out, grad_hidden, preferred_element_type=jnp.float32)
        grad_attn = jnp.einsum('bsd,hed->bhse', grad_hidden, w_o, preferred_element_type=jnp.float32).astype(jnp.bfloat16)
        row_dot = jnp.sum(grad_attn.astype(jnp.float32) * attn_out.astype(jnp.float32), axis=-1)
        grad_low, grad_high = grad_attn[:, :, :half_len], grad_attn[:, :, half_len:]
        dot_low, dot_high = row_dot[:, :, :half_len], row_dot[:, :, half_len:]

        part_a = block_backward(q_low, grad_low, lse_low, dot_low, key_own_a, val_own_a, True)
        part_b = block_backward(q_high, grad_high, lse_high, dot_high, key_own_a, val_own_a, False)
        part_c = block_backward(q_high, grad_high, lse_high, dot_high, key_own_b, val_own_b, True)
        kv_grads = (part_a[1] + part_b[1], part_c[1], part_a[2] + part_b[2], part_c[2])
        dq_low = part_a[0]
        dq_high = part_b[0] + part_c[0]

        def backward_step(step_idx, loop_carry):
            key_val, kv_grads, dq_low, dq_high = loop_carry
            key_val = rotate(key_val)
            kv_grads = rotate(kv_grads)
            key_all, val_all = key_val
            key_first, key_second = key_all[:, :half_len], key_all[:, half_len:]
            val_first, val_second = val_all[:, :half_len], val_all[:, half_len:]
            src_rank = (my_rank - step_idx) % cp_size

            def from_lower(operand):
                grad_acc, acc_low, acc_high = operand
                low_part = block_backward(q_low, grad_low, lse_low, dot_low, key_first, val_first, False)
                high_part = block_backward(q_high, grad_high, lse_high, dot_high, key_first, val_first, False)
                return ((grad_acc[0] + low_part[1] + high_part[1], grad_acc[1],
                         grad_acc[2] + low_part[2] + high_part[2], grad_acc[3]),
                        acc_low + low_part[0], acc_high + high_part[0])

            def from_higher(operand):
                grad_acc, acc_low, acc_high = operand
                first_part = block_backward(q_high, grad_high, lse_high, dot_high, key_first, val_first, False)
                second_part = block_backward(q_high, grad_high, lse_high, dot_high, key_second, val_second, False)
                return ((grad_acc[0] + first_part[1], grad_acc[1] + second_part[1],
                         grad_acc[2] + first_part[2], grad_acc[3] + second_part[2]),
                        acc_low, acc_high + first_part[0] + second_part[0])

            kv_grads, dq_low, dq_high = lax.cond(src_rank < my_rank, from_lower, from_higher, (kv_grads, dq_low, dq_high))
            return key_val, kv_grads, dq_low, dq_high

        bwd_result = lax.fori_loop(1, cp_size, backward_step, ((k_proj, v_proj), kv_grads, dq_low, dq_high))
        kv_grads = rotate(bwd_result[1])
        grad_query = jnp.concatenate([bwd_result[2], bwd_result[3]], axis=2).astype(jnp.bfloat16)
        grad_key = jnp.concatenate([kv_grads[0], kv_grads[1]], axis=1).astype(jnp.bfloat16)
        grad_value = jnp.concatenate([kv_grads[2], kv_grads[3]], axis=1).astype(jnp.bfloat16)
        grad_q_w = jnp.einsum('bsd,bhse->dhe', x_in, grad_query, preferred_element_type=jnp.float32)
        grad_k_w = jnp.einsum('bsd,bshe->dhe', x_in, grad_key, preferred_element_type=jnp.float32)
        grad_v_w = jnp.einsum('bsd,bshe->dhe', x_in, grad_value, preferred_element_type=jnp.float32)
        d_x = (grad_hidden.astype(jnp.float32)
               + jnp.einsum('bhse,dhe->bsd', grad_query, w_q, preferred_element_type=jnp.float32)
               + jnp.einsum('bshe,dhe->bsd', grad_key, w_k, preferred_element_type=jnp.float32)
               + jnp.einsum('bshe,dhe->bsd', grad_value, w_v, preferred_element_type=jnp.float32)).astype(jnp.bfloat16)
        summed = lax.psum((grad_q_w, grad_k_w, grad_v_w, grad_o, grad_up, grad_down), ('dp', 'cp'))
        return (d_x,) + tuple(item / n_total for item in summed)

    act_spec = P('dp', 'cp', None)
    return jax.shard_map(per_device, mesh=mesh,
                         in_specs=(act_spec, act_spec, P(), P(), P(), P(), P(), P()),
                         out_specs=(act_spec, P(), P(), P(), P(), P(), P()),
                         check_vma=False)
```

profile of v0, /device:TPU:0, one launch (start us, length us, event | category | flops | bytes accessed | tf_op | source)
XLA Modules:
  0.0 2218.9 jit_solution(9200584962782910615)
XLA Ops:
  52.8 10.3 fusion.154
  72.7 10.5 add_bitcast_fusion.4
  99.5 11.1 add_bitcast_fusion.3
  110.6 347.5 %while.58 = (s32[]{:T(128)}, bf16[1,1024,16,64]{1,3,2,0:T(8,128)(2,1)}, bf16[1,1024,16,64]{1,3,2,0:T(8,128)(2,1)}, f32[1,16,512]{2,1,0:T(8,128)S(1)}, f32[1,16,5...) while((s32[]{:T(128)}, ...), condition=%wide.region_17.18_spmd, body=%wide.region_6.17_spmd.sunk | while | flops 2216747008 | bytes 156500608 | solution.py:91
  113.9 23.0 %collective-permute-done = bf16[1,1024,16,64]{1,3,2,0:T(8,128)(2,1)} collective-permute-done((bf16[1,1024,16,64]{1,3,2,0:T(8,128)(2,1)}, bf16[1,1024,16,64]{1,3,2,0:T(8,128)(2,1)}, u32[]{:S(2)}, u32[]{:S(2)}) %collective-permute-start) | collective-permute-done | bytes 2097184 | tf_op jit(solution)/shard_map/while/body/eval_jaxpr/ppermute | solution.py:49
  139.2 20.2 collective-permute-done.1
  161.7 35.6 %conditional.4 = (f32[1,16,512]{2,1,0:T(8,128)S(1)}, f32[1,16,512]{2,1,0:T(8,128)S(1)}, f32[1,16,512,64]{3,2,1,0:T(8,128)}, f32[1,16,512]{2,1,0:T(8,128)S(1)}, f...) conditional(s32[]{:T(128)} %convert_element_type.448, (bf16[1,512,16,64]{1,3,2,0:T(8,128)(2,1)S(1)}, ...), branch_computations={%region_7.11_spmd, %region_12.16_spmd} | conditional | flops 2216747008 | bytes 127074408 | solution.py:88
  165.3 9.4 multiply_reduce_fusion
  203.6 33.8 %collective-permute-start = (bf16[1,1024,16,64]{1,3,2,0:T(8,128)(2,1)}, bf16[1,1024,16,64]{1,3,2,0:T(8,128)(2,1)}, u32[]{:S(2)}, u32[]{:S(2)}) collective-permute-start(bf16[1,1024,16,64]{1,3,2,0:T(8,128)(2,1)} %get-tuple-element.1458), channel_id=1, source_target_pairs={{0,1},{1,2},{2,3},{3,0},{4,5},{5,6},{6,7},{7,4},{8,9},{9,10},{10,1... | collective-permute-start | bytes 6291464 | tf_op jit(solution)/shard_map/while/body/eval_jaxpr/ppermute | solution.py:49
  239.9 20.5 collective-permute-done
  262.7 20.2 collective-permute-done.1
  285.2 35.6 %conditional.4 = (f32[1,16,512]{2,1,0:T(8,128)S(1)}, f32[1,16,512]{2,1,0:T(8,128)S(1)}, f32[1,16,512,64]{3,2,1,0:T(8,128)}, f32[1,16,512]{2,1,0:T(8,128)S(1)}, f...) conditional(s32[]{:T(128)} %convert_element_type.448, (bf16[1,512,16,64]{1,3,2,0:T(8,128)(2,1)S(1)}, ...), branch_computations={%region_7.11_spmd, %region_12.16_spmd} | conditional | flops 2216747008 | bytes 127074408 | solution.py:88
  288.8 9.4 multiply_reduce_fusion
  329.4 36.4 %collective-permute-start.1 = (bf16[1,1024,16,64]{1,3,2,0:T(8,128)(2,1)}, bf16[1,1024,16,64]{1,3,2,0:T(8,128)(2,1)}, u32[]{:S(2)}, u32[]{:S(2)}) collective-permute-start(bf16[1,1024,16,64]{1,3,2,0:T(8,128)(2,1)} %get-tuple-element.1459), channel_id=1, source_target_pairs={{0,1},{1,2},{2,3},{3,0},{4,5},{5,6},{6,7},{7,4},{8,9},{9,10},{10,1... | collective-permute-start | bytes 6291464 | tf_op jit(solution)/shard_map/while/body/eval_jaxpr/ppermute | solution.py:49
  365.8 18.0 collective-permute-done
  386.1 20.2 collective-permute-done.1
  408.6 35.6 %conditional.4 = (f32[1,16,512]{2,1,0:T(8,128)S(1)}, f32[1,16,512]{2,1,0:T(8,128)S(1)}, f32[1,16,512,64]{3,2,1,0:T(8,128)}, f32[1,16,512]{2,1,0:T(8,128)S(1)}, f...) conditional(s32[]{:T(128)} %convert_element_type.448, (bf16[1,512,16,64]{1,3,2,0:T(8,128)(2,1)S(1)}, ...), branch_computations={%region_7.11_spmd, %region_12.16_spmd} | conditional | flops 2216747008 | bytes 127074408 | solution.py:88
  412.2 9.4 multiply_reduce_fusion
  472.1 10.9 convolution_convert_fusion
  483.0 22.6 %fusion.129 = bf16[1024,4096]{1,0:T(8,128)(2,1)} fusion(bf16[1024,4096]{1,0:T(8,128)(2,1)} %convolution_convert_fusion, bf16[4096,1024]{1,0:T(8,128)(2,1)} %param.23, bf16[1,1024,1024]{2,1,0:T(8,128)(2,1)S(1)} %copy-done.43), kind=kOutput, calls=%fused_computation.159 | convolution fusion | flops 8686403584 | bytes 27262976 | tf_op jit(solution)/shard_map/bsd,fd->bsf/dot_general | solution.py:103
  505.6 14.0 fusion.173
  522.2 11.1 multiply_convert_fusion.5
  533.3 10.7 multiply_convert_fusion.4
  544.0 9.8 fusion.195
  553.9 9.8 fusion.152
  604.9 11.0 add_bitcast_fusion.1
  629.0 755.5 %while.59 = (s32[]{:T(128)}, bf16[1,1024,16,64]{1,3,2,0:T(8,128)(2,1)}, bf16[1,1024,16,64]{1,3,2,0:T(8,128)(2,1)}, f32[1,512,16,64]{1,3,2,0:T(8,128)}, f32[1,512...) while((s32[]{:T(128)}, ...), condition=%wide.region_22.23_spmd, body=%wide.region_19.22_spmd.sunk | while | flops 5464129536 | bytes 442696960 | solution.py:148
  662.6 26.2 %collective-permute-start.5 = (f32[1,512,16,64]{1,3,2,0:T(8,128)}, f32[1,512,16,64]{1,3,2,0:T(8,128)}, u32[]{:S(2)}, u32[]{:S(2)}) collective-permute-start(f32[1,512,16,64]{1,3,2,0:T(8,128)} %copy.104), channel_id=1, source_target_pairs={{0,1},{1,2},{2,3},{3,0},{4,5},{5,6},{6,7},{7,4},{8,9},{9,10},{10,1... | collective-permute-start | bytes 6291464 | tf_op jit(solution)/shard_map/while/body/eval_jaxpr/ppermute | solution.py:49
  692.7 15.5 collective-permute-done.2
  709.6 21.1 collective-permute-done.3
  731.9 21.2 collective-permute-done.5
  753.1 22.5 %collective-permute-done.7 = f32[1,512,16,64]{1,3,2,0:T(8,128)} collective-permute-done((f32[1,512,16,64]{1,3,2,0:T(8,128)}, f32[1,512,16,64]{1,3,2,0:T(8,128)}, u32[]{:S(2)}, u32[]{:S(2)}) %collective-permute-start.7) | collective-permute-done | bytes 2097184 | tf_op jit(solution)/shard_map/while/body/eval_jaxpr/ppermute | solution.py:49
  775.6 22.5 %collective-permute-done.4 = f32[1,512,16,64]{1,3,2,0:T(8,128)} collective-permute-done((f32[1,512,16,64]{1,3,2,0:T(8,128)}, f32[1,512,16,64]{1,3,2,0:T(8,128)}, u32[]{:S(2)}, u32[]{:S(2)}) %collective-permute-start.4) | collective-permute-done | bytes 2097184 | tf_op jit(solution)/shard_map/while/body/eval_jaxpr/ppermute | solution.py:49
  798.1 22.5 %collective-permute-done.6 = f32[1,512,16,64]{1,3,2,0:T(8,128)} collective-permute-done((f32[1,512,16,64]{1,3,2,0:T(8,128)}, f32[1,512,16,64]{1,3,2,0:T(8,128)}, u32[]{:S(2)}, u32[]{:S(2)}) %collective-permute-start.6) | collective-permute-done | bytes 2097184 | tf_op jit(solution)/shard_map/while/body/eval_jaxpr/ppermute | solution.py:49
  820.5 87.4 %conditional.5 = (f32[1,512,16,64]{1,3,2,0:T(8,128)}, f32[1,512,16,64]{3,2,1,0:T(8,128)}, f32[1,512,16,64]{1,3,2,0:T(8,128)}, f32[1,512,16,64]{3,2,1,0:T(8,128)}...) conditional(s32[]{:T(128)} %convert_element_type.449, (bf16[1,512,16,64]{1,3,2,0:T(8,128)(2,1)S(1)}, ...), branch_computations={%region_20.20_spmd, %region_21.21_spmd} | conditional | flops 5464129536 | bytes 367198656 | solution.py:145
  842.0 9.8 fusion.75
  851.7 9.3 multiply_convert_fusion
  883.6 9.6 bitcast_add_fusion.8
  898.0 9.9 bitcast_add_fusion.9
  924.1 15.6 collective-permute-done.2
  941.1 21.1 collective-permute-done.3
  963.4 21.2 collective-permute-done.5
  984.6 22.5 %collective-permute-done.7 = f32[1,512,16,64]{1,3,2,0:T(8,128)} collective-permute-done((f32[1,512,16,64]{1,3,2,0:T(8,128)}, f32[1,512,16,64]{1,3,2,0:T(8,128)}, u32[]{:S(2)}, u32[]{:S(2)}) %collective-permute-start.7) | collective-permute-done | bytes 2097184 | tf_op jit(solution)/shard_map/while/body/eval_jaxpr/ppermute | solution.py:49
  1007.1 22.5 %collective-permute-done.4 = f32[1,512,16,64]{1,3,2,0:T(8,128)} collective-permute-done((f32[1,512,16,64]{1,3,2,0:T(8,128)}, f32[1,512,16,64]{1,3,2,0:T(8,128)}, u32[]{:S(2)}, u32[]{:S(2)}) %collective-permute-start.4) | collective-permute-done | bytes 2097184 | tf_op jit(solution)/shard_map/while/body/eval_jaxpr/ppermute | solution.py:49
  1029.5 22.5 %collective-permute-done.6 = f32[1,512,16,64]{1,3,2,0:T(8,128)} collective-permute-done((f32[1,512,16,64]{1,3,2,0:T(8,128)}, f32[1,512,16,64]{1,3,2,0:T(8,128)}, u32[]{:S(2)}, u32[]{:S(2)}) %collective-permute-start.6) | collective-permute-done | bytes 2097184 | tf_op jit(solution)/shard_map/while/body/eval_jaxpr/ppermute | solution.py:49
  1052.0 87.4 %conditional.5 = (f32[1,512,16,64]{1,3,2,0:T(8,128)}, f32[1,512,16,64]{3,2,1,0:T(8,128)}, f32[1,512,16,64]{1,3,2,0:T(8,128)}, f32[1,512,16,64]{3,2,1,0:T(8,128)}...) conditional(s32[]{:T(128)} %convert_element_type.449, (bf16[1,512,16,64]{1,3,2,0:T(8,128)(2,1)S(1)}, ...), branch_computations={%region_20.20_spmd, %region_21.21_spmd} | conditional | flops 5464129536 | bytes 367198656 | solution.py:145
  1073.4 9.8 fusion.75
  1083.2 9.3 multiply_convert_fusion
  1115.1 9.6 bitcast_add_fusion.8
  1129.5 9.9 bitcast_add_fusion.9
  1155.6 15.6 collective-permute-done.2
  1172.5 21.1 collective-permute-done.3
  1194.9 21.2 collective-permute-done.5
  1216.1 22.5 %collective-permute-done.7 = f32[1,512,16,64]{1,3,2,0:T(8,128)} collective-permute-done((f32[1,512,16,64]{1,3,2,0:T(8,128)}, f32[1,512,16,64]{1,3,2,0:T(8,128)}, u32[]{:S(2)}, u32[]{:S(2)}) %collective-permute-start.7) | collective-permute-done | bytes 2097184 | tf_op jit(solution)/shard_map/while/body/eval_jaxpr/ppermute | solution.py:49
  1238.6 22.5 %collective-permute-done.4 = f32[1,512,16,64]{1,3,2,0:T(8,128)} collective-permute-done((f32[1,512,16,64]{1,3,2,0:T(8,128)}, f32[1,512,16,64]{1,3,2,0:T(8,128)}, u32[]{:S(2)}, u32[]{:S(2)}) %collective-permute-start.4) | collective-permute-done | bytes 2097184 | tf_op jit(solution)/shard_map/while/body/eval_jaxpr/ppermute | solution.py:49
  1261.0 22.5 %collective-permute-done.6 = f32[1,512,16,64]{1,3,2,0:T(8,128)} collective-permute-done((f32[1,512,16,64]{1,3,2,0:T(8,128)}, f32[1,512,16,64]{1,3,2,0:T(8,128)}, u32[]{:S(2)}, u32[]{:S(2)}) %collective-permute-start.6) | collective-permute-done | bytes 2097184 | tf_op jit(solution)/shard_map/while/body/eval_jaxpr/ppermute | solution.py:49
  1283.5 87.4 %conditional.5 = (f32[1,512,16,64]{1,3,2,0:T(8,128)}, f32[1,512,16,64]{3,2,1,0:T(8,128)}, f32[1,512,16,64]{1,3,2,0:T(8,128)}, f32[1,512,16,64]{3,2,1,0:T(8,128)}...) conditional(s32[]{:T(128)} %convert_element_type.449, (bf16[1,512,16,64]{1,3,2,0:T(8,128)(2,1)S(1)}, ...), branch_computations={%region_20.20_spmd, %region_21.21_spmd} | conditional | flops 5464129536 | bytes 367198656 | solution.py:145
  1304.9 9.8 fusion.75
  1346.6 9.6 bitcast_add_fusion.8
  1361.0 9.9 bitcast_add_fusion.9
  1398.5 16.4 fusion.182
  1419.3 14.3 fusion.146
  1464.1 711.2 %all-reduce.3.cloned.1.call-done = (f32[1024,16,64]{0,2,1:T(8,128)}, f32[1024,16,64]{0,2,1:T(8,128)}, f32[1024,16,64]{0,2,1:T(8,128)}, f32[16,64,1024]{2,1,0:T(8...) async-done(((f32[1024,16,64]{0,2,1:T(8,128)}, f32[1024,16,64]{0,2,1:T(8,128)}, f32[1024,16,64]{0,2,1:T(8,128)}, f32[16,64,1024]{2,1,0:T(8,128)}, f32[1024,4096]{1,0:T(8,128)}, ...) | async-done | bytes 50331664 | tf_op jit(solution)/shard_map/psum | solution.py:160
  2175.2 13.4 broadcast_multiply_fusion
  (286 shorter events, 550.5 us)
Async XLA Ops:
  7.2 4.9 copy-start
  7.2 2168.0 %all-reduce.3.cloned.1.call-start = ((), (), s32[]{:S(2)}) async-start(), calls=%async_computation | async-start | bytes 100663296 | tf_op jit(solution)/shard_map/psum | solution.py:160
  7.3 4.8 copy-start.45
  15.1 22.7 %copy-start.18 = (bf16[1,1024,16,64]{1,3,2,0:T(8,128)(2,1)}, bf16[1,1024,16,64]{1,3,2,0:T(8,128)(2,1)S(1)}, u32[]{:S(2)}) copy-start(bf16[1,1024,16,64]{1,3,2,0:T(8,128)(2,1)S(1)} %get-tuple-element.1209) | copy-start | bytes 6291460
  15.2 24.0 %copy-start.15 = (bf16[1,1024,16,64]{1,3,2,0:T(8,128)(2,1)}, bf16[1,1024,16,64]{1,3,2,0:T(8,128)(2,1)S(1)}, u32[]{:S(2)}) copy-start(bf16[1,1024,16,64]{1,3,2,0:T(8,128)(2,1)S(1)} %get-tuple-element.1490) | copy-start | bytes 6291460
  52.8 10.3 copy-start.23
  110.7 26.2 %collective-permute-start = (bf16[1,1024,16,64]{1,3,2,0:T(8,128)(2,1)}, bf16[1,1024,16,64]{1,3,2,0:T(8,128)(2,1)}, u32[]{:S(2)}, u32[]{:S(2)}) collective-permute-start(bf16[1,1024,16,64]{1,3,2,0:T(8,128)(2,1)} %get-tuple-element.1458), channel_id=1, source_target_pairs={{0,1},{1,2},{2,3},{3,0},{4,5},{5,6},{6,7},{7,4},{8,9},{9,10},{10,1... | collective-permute-start | bytes 6291464 | tf_op jit(solution)/shard_map/while/body/eval_jaxpr/ppermute | solution.py:49
  111.3 48.1 %collective-permute-start.1 = (bf16[1,1024,16,64]{1,3,2,0:T(8,128)(2,1)}, bf16[1,1024,16,64]{1,3,2,0:T(8,128)(2,1)}, u32[]{:S(2)}, u32[]{:S(2)}) collective-permute-start(bf16[1,1024,16,64]{1,3,2,0:T(8,128)(2,1)} %get-tuple-element.1459), channel_id=1, source_target_pairs={{0,1},{1,2},{2,3},{3,0},{4,5},{5,6},{6,7},{7,4},{8,9},{9,10},{10,1... | collective-permute-start | bytes 6291464 | tf_op jit(solution)/shard_map/while/body/eval_jaxpr/ppermute | solution.py:49
  203.6 56.8 %collective-permute-start = (bf16[1,1024,16,64]{1,3,2,0:T(8,128)(2,1)}, bf16[1,1024,16,64]{1,3,2,0:T(8,128)(2,1)}, u32[]{:S(2)}, u32[]{:S(2)}) collective-permute-start(bf16[1,1024,16,64]{1,3,2,0:T(8,128)(2,1)} %get-tuple-element.1458), channel_id=1, source_target_pairs={{0,1},{1,2},{2,3},{3,0},{4,5},{5,6},{6,7},{7,4},{8,9},{9,10},{10,1... | collective-permute-start | bytes 6291464 | tf_op jit(solution)/shard_map/while/body/eval_jaxpr/ppermute | solution.py:49
  237.4 45.5 %collective-permute-start.1 = (bf16[1,1024,16,64]{1,3,2,0:T(8,128)(2,1)}, bf16[1,1024,16,64]{1,3,2,0:T(8,128)(2,1)}, u32[]{:S(2)}, u32[]{:S(2)}) collective-permute-start(bf16[1,1024,16,64]{1,3,2,0:T(8,128)(2,1)} %get-tuple-element.1459), channel_id=1, source_target_pairs={{0,1},{1,2},{2,3},{3,0},{4,5},{5,6},{6,7},{7,4},{8,9},{9,10},{10,1... | collective-permute-start | bytes 6291464 | tf_op jit(solution)/shard_map/while/body/eval_jaxpr/ppermute | solution.py:49
  327.0 56.8 %collective-permute-start = (bf16[1,1024,16,64]{1,3,2,0:T(8,128)(2,1)}, bf16[1,1024,16,64]{1,3,2,0:T(8,128)(2,1)}, u32[]{:S(2)}, u32[]{:S(2)}) collective-permute-start(bf16[1,1024,16,64]{1,3,2,0:T(8,128)(2,1)} %get-tuple-element.1458), channel_id=1, source_target_pairs={{0,1},{1,2},{2,3},{3,0},{4,5},{5,6},{6,7},{7,4},{8,9},{9,10},{10,1... | collective-permute-start | bytes 6291464 | tf_op jit(solution)/shard_map/while/body/eval_jaxpr/ppermute | solution.py:49
  329.4 76.9 %collective-permute-start.1 = (bf16[1,1024,16,64]{1,3,2,0:T(8,128)(2,1)}, bf16[1,1024,16,64]{1,3,2,0:T(8,128)(2,1)}, u32[]{:S(2)}, u32[]{:S(2)}) collective-permute-start(bf16[1,1024,16,64]{1,3,2,0:T(8,128)(2,1)} %get-tuple-element.1459), channel_id=1, source_target_pairs={{0,1},{1,2},{2,3},{3,0},{4,5},{5,6},{6,7},{7,4},{8,9},{9,10},{10,1... | collective-permute-start | bytes 6291464 | tf_op jit(solution)/shard_map/while/body/eval_jaxpr/ppermute | solution.py:49
  458.0 6.2 copy-start.1
  464.4 5.1 copy-start.36
  464.4 5.1 copy-start.41
  464.4 5.1 copy-start.46
  467.2 4.8 slice-start.4
  472.1 10.9 copy-start.55
  472.1 10.9 copy-start.43
  505.6 14.1 copy-start.42
  522.2 57.1 %copy-start.29 = (bf16[1,16,1024,64]{2,3,1,0:T(8,128)(2,1)}, bf16[1,16,1024,64]{2,3,1,0:T(8,128)(2,1)S(1)}, u32[]{:S(2)}) copy-start(bf16[1,16,1024,64]{2,3,1,0:T(8,128)(2,1)S(1)} %get-tuple-element.1208) | copy-start | bytes 6291460
  563.6 8.7 copy-start.16
  580.9 5.4 copy-start.20
  586.3 7.5 copy-start.17
  620.7 8.3 copy-start.2
  651.3 56.9 %collective-permute-start.2 = (bf16[1,1024,16,64]{1,3,2,0:T(8,128)(2,1)}, bf16[1,1024,16,64]{1,3,2,0:T(8,128)(2,1)}, u32[]{:S(2)}, u32[]{:S(2)}) collective-permute-start(bf16[1,1024,16,64]{1,3,2,0:T(8,128)(2,1)} %get-tuple-element.1512), channel_id=1, source_target_pairs={{0,1},{1,2},{2,3},{3,0},{4,5},{5,6},{6,7},{7,4},{8,9},{9,10},{10,1... | collective-permute-start | bytes 6291464 | tf_op jit(solution)/shard_map/while/body/eval_jaxpr/ppermute | solution.py:49
  656.3 74.4 %collective-permute-start.3 = (bf16[1,1024,16,64]{1,3,2,0:T(8,128)(2,1)}, bf16[1,1024,16,64]{1,3,2,0:T(8,128)(2,1)}, u32[]{:S(2)}, u32[]{:S(2)}) collective-permute-start(bf16[1,1024,16,64]{1,3,2,0:T(8,128)(2,1)} %get-tuple-element.1513), channel_id=1, source_target_pairs={{0,1},{1,2},{2,3},{3,0},{4,5},{5,6},{6,7},{7,4},{8,9},{9,10},{10,1... | collective-permute-start | bytes 6291464 | tf_op jit(solution)/shard_map/while/body/eval_jaxpr/ppermute | solution.py:49
  662.6 90.6 %collective-permute-start.5 = (f32[1,512,16,64]{1,3,2,0:T(8,128)}, f32[1,512,16,64]{1,3,2,0:T(8,128)}, u32[]{:S(2)}, u32[]{:S(2)}) collective-permute-start(f32[1,512,16,64]{1,3,2,0:T(8,128)} %copy.104), channel_id=1, source_target_pairs={{0,1},{1,2},{2,3},{3,0},{4,5},{5,6},{6,7},{7,4},{8,9},{9,10},{10,1... | collective-permute-start | bytes 6291464 | tf_op jit(solution)/shard_map/while/body/eval_jaxpr/ppermute | solution.py:49
  692.6 83.0 %collective-permute-start.7 = (f32[1,512,16,64]{1,3,2,0:T(8,128)}, f32[1,512,16,64]{1,3,2,0:T(8,128)}, u32[]{:S(2)}, u32[]{:S(2)}) collective-permute-start(f32[1,512,16,64]{1,3,2,0:T(8,128)} %copy.105), channel_id=1, source_target_pairs={{0,1},{1,2},{2,3},{3,0},{4,5},{5,6},{6,7},{7,4},{8,9},{9,10},{10,1... | collective-permute-start | bytes 6291464 | tf_op jit(solution)/shard_map/while/body/eval_jaxpr/ppermute | solution.py:49
  692.6 105.4 %collective-permute-start.4 = (f32[1,512,16,64]{1,3,2,0:T(8,128)}, f32[1,512,16,64]{1,3,2,0:T(8,128)}, u32[]{:S(2)}, u32[]{:S(2)}) collective-permute-start(f32[1,512,16,64]{1,3,2,0:T(8,128)} %get-tuple-element.1514), channel_id=1, source_target_pairs={{0,1},{1,2},{2,3},{3,0},{4,5},{5,6},{6,7},{7,4},{8,9},{9,10},{10,1... | collective-permute-start | bytes 6291464 | tf_op jit(solution)/shard_map/while/body/eval_jaxpr/ppermute | solution.py:49
  708.2 112.4 %collective-permute-start.6 = (f32[1,512,16,64]{1,3,2,0:T(8,128)}, f32[1,512,16,64]{1,3,2,0:T(8,128)}, u32[]{:S(2)}, u32[]{:S(2)}) collective-permute-start(f32[1,512,16,64]{1,3,2,0:T(8,128)} %get-tuple-element.1516), channel_id=1, source_target_pairs={{0,1},{1,2},{2,3},{3,0},{4,5},{5,6},{6,7},{7,4},{8,9},{9,10},{10,1... | collective-permute-start | bytes 6291464 | tf_op jit(solution)/shard_map/while/body/eval_jaxpr/ppermute | solution.py:49
  708.2 112.4 %copy-start.9 = (bf16[1,16,512,64]{2,3,1,0:T(8,128)(2,1)S(1)}, bf16[1,16,512,64]{2,3,1,0:T(8,128)(2,1)}, u32[]{:S(2)}) copy-start(bf16[1,16,512,64]{2,3,1,0:T(8,128)(2,1)} %get-tuple-element.1545) | copy-start | bytes 3145732 | tf_op jit(solution)/shard_map/while
  820.5 31.2 %copy-start.10 = (bf16[1,16,512,64]{2,3,1,0:T(8,128)(2,1)}, bf16[1,16,512,64]{2,3,1,0:T(8,128)(2,1)S(1)}, u32[]{:S(2)}) copy-start(bf16[1,16,512,64]{2,3,1,0:T(8,128)(2,1)S(1)} %get-tuple-element.882) | copy-start | bytes 3145732 | tf_op jit(solution)/shard_map/while/body/eval_jaxpr/cond
  876.8 6.8 copy-start.11
  914.2 25.5 %collective-permute-start.2 = (bf16[1,1024,16,64]{1,3,2,0:T(8,128)(2,1)}, bf16[1,1024,16,64]{1,3,2,0:T(8,128)(2,1)}, u32[]{:S(2)}, u32[]{:S(2)}) collective-permute-start(bf16[1,1024,16,64]{1,3,2,0:T(8,128)(2,1)} %get-tuple-element.1512), channel_id=1, source_target_pairs={{0,1},{1,2},{2,3},{3,0},{4,5},{5,6},{6,7},{7,4},{8,9},{9,10},{10,1... | collective-permute-start | bytes 6291464 | tf_op jit(solution)/shard_map/while/body/eval_jaxpr/ppermute | solution.py:49
  914.2 47.9 %collective-permute-start.3 = (bf16[1,1024,16,64]{1,3,2,0:T(8,128)(2,1)}, bf16[1,1024,16,64]{1,3,2,0:T(8,128)(2,1)}, u32[]{:S(2)}, u32[]{:S(2)}) collective-permute-start(bf16[1,1024,16,64]{1,3,2,0:T(8,128)(2,1)} %get-tuple-element.1513), channel_id=1, source_target_pairs={{0,1},{1,2},{2,3},{3,0},{4,5},{5,6},{6,7},{7,4},{8,9},{9,10},{10,1... | collective-permute-start | bytes 6291464 | tf_op jit(solution)/shard_map/while/body/eval_jaxpr/ppermute | solution.py:49
  918.0 66.6 %collective-permute-start.5 = (f32[1,512,16,64]{1,3,2,0:T(8,128)}, f32[1,512,16,64]{1,3,2,0:T(8,128)}, u32[]{:S(2)}, u32[]{:S(2)}) collective-permute-start(f32[1,512,16,64]{1,3,2,0:T(8,128)} %copy.104), channel_id=1, source_target_pairs={{0,1},{1,2},{2,3},{3,0},{4,5},{5,6},{6,7},{7,4},{8,9},{9,10},{10,1... | collective-permute-start | bytes 6291464 | tf_op jit(solution)/shard_map/while/body/eval_jaxpr/ppermute | solution.py:49
  922.8 84.3 %collective-permute-start.7 = (f32[1,512,16,64]{1,3,2,0:T(8,128)}, f32[1,512,16,64]{1,3,2,0:T(8,128)}, u32[]{:S(2)}, u32[]{:S(2)}) collective-permute-start(f32[1,512,16,64]{1,3,2,0:T(8,128)} %copy.105), channel_id=1, source_target_pairs={{0,1},{1,2},{2,3},{3,0},{4,5},{5,6},{6,7},{7,4},{8,9},{9,10},{10,1... | collective-permute-start | bytes 6291464 | tf_op jit(solution)/shard_map/while/body/eval_jaxpr/ppermute | solution.py:49
  924.1 105.5 %collective-permute-start.4 = (f32[1,512,16,64]{1,3,2,0:T(8,128)}, f32[1,512,16,64]{1,3,2,0:T(8,128)}, u32[]{:S(2)}, u32[]{:S(2)}) collective-permute-start(f32[1,512,16,64]{1,3,2,0:T(8,128)} %get-tuple-element.1514), channel_id=1, source_target_pairs={{0,1},{1,2},{2,3},{3,0},{4,5},{5,6},{6,7},{7,4},{8,9},{9,10},{10,1... | collective-permute-start | bytes 6291464 | tf_op jit(solution)/shard_map/while/body/eval_jaxpr/ppermute | solution.py:49
  939.7 112.4 %collective-permute-start.6 = (f32[1,512,16,64]{1,3,2,0:T(8,128)}, f32[1,512,16,64]{1,3,2,0:T(8,128)}, u32[]{:S(2)}, u32[]{:S(2)}) collective-permute-start(f32[1,512,16,64]{1,3,2,0:T(8,128)} %get-tuple-element.1516), channel_id=1, source_target_pairs={{0,1},{1,2},{2,3},{3,0},{4,5},{5,6},{6,7},{7,4},{8,9},{9,10},{10,1... | collective-permute-start | bytes 6291464 | tf_op jit(solution)/shard_map/while/body/eval_jaxpr/ppermute | solution.py:49
  939.7 112.4 %copy-start.9 = (bf16[1,16,512,64]{2,3,1,0:T(8,128)(2,1)S(1)}, bf16[1,16,512,64]{2,3,1,0:T(8,128)(2,1)}, u32[]{:S(2)}) copy-start(bf16[1,16,512,64]{2,3,1,0:T(8,128)(2,1)} %get-tuple-element.1545) | copy-start | bytes 3145732 | tf_op jit(solution)/shard_map/while
  1052.0 31.2 %copy-start.10 = (bf16[1,16,512,64]{2,3,1,0:T(8,128)(2,1)}, bf16[1,16,512,64]{2,3,1,0:T(8,128)(2,1)S(1)}, u32[]{:S(2)}) copy-start(bf16[1,16,512,64]{2,3,1,0:T(8,128)(2,1)S(1)} %get-tuple-element.882) | copy-start | bytes 3145732 | tf_op jit(solution)/shard_map/while/body/eval_jaxpr/cond
  1108.3 6.8 copy-start.11
  1145.7 25.5 %collective-permute-start.2 = (bf16[1,1024,16,64]{1,3,2,0:T(8,128)(2,1)}, bf16[1,1024,16,64]{1,3,2,0:T(8,128)(2,1)}, u32[]{:S(2)}, u32[]{:S(2)}) collective-permute-start(bf16[1,1024,16,64]{1,3,2,0:T(8,128)(2,1)} %get-tuple-element.1512), channel_id=1, source_target_pairs={{0,1},{1,2},{2,3},{3,0},{4,5},{5,6},{6,7},{7,4},{8,9},{9,10},{10,1... | collective-permute-start | bytes 6291464 | tf_op jit(solution)/shard_map/while/body/eval_jaxpr/ppermute | solution.py:49
  1145.7 47.9 %collective-permute-start.3 = (bf16[1,1024,16,64]{1,3,2,0:T(8,128)(2,1)}, bf16[1,1024,16,64]{1,3,2,0:T(8,128)(2,1)}, u32[]{:S(2)}, u32[]{:S(2)}) collective-permute-start(bf16[1,1024,16,64]{1,3,2,0:T(8,128)(2,1)} %get-tuple-element.1513), channel_id=1, source_target_pairs={{0,1},{1,2},{2,3},{3,0},{4,5},{5,6},{6,7},{7,4},{8,9},{9,10},{10,1... | collective-permute-start | bytes 6291464 | tf_op jit(solution)/shard_map/while/body/eval_jaxpr/ppermute | solution.py:49
  1149.5 66.6 %collective-permute-start.5 = (f32[1,512,16,64]{1,3,2,0:T(8,128)}, f32[1,512,16,64]{1,3,2,0:T(8,128)}, u32[]{:S(2)}, u32[]{:S(2)}) collective-permute-start(f32[1,512,16,64]{1,3,2,0:T(8,128)} %copy.104), channel_id=1, source_target_pairs={{0,1},{1,2},{2,3},{3,0},{4,5},{5,6},{6,7},{7,4},{8,9},{9,10},{10,1... | collective-permute-start | bytes 6291464 | tf_op jit(solution)/shard_map/while/body/eval_jaxpr/ppermute | solution.py:49
  1154.2 84.3 %collective-permute-start.7 = (f32[1,512,16,64]{1,3,2,0:T(8,128)}, f32[1,512,16,64]{1,3,2,0:T(8,128)}, u32[]{:S(2)}, u32[]{:S(2)}) collective-permute-start(f32[1,512,16,64]{1,3,2,0:T(8,128)} %copy.105), channel_id=1, source_target_pairs={{0,1},{1,2},{2,3},{3,0},{4,5},{5,6},{6,7},{7,4},{8,9},{9,10},{10,1... | collective-permute-start | bytes 6291464 | tf_op jit(solution)/shard_map/while/body/eval_jaxpr/ppermute | solution.py:49
  1155.5 105.5 %collective-permute-start.4 = (f32[1,512,16,64]{1,3,2,0:T(8,128)}, f32[1,512,16,64]{1,3,2,0:T(8,128)}, u32[]{:S(2)}, u32[]{:S(2)}) collective-permute-start(f32[1,512,16,64]{1,3,2,0:T(8,128)} %get-tuple-element.1514), channel_id=1, source_target_pairs={{0,1},{1,2},{2,3},{3,0},{4,5},{5,6},{6,7},{7,4},{8,9},{9,10},{10,1... | collective-permute-start | bytes 6291464 | tf_op jit(solution)/shard_map/while/body/eval_jaxpr/ppermute | solution.py:49
  1171.2 112.4 %collective-permute-start.6 = (f32[1,512,16,64]{1,3,2,0:T(8,128)}, f32[1,512,16,64]{1,3,2,0:T(8,128)}, u32[]{:S(2)}, u32[]{:S(2)}) collective-permute-start(f32[1,512,16,64]{1,3,2,0:T(8,128)} %get-tuple-element.1516), channel_id=1, source_target_pairs={{0,1},{1,2},{2,3},{3,0},{4,5},{5,6},{6,7},{7,4},{8,9},{9,10},{10,1... | collective-permute-start | bytes 6291464 | tf_op jit(solution)/shard_map/while/body/eval_jaxpr/ppermute | solution.py:49
  1171.2 112.4 %copy-start.9 = (bf16[1,16,512,64]{2,3,1,0:T(8,128)(2,1)S(1)}, bf16[1,16,512,64]{2,3,1,0:T(8,128)(2,1)}, u32[]{:S(2)}) copy-start(bf16[1,16,512,64]{2,3,1,0:T(8,128)(2,1)} %get-tuple-element.1545) | copy-start | bytes 3145732 | tf_op jit(solution)/shard_map/while
  1283.5 31.2 %copy-start.10 = (bf16[1,16,512,64]{2,3,1,0:T(8,128)(2,1)}, bf16[1,16,512,64]{2,3,1,0:T(8,128)(2,1)S(1)}, u32[]{:S(2)}) copy-start(bf16[1,16,512,64]{2,3,1,0:T(8,128)(2,1)S(1)} %get-tuple-element.882) | copy-start | bytes 3145732 | tf_op jit(solution)/shard_map/while/body/eval_jaxpr/cond
  1339.7 6.8 copy-start.11
  1388.0 52.2 %collective-permute-start.11 = (bf16[1,512,16,64]{1,3,2,0:T(8,128)(2,1)}, bf16[1,512,16,64]{1,3,2,0:T(8,128)(2,1)}, u32[]{:S(2)}, u32[]{:S(2)}) collective-permute-start(bf16[1,512,16,64]{1,3,2,0:T(8,128)(2,1)} %copy.82), channel_id=1, source_target_pairs={{0,1},{1,2},{2,3},{3,0},{4,5},{5,6},{6,7},{7,4},{8,9},{9,10},{10,1... | collective-permute-start | bytes 3145736 | tf_op jit(solution)/shard_map/ppermute | solution.py:49
  1390.7 49.5 %collective-permute-start.10 = (bf16[1,512,16,64]{1,3,2,0:T(8,128)(2,1)}, bf16[1,512,16,64]{1,3,2,0:T(8,128)(2,1)}, u32[]{:S(2)}, u32[]{:S(2)}) collective-permute-start(bf16[1,512,16,64]{1,3,2,0:T(8,128)(2,1)} %convert.67), channel_id=1, source_target_pairs={{0,1},{1,2},{2,3},{3,0},{4,5},{5,6},{6,7},{7,4},{8,9},{9,10},{10,1... | collective-permute-start | bytes 3145736 | tf_op jit(solution)/shard_map/ppermute | solution.py:49
  1394.3 51.9 %collective-permute-start.9 = (bf16[1,512,16,64]{1,3,2,0:T(8,128)(2,1)}, bf16[1,512,16,64]{1,3,2,0:T(8,128)(2,1)S(1)}, u32[]{:S(2)}, u32[]{:S(2)}) collective-permute-start(bf16[1,512,16,64]{1,3,2,0:T(8,128)(2,1)} %copy.81), channel_id=1, source_target_pairs={{0,1},{1,2},{2,3},{3,0},{4,5},{5,6},{6,7},{7,4},{8,9},{9,10},{10,1... | collective-permute-start | bytes 3145736 | tf_op jit(solution)/shard_map/ppermute | solution.py:49
  1395.2 24.1 %slice-start.6 = ((s8[8388608]{0:T(1024)(128)(4,1)}), s8[4194304]{0:T(1024)(128)(4,1)S(1)}, s32[]{:S(2)}) async-start(s8[8388608]{0:T(1024)(128)(4,1)} %bitcast.542), calls=%async_computation.7 | async-start | bytes 8388608
  1397.1 17.9 copy-start.37
  1397.1 17.8 copy-start.39
  1397.1 17.8 copy-start.57
  1397.1 22.2 %slice-start.7 = ((s8[8388608]{0:T(1024)(128)(4,1)}), s8[4194304]{0:T(1024)(128)(4,1)S(1)}, s32[]{:S(2)}) async-start(s8[8388608]{0:T(1024)(128)(4,1)} %bitcast.542), calls=%async_computation.8 | async-start | bytes 8388608
  1397.1 49.0 %collective-permute-start.8 = (bf16[1,512,16,64]{1,3,2,0:T(8,128)(2,1)S(1)}, bf16[1,512,16,64]{1,3,2,0:T(8,128)(2,1)S(1)}, u32[]{:S(2)}, u32[]{:S(2)}) collective-permute-start(bf16[1,512,16,64]{1,3,2,0:T(8,128)(2,1)S(1)} %convert.66), channel_id=1, source_target_pairs={{0,1},{1,2},{2,3},{3,0},{4,5},{5,6},{6,7},{7,4},{8,9},{9,10},{10,1... | collective-permute-start | bytes 3145736 | tf_op jit(solution)/shard_map/ppermute | solution.py:49
  1419.3 14.3 copy-start.8
  2175.2 16.4 copy-start.31
  2191.7 6.6 copy-start.35
  (24 other events, 72.2 us)
Sparse Core Ops, SparseCore 0:
  1452.0 723.1 all-reduce.2
where the time goes:
time: 2230 us; the launch traced here: 2220 us
  waiting for transfers between devices  1210 us (54%)
  matrix products  587 us (26%)
  local copies, waits for them, and re-layouts  155 us (7%)
  starting transfers between devices  119 us (5%)
  other arithmetic  96.3 us (4%)
  loops' own time  37.6 us (2%)
    psum x1, waiting for transfers between devices, per_device(): lax.psum((grad_q_w, grad_k_w, grad_v_w, grad_o, grad_up, grad_down), ('dp...  711 us
    ppermute x28, waiting for transfers between devices, rotate(): lax.ppermute(tensor, 'cp', shift_pairs)  498 us
    ppermute x28, starting transfers between devices, rotate(): lax.ppermute(tensor, 'cp', shift_pairs)  119 us
    dot_general x9, matrix products, block_backward(): jnp.einsum('bhqk,bhqe->bkhe', prob_f.astype(jnp.bfloat16), grad_rows, pre...  89 us
    dot_general x9, matrix products, block_backward(): jnp.einsum('bhqe,bkhe->bhqk', grad_rows, val_blk, preferred_element_type=...  84.7 us
    dot_general x9, matrix products, block_forward(): jnp.einsum('bhqk,bkhe->bhqe', prob_f.astype(jnp.bfloat16), val_blk, prefe...  72.9 us
    dot_general x9, matrix products, block_forward(): jnp.einsum('bqhe,bkhe->bhqk', q_rows, key_blk, preferred_element_type=jnp...  61.7 us
    dot_general x6, matrix products, block_backward(): jnp.einsum('bqhe,bkhe->bhqk', q_rows, key_blk, preferred_element_type=jnp...  55 us
  transfers between devices with their start and end apart: 29, of which 25 were waited for; matrix products, arithmetic and copies ran while one was open for 5% of the time, Pallas kernels for 0%

commit v1 on v0

v1 whole, which is shorter than its diff:
```python
import functools
import jax
import jax.numpy as jnp
from jax import lax
from jax.experimental import pallas as pl
from jax.experimental.pallas import tpu as pltpu
from jax.sharding import PartitionSpec as P


LOG2E = 1.4426950408889634
NEG_BIG = -1e30
BLK = 512
F32 = jnp.float32
BF16 = jnp.bfloat16


def nt(a, b):
    return lax.dot_general(a, b, (((1,), (1,)), ((), ())), preferred_element_type=F32)


def nn(a, b):
    return lax.dot_general(a, b, (((1,), (0,)), ((), ())), preferred_element_type=F32)


def lane_mask(half):
    lanes = lax.broadcasted_iota(jnp.int32, (BLK, 128), 1)
    return (lanes < 64) if half == 0 else (lanes >= 64)


def pick(arr, half):
    return jnp.where(lane_mask(half), arr, jnp.zeros_like(arr))


def load_all(srcs, dsts, sem):
    copies = []
    for parts, dst in zip(srcs, dsts):
        for j, (ref, c) in enumerate(parts):
            rows = ref.shape[0]
            copies.append(pltpu.make_async_copy(ref.at[:, pl.ds(c, 128)], dst.at[pl.ds(j * rows, rows), :], sem))
    for c in copies:
        c.start()
    for c in copies:
        c.wait()


def attn_fwd_kernel(pair, tab_ref, *refs):
    qkv_refs = refs[:4]
    o_ref, lse_ref, q_ref, k_ref, v_ref, vt_ref, sem = refs[4:]
    n_blk = q_ref.shape[0] // BLK
    step = pl.program_id(0)

    @pl.when(step == 0)
    def _():
        load_all([[(r, 384 * pair + 128 * t) for r in qkv_refs] for t in range(3)], [q_ref, k_ref, v_ref], sem)
        for b in range(n_blk):
            rows = pl.ds(b * BLK, BLK)
            vt_ref[:, rows] = v_ref[rows, :].astype(F32).T.astype(BF16)

    q_off = pl.multiple_of(tab_ref[step] * BLK, BLK)
    q_blk = q_ref[pl.ds(q_off, BLK), :] * jnp.asarray(0.125, BF16)
    q_half = [pick(q_blk, 0), pick(q_blk, 1)]

    def update(key_idx, state, diag):
        off = pl.multiple_of(tab_ref[key_idx] * BLK, BLK)
        k_blk = k_ref[pl.ds(off, BLK), :]
        out = []
        for h in range(2):
            m_row, l_row, acc = state[3 * h:3 * h + 3]
            s = nt(k_blk, q_half[h])
            if diag:
                kk = lax.broadcasted_iota(jnp.int32, (BLK, BLK), 0)
                qq = lax.broadcasted_iota(jnp.int32, (BLK, BLK), 1)
                s = jnp.where(kk <= qq, s, NEG_BIG)
            m_new = jnp.maximum(m_row, jnp.max(s, axis=0, keepdims=True))
            fac = jnp.exp2((m_row - m_new) * LOG2E)
            p = jnp.exp2((s - m_new) * LOG2E)
            l_row = l_row * fac + jnp.sum(p, axis=0, keepdims=True)
            vt = vt_ref[64 * h:64 * h + 64, pl.ds(off, BLK)]
            acc = acc * fac + nn(vt, p.astype(BF16))
            out += [m_new, l_row, acc]
        return tuple(out)

    fresh = (jnp.full((1, BLK), NEG_BIG, F32), jnp.zeros((1, BLK), F32), jnp.zeros((64, BLK), F32))
    state = lax.fori_loop(0, step, lambda j, st: update(j, st, False), fresh + fresh)
    state = update(step, state, True)
    o_t = jnp.concatenate([state[2] / state[1], state[5] / state[4]], axis=0)
    o_ref[pl.ds(q_off, BLK), :] = o_t.T.astype(BF16)
    for h in range(2):
        lse_ref[0, h:h + 1, pl.ds(q_off, BLK)] = (state[3 * h] + jnp.log(state[3 * h + 1])) * LOG2E


def attn_bwd_kernel(pair, tab_ref, *refs):
    qkv_refs, do_refs = refs[:4], refs[4:8]
    o_ref, lse_ref = refs[8:10]
    out_refs = refs[10:14]
    q_ref, k_ref, v_ref, do_ref, dqt_ref, dot_ref, dkv_ref, sem = refs[14:]
    n_blk = q_ref.shape[0] // BLK
    step = pl.program_id(0)

    @pl.when(step == 0)
    def _():
        load_all([[(r, 384 * pair + 128 * t) for r in qkv_refs] for t in range(3)] + [[(r, 0) for r in do_refs]],
                 [q_ref, k_ref, v_ref, do_ref], sem)
        dqt_ref[...] = jnp.zeros_like(dqt_ref)
        for b in range(n_blk):
            rows = pl.ds(b * BLK, BLK)
            prod = (do_ref[rows, :].astype(F32) * o_ref[rows, :].astype(F32)).T
            dot_ref[0:1, rows] = jnp.sum(prod[:64], axis=0, keepdims=True)
            dot_ref[1:2, rows] = jnp.sum(prod[64:], axis=0, keepdims=True)

    k_off = pl.multiple_of(tab_ref[step] * BLK, BLK)
    k_blk = k_ref[pl.ds(k_off, BLK), :]
    v_blk = v_ref[pl.ds(k_off, BLK), :]
    k_t = k_blk.astype(F32).T.astype(BF16)

    def update(q_idx, state, diag):
        dk, dv = state
        off = pl.multiple_of(tab_ref[q_idx] * BLK, BLK)
        q_blk = q_ref[pl.ds(off, BLK), :] * jnp.asarray(0.125, BF16)
        do_blk = do_ref[pl.ds(off, BLK), :]
        for h in range(2):
            q_h = pick(q_blk, h)
            do_h = pick(do_blk, h)
            s = nt(k_blk, q_h)
            if diag:
                kk = lax.broadcasted_iota(jnp.int32, (BLK, BLK), 0)
                qq = lax.broadcasted_iota(jnp.int32, (BLK, BLK), 1)
                s = jnp.where(kk <= qq, s, NEG_BIG)
            p = jnp.exp2(s * LOG2E - lse_ref[0, h:h + 1, pl.ds(off, BLK)])
            dp = nt(v_blk, do_h).astype(BF16).astype(F32)
            ds = (p * (dp - dot_ref[h:h + 1, pl.ds(off, BLK)])).astype(BF16)
            dv = dv + nn(p.astype(BF16), do_h)
            dk = dk + nn(ds, q_h)
            cols = pl.ds(off, BLK)
            dqt_ref[64 * h:64 * h + 64, cols] += nn(k_t[64 * h:64 * h + 64], ds)
        return dk, dv

    zero = jnp.zeros((BLK, 128), F32)
    state = update(step, (zero, zero), True)
    dk, dv = lax.fori_loop(step + 1, n_blk, lambda i, st: update(i, st, False), state)
    dkv_ref[pl.ds(k_off, BLK), 0:128] = dk.astype(BF16)
    dkv_ref[pl.ds(k_off, BLK), 128:256] = dv.astype(BF16)

    @pl.when(step == n_blk - 1)
    def _():
        rows = q_ref.shape[0] // 4
        for j in range(4):
            span = pl.ds(j * rows, rows)
            out_refs[j][:, 0:128] = (dqt_ref[:, span] * 0.125).T.astype(BF16)
            out_refs[j][:, 128:384] = dkv_ref[span, :]


def pair_cost(seq_len, n_dots):
    return pl.CostEstimate(flops=2 * seq_len * seq_len * 128 * n_dots * 2, bytes_accessed=16 * seq_len * 128,
                           transcendentals=seq_len * seq_len)


ANY = pl.BlockSpec(memory_space=pl.ANY)


def attn_fwd(tab, qkv, pair):
    rows = qkv[0].shape[0]
    seq_len = 4 * rows
    n_blk = seq_len // BLK
    whole = pl.BlockSpec((seq_len, 128), lambda i, tab: (0, 0))
    buf = pltpu.VMEM((seq_len, 128), BF16)
    return pl.pallas_call(
        functools.partial(attn_fwd_kernel, pair),
        out_shape=[jax.ShapeDtypeStruct((seq_len, 128), BF16), jax.ShapeDtypeStruct((1, 2, seq_len), F32)],
        grid_spec=pltpu.PrefetchScalarGridSpec(
            num_scalar_prefetch=1, grid=(n_blk,),
            in_specs=[ANY] * 4,
            out_specs=[whole, pl.BlockSpec((1, 2, seq_len), lambda i, tab: (0, 0, 0))],
            scratch_shapes=[buf, buf, buf, pltpu.VMEM((128, seq_len), BF16), pltpu.SemaphoreType.DMA]),
        compiler_params=pltpu.CompilerParams(vmem_limit_bytes=48 * 1024 * 1024),
        cost_estimate=pair_cost(seq_len, 2),
        name='attn_fwd')(tab, *qkv)


def attn_bwd(tab, qkv, d_o, out_o, lse, pair):
    rows = qkv[0].shape[0]
    seq_len = 4 * rows
    n_blk = seq_len // BLK
    whole = pl.BlockSpec((seq_len, 128), lambda i, tab: (0, 0))
    buf = pltpu.VMEM((seq_len, 128), BF16)
    return pl.pallas_call(
        functools.partial(attn_bwd_kernel, pair),
        out_shape=[jax.ShapeDtypeStruct((rows, 384), BF16)] * 4,
        grid_spec=pltpu.PrefetchScalarGridSpec(
            num_scalar_prefetch=1, grid=(n_blk,),
            in_specs=[ANY] * 8 + [whole, pl.BlockSpec((1, 2, seq_len), lambda i, tab: (0, 0, 0))],
            out_specs=[pl.BlockSpec((rows, 384), lambda i, tab: (0, 0))] * 4,
            scratch_shapes=[buf, buf, buf, buf, pltpu.VMEM((128, seq_len), F32), pltpu.VMEM((2, seq_len), F32),
                            pltpu.VMEM((seq_len, 256), BF16), pltpu.SemaphoreType.DMA]),
        compiler_params=pltpu.CompilerParams(vmem_limit_bytes=48 * 1024 * 1024),
        cost_estimate=pair_cost(seq_len, 5),
        name='attn_bwd')(tab, *qkv, *d_o, out_o, lse)


MESH = pl.DeviceIdType.MESH
LAG = 2
UNIT = 256
WIDE = 1024


def sum_kernel(up_ref, mine_ref, up_out, qkv_out, acc, rc, r1, r2, rz, macc, my, mz,
               one, pairs, tri_s, tri_r, tri_as, tri_ar, m_one, m_pairs, m_tri_s, m_tri_r, m_tri_as, m_tri_ar):
    dp, cp = lax.axis_index('dp'), lax.axis_index('cp')
    z, y, x, c = dp // 2, dp % 2, cp // 2, cp % 2
    n_up, n_mine = acc.shape[0], macc.shape[0]
    blocks = up_ref.shape[1] // WIDE
    ids = lambda d, p: {'dp': d, 'cp': p}
    core_id = ids(dp, 2 * x + 1 - c)
    x_id = ids(dp, 2 * (1 - x) + c)
    y_id = ids(2 * z + 1 - y, cp)
    z_ids = [ids(2 * ((z + k) % 4) + y, cp) for k in (1, 2, 3)]

    barrier = pltpu.get_barrier_semaphore()
    for peer in [core_id, x_id, y_id] + z_ids:
        pl.semaphore_signal(barrier, inc=1, device_id=peer, device_id_type=MESH)
    pl.semaphore_wait(barrier, 6)

    def remote(src, dst, s_sem, r_sem, dev):
        return pltpu.make_async_remote_copy(src_ref=src, dst_ref=dst, send_sem=s_sem, recv_sem=r_sem,
                                            device_id=dev, device_id_type=MESH)

    class Up:
        def __init__(self, u):
            color = u % 2
            self.u = u
            self.row = (u // blocks) * UNIT
            self.cols = pl.ds(pl.multiple_of((u % blocks) * WIDE, WIDE), WIDE)
            self.b1 = x + color * (y - x)
            self.b2 = y + color * (x - y)
            self.d1 = ids(2 * z + y + color * (1 - 2 * y), 2 * (x + (1 - color) * (1 - 2 * x)) + c)
            self.d2 = ids(2 * z + y + (1 - color) * (1 - 2 * y), 2 * (x + color * (1 - 2 * x)) + c)
            self.base = self.b1 * (UNIT // 4) + self.b2 * (UNIT // 8)

        def src(self, off, n):
            return up_ref.at[pl.ds(pl.multiple_of(self.row + off, 8), n), self.cols]

        def out(self, off, n):
            return up_out.at[pl.ds(pl.multiple_of(self.row + off, 8), n), self.cols]

        def part(self, off, n):
            return acc.at[self.u, pl.ds(pl.multiple_of(off, 8), n), :]

        def pair(self, i, src, dst, dev):
            return remote(src, dst, pairs.at[self.u, i, 0], pairs.at[self.u, i, 1], dev)

        def load(self):
            return pltpu.make_async_copy(self.src(c * (UNIT // 2), UNIT // 2), acc.at[self.u], one.at[self.u, 0])

        def core(self):
            return self.pair(0, self.src((1 - c) * (UNIT // 2), UNIT // 2), rc.at[self.u], core_id)

        def first(self):
            return self.pair(1, self.part((1 - self.b1) * (UNIT // 4), UNIT // 4), r1.at[self.u], self.d1)

        def second(self):
            return self.pair(2, self.part(self.b1 * (UNIT // 4) + (1 - self.b2) * (UNIT // 8), UNIT // 8),
                             r2.at[self.u], self.d2)

        def zs(self):
            n = UNIT // 32
            return [remote(self.part(self.base + ((z + k) % 4) * n, n), rz.at[self.u, k - 1],
                           tri_s.at[self.u, k - 1], tri_r.at[self.u, k - 1], z_ids[k - 1]) for k in (1, 2, 3)]

        def back_zs(self):
            n = UNIT // 32
            dst = self.out(c * (UNIT // 2) + self.base + z * n, n)
            return [remote(self.part(self.base + z * n, n), dst,
                           tri_as.at[self.u, k - 1], tri_ar.at[self.u, k - 1], z_ids[k - 1]) for k in (1, 2, 3)]

        def keep(self):
            n = UNIT // 32
            return pltpu.make_async_copy(self.part(self.base + z * n, n),
                                         self.out(c * (UNIT // 2) + self.base + z * n, n), one.at[self.u, 1])

        def back(self, i, off, n, dev):
            return self.pair(i, self.out(off, n), self.out(off, n), dev)

        def back_second(self):
            return self.back(3, c * (UNIT // 2) + self.base, UNIT // 8, self.d2)

        def back_first(self):
            return self.back(4, c * (UNIT // 2) + self.b1 * (UNIT // 4), UNIT // 4, self.d1)

        def back_core(self):
            return self.back(5, c * (UNIT // 2), UNIT // 2, core_id)

    def add_into(ref, other):
        ref[...] = ref[...] + other[...]

    def up_take(s, u):
        w = Up(u)
        if s == 1:
            w.load().wait()
            w.core().wait_recv()
            add_into(acc.at[u], rc.at[u])
        elif s == 2:
            w.first().wait_recv()
            add_into(w.part(w.b1 * (UNIT // 4), UNIT // 4), r1.at[u])
        elif s == 3:
            w.second().wait_recv()
            add_into(w.part(w.base, UNIT // 8), r2.at[u])
        elif s == 4:
            for cpy in w.zs():
                cpy.wait_recv()
            n = UNIT // 32
            dst = w.part(w.base + z * n, n)
            dst[...] = dst[...] + (rz[u, 0] + rz[u, 1] + rz[u, 2])
        elif s == 5:
            for cpy in w.back_zs():
                cpy.wait_recv()
            w.keep().wait()
        elif s == 6:
            w.back_second().wait_recv()
        elif s == 7:
            w.back_first().wait_recv()
        elif s == 8:
            w.back_core().wait_recv()
            for cpy in [w.core(), w.first(), w.second()] + w.zs() + w.back_zs() + [
                    w.back_second(), w.back_first(), w.back_core()]:
                cpy.wait_send()

    def up_give(s, u):
        w = Up(u)
        todo = [lambda: [w.load(), w.core()], lambda: [w.first()], lambda: [w.second()], w.zs,
                lambda: w.back_zs() + [w.keep()], lambda: [w.back_second()], lambda: [w.back_first()],
                lambda: [w.back_core()]][s]
        for cpy in todo():
            cpy.start()

    class Mine:
        def __init__(self, m):
            self.m = m
            self.orow = (m // 4) * 1024 + (m % 4) * 64

        def out(self, holder, off, n):
            return qkv_out.at[pl.ds(pl.multiple_of(self.orow + holder * 256 + off, 8), n), :]

        def part(self, off, n):
            return macc.at[self.m, pl.ds(pl.multiple_of(off, 8), n), :]

        def pair(self, i, src, dst, dev):
            return remote(src, dst, m_pairs.at[self.m, i, 0], m_pairs.at[self.m, i, 1], dev)

        def load(self):
            return pltpu.make_async_copy(mine_ref.at[pl.ds(pl.multiple_of(self.m * 64, 8), 64), :], macc.at[self.m],
                                         m_one.at[self.m, 0])

        def ys(self):
            return self.pair(0, mine_ref.at[pl.ds(pl.multiple_of(self.m * 64 + (1 - y) * 32, 8), 32), :],
                             my.at[self.m], y_id)

        def zs(self):
            return [remote(self.part(y * 32 + ((z + k) % 4) * 8, 8), mz.at[self.m, k - 1],
                           m_tri_s.at[self.m, k - 1], m_tri_r.at[self.m, k - 1], z_ids[k - 1]) for k in (1, 2, 3)]

        def back_zs(self):
            return [remote(self.part(y * 32 + z * 8, 8), self.out(cp, y * 32 + z * 8, 8),
                           m_tri_as.at[self.m, k - 1], m_tri_ar.at[self.m, k - 1], z_ids[k - 1]) for k in (1, 2, 3)]

        def keep(self):
            return pltpu.make_async_copy(self.part(y * 32 + z * 8, 8), self.out(cp, y * 32 + z * 8, 8),
                                         m_one.at[self.m, 1])

        def back_y(self):
            return self.pair(1, self.out(cp, y * 32, 32), self.out(cp, y * 32, 32), y_id)

        def back_x(self):
            return self.pair(2, self.out(cp, 0, 64), self.out(cp, 0, 64), x_id)

        def back_core(self):
            return self.pair(3, self.out(cp, 0, 64), self.out(cp, 0, 64), core_id)

        def back_far(self):
            far = 2 * (1 - x) + c
            return self.pair(4, self.out(far, 0, 64), self.out(far, 0, 64), core_id)

    def mine_take(s, m):
        w = Mine(m)
        if s == 1:
            w.load().wait()
            w.ys().wait_recv()
            add_into(w.part(y * 32, 32), my.at[m])
        elif s == 2:
            for cpy in w.zs():
                cpy.wait_recv()
            dst = w.part(y * 32 + z * 8, 8)
            dst[...] = dst[...] + (mz[m, 0] + mz[m, 1] + mz[m, 2])
        elif s == 3:
            for cpy in w.back_zs():
                cpy.wait_recv()
            w.keep().wait()
        elif s == 4:
            w.back_y().wait_recv()
        elif s == 5:
            w.back_x().wait_recv()
        elif s == 6:
            w.back_core().wait_recv()
            w.back_far().wait_recv()
            for cpy in [w.ys()] + w.zs() + w.back_zs() + [w.back_y(), w.back_x(), w.back_core(), w.back_far()]:
                cpy.wait_send()

    def mine_give(s, m):
        w = Mine(m)
        todo = [lambda: [w.load(), w.ys()], w.zs, lambda: w.back_zs() + [w.keep()], lambda: [w.back_y()],
                lambda: [w.back_x(), w.back_core()], lambda: [w.back_far()]][s]
        for cpy in todo():
            cpy.start()

    def at_step(fn, t, s, n):
        u = t - LAG * s

        @pl.when((u >= 0) & (u < n))
        def _():
            fn(s, u)

    def step(t, carry):
        for s in range(8, 0, -1):
            at_step(up_take, t, s, n_up)
        for s in range(6, 0, -1):
            at_step(mine_take, t, s, n_mine)
        for s in range(7, -1, -1):
            at_step(up_give, t, s, n_up)
        for s in range(5, -1, -1):
            at_step(mine_give, t, s, n_mine)
        return carry

    lax.fori_loop(0, max(n_up + 8 * LAG, n_mine + 6 * LAG), step, 0)


def sum_grads(up, mine):
    n_up = up.shape[0] * up.shape[1] // (UNIT * WIDE)
    n_mine = mine.shape[0] // 64
    cols = mine.shape[1]
    dma = pltpu.SemaphoreType.DMA
    vm = lambda *shape: pltpu.VMEM(shape, F32)
    return pl.pallas_call(
        sum_kernel,
        out_shape=[jax.ShapeDtypeStruct(up.shape, F32), jax.ShapeDtypeStruct((4 * mine.shape[0], cols), F32)],
        in_specs=[ANY] * 2, out_specs=[ANY] * 2,
        scratch_shapes=[vm(n_up, UNIT // 2, WIDE), vm(n_up, UNIT // 2, WIDE), vm(n_up, UNIT // 4, WIDE),
                        vm(n_up, UNIT // 8, WIDE), vm(n_up, 3, UNIT // 32, WIDE),
                        vm(n_mine, 64, cols), vm(n_mine, 32, cols), vm(n_mine, 3, 8, cols),
                        dma((n_up, 2)), dma((n_up, 6, 2))] + [dma((n_up, 3))] * 4
                       + [dma((n_mine, 2)), dma((n_mine, 5, 2))] + [dma((n_mine, 3))] * 4,
        compiler_params=pltpu.CompilerParams(collective_id=0, has_side_effects=True,
                                             vmem_limit_bytes=56 * 1024 * 1024),
        cost_estimate=pl.CostEstimate(flops=200 * 10 ** 9, bytes_accessed=2 ** 26, transcendentals=0),
        name='sum_grads')(up, mine)


def tn(a, b):
    return lax.dot_general(a, b, (((0,), (0,)), ((), ())), preferred_element_type=F32)


def solution(mesh):
    cp_size = mesh.shape['cp']
    n_total = mesh.shape['dp'] * cp_size
    inv = 1.0 / n_total

    def flip(arr, bit):
        return lax.ppermute(arr, 'cp', [(i, i ^ bit) for i in range(cp_size)]) if bit else arr

    def per_device(x_in, d_out, w_q, w_k, w_v, w_o, w_up, w_down):
        rank = lax.axis_index('cp')
        x_own, g_out = x_in[0], d_out[0]
        tokens, d_model = x_own.shape
        width = d_model // cp_size
        n_pairs = width // 128
        w_t = [jnp.transpose(w, (1, 2, 0)).reshape(d_model // 128, 1, 128, d_model) for w in (w_q, w_k, w_v)]
        w_qkv = jnp.concatenate(w_t, axis=1).reshape(3 * d_model, d_model)
        wo2 = w_o.reshape(d_model, d_model)
        w_mine = lax.dynamic_slice(w_qkv, (rank * 3 * width, 0), (3 * width, d_model))
        slots = range(cp_size)

        x_all = [x_own, flip(x_own, 1), flip(x_own, 2)]
        grad_act = nt(g_out, w_down).astype(BF16)
        x_far, grad_act = lax.optimization_barrier((x_all[2], grad_act))
        x_all = [x_all[0], x_all[1], x_far, flip(x_far, 1)]
        seq_blk = jnp.arange(2 * cp_size)
        holder = jnp.where(seq_blk < cp_size, seq_blk, 2 * cp_size - 1 - seq_blk)
        tab = (2 * jnp.bitwise_xor(holder, rank) + (seq_blk >= cp_size)).astype(jnp.int32)
        qkv = [nt(x_j, w_mine).astype(BF16) for x_j in x_all]

        def absolute(parts, w):
            rel = jnp.concatenate(parts, axis=1)
            return jnp.concatenate([lax.dynamic_slice(rel, (0, (b ^ rank) * w), (tokens, w)) for b in slots], axis=1)

        attn_o, lses, o_parts = [], [], {}
        for pair in range(n_pairs):
            o_pair, lse = attn_fwd(tab, qkv, pair)
            attn_o.append(o_pair)
            lses.append(lse)
            for j in slots:
                o_parts[j, pair] = flip(o_pair[j * tokens:(j + 1) * tokens], j)
        o_own = absolute([o_parts[j, p] for j in slots for p in range(n_pairs)], width)

        hidden = (x_own.astype(F32) + nn(o_own, wo2)).astype(BF16)
        up_pre = nn(hidden, w_up).astype(BF16)
        act_val, gelu_pull = jax.vjp(functools.partial(jax.nn.gelu, approximate=True), up_pre.astype(F32))
        act_b = act_val.astype(BF16)
        grad_pre = gelu_pull(grad_act.astype(F32))[0].astype(BF16)
        grad_down = tn(act_b, g_out) * inv
        grad_hidden = (g_out.astype(F32) + nt(grad_pre, w_up)).astype(BF16)
        grad_attn = nt(grad_hidden, wo2).astype(BF16)
        grad_up = tn(hidden, grad_pre) * inv
        grad_o = tn(o_own, grad_hidden) * inv

        d_o = []
        for pair in range(n_pairs):
            pieces = [lax.dynamic_slice(grad_attn, (0, (rank ^ j) * width + 128 * pair), (tokens, 128)) for j in slots]
            d_o.append([flip(pieces[j], j) for j in slots])
        d_o[0], grad_down, grad_up, grad_o = lax.optimization_barrier((d_o[0], grad_down, grad_up, grad_o))
        grad_down, grad_o = lax.psum((grad_down, grad_o), ('dp', 'cp'))

        grads, back = [], {}
        for pair in range(n_pairs):
            parts = attn_bwd(tab, qkv, d_o[pair], attn_o[pair], lses[pair], pair)
            for j in slots:
                back[j, pair] = flip(parts[j], j)
            grads.append(sum(tn(parts[j], x_all[j]) for j in slots) * inv)
        mine = jnp.concatenate(grads, axis=0).reshape(n_pairs, 3, 128, d_model)
        mine = jnp.transpose(mine, (1, 0, 2, 3)).reshape(3 * width, d_model)
        grad_up, g_qkv = sum_grads(grad_up, mine)
        outs = [jnp.transpose(g_qkv[t * d_model:(t + 1) * d_model].reshape(w.shape[1], w.shape[2], d_model), (2, 0, 1))
                for t, w in enumerate((w_q, w_k, w_v))]
        back_abs = absolute([back[j, p] for j in slots for p in range(n_pairs)], 3 * width)
        d_x = (grad_hidden.astype(F32) + nn(back_abs, w_qkv)).astype(BF16)
        return (d_x[None], *outs, grad_o.reshape(w_o.shape), grad_up, grad_down)

    act_spec = P('dp', 'cp', None)
    return jax.shard_map(per_device, mesh=mesh,
                         in_specs=(act_spec, act_spec, P(), P(), P(), P(), P(), P()),
                         out_specs=(act_spec, P(), P(), P(), P(), P(), P()),
                         check_vma=False)
```

time: 2230 us -> 965 us (0.43)
  waiting for transfers between devices: 1210 us -> 204 us
  Pallas kernels: 0 us -> 520 us
  matrix products: 587 us -> 117 us
  starting transfers between devices: 119 us -> 16.7 us
  local copies, waits for them, and re-layouts: 155 us -> 65.5 us
  other arithmetic: 96.3 us -> 18.1 us
  loops' own time: 37.6 us -> 0 us
    psum x1, waiting for transfers between devices: 711 us -> 136 us  [per_device(): grad_down, grad_o = lax.psum((grad_down, grad_o), ('dp', 'cp'))]
    pallas_call x0 -> x5, Pallas kernels: none -> 520 us  [the longest x1 308 us: sum_grads(): pl.pallas_call(sum_kernel, out_shape=[jax.ShapeDtypeStruct(up.shape, F32)...]
    dot_general x74 -> x21, matrix products: 577 us -> 117 us  [the longest x11 51 us: tn(): lax.dot_general(a, b, (((0,), (0,)), ((), ())), preferred_element_type=F32)]
    ppermute x28 -> x21, waiting for transfers between devices: 498 us -> 67.3 us  [flip(): lax.ppermute(arr, 'cp', [(i, i ^ bit) for i in range(cp_size)])]
    ppermute x28 -> x21, starting transfers between devices: 119 us -> 16.6 us  [flip(): lax.ppermute(arr, 'cp', [(i, i ^ bit) for i in range(cp_size)])]
    while x28 -> x0, local copies, waits for them, and re-layouts: 66.3 us -> none
    another operation x12 -> x0, local copies, waits for them, and re-layouts: 51.9 us -> none
    reduce_sum x6 -> x0, other arithmetic: 51.5 us -> none  [block_forward(): row_sum = row_sum * factor + jnp.sum(prob_f, axis=-1)]
  transfers between devices with their start and end apart: 29 -> 22, of which waited for: 25 -> 9; matrix products, arithmetic and copies ran while one was open for 5% -> 9% of each run, Pallas kernels for 0% -> 45%
where the time goes in v1:
time: 965 us; the launch traced here: 956 us
  Pallas kernels  520 us (54%)
  waiting for transfers between devices  204 us (21%)
  matrix products  117 us (12%)
  local copies, waits for them, and re-layouts  65.5 us (7%)
  other arithmetic  18.1 us (2%)
  starting transfers between devices  16.7 us (2%)
  between operations  15.1 us (2%)
    pallas_call x1, Pallas kernels, sum_grads(): pl.pallas_call(sum_kernel, out_shape=[jax.ShapeDtypeStruct(up.shape, F32)...  308 us
    psum x1, waiting for transfers between devices, per_device(): grad_down, grad_o = lax.psum((grad_down, grad_o), ('dp', 'cp'))  136 us
    pallas_call x2, Pallas kernels, attn_bwd(): pl.pallas_call(functools.partial(attn_bwd_kernel, pair), out_shape=[jax.S...  120 us
    pallas_call x2, Pallas kernels, attn_fwd(): pl.pallas_call(functools.partial(attn_fwd_kernel, pair), out_shape=[jax.S...  92.2 us
    ppermute x21, waiting for transfers between devices, flip(): lax.ppermute(arr, 'cp', [(i, i ^ bit) for i in range(cp_size)])  67.3 us
    dot_general x11, matrix products, tn(): lax.dot_general(a, b, (((0,), (0,)), ((), ())), preferred_element_type=F32)  51 us
    unnamed x75, local copies, waits for them, and re-layouts  47.4 us
    dot_general x7, matrix products, nt(): lax.dot_general(a, b, (((1,), (1,)), ((), ())), preferred_element_type=F32)  44 us
  transfers between devices with their start and end apart: 22, of which 9 were waited for; matrix products, arithmetic and copies ran while one was open for 9% of the time, Pallas kernels for 45%

profile of v1, /device:TPU:0, one launch (start us, length us, event | category | flops | bytes accessed | tf_op | source)
XLA Modules:
  0.0 956.4 jit_solution(4290680636551075582)
XLA Ops:
  7.2 3.0 collective-permute-start
  10.3 14.8 %convolution_convert_fusion.1 = bf16[1024,4096]{1,0:T(8,128)(2,1)} fusion(bf16[4096,1024]{1,0:T(8,128)(2,1)} %param.15, bf16[1,1024,1024]{2,1,0:T(8,128)(2,1)} %param.9), kind=kOutput, calls=%fused_computation.24 | convolution fusion | flops 8594128896 | bytes 18874368 | tf_op jit(solution)/shard_map/dot_general | solution.py:18
  25.1 31.1 %collective-permute-done = bf16[1024,1024]{1,0:T(8,128)(2,1)} collective-permute-done((bf16[1024,1024]{1,0:T(8,128)(2,1)}, bf16[1024,1024]{1,0:T(8,128)(2,1)}, u32[]{:S(2)}, u32[]{:S(2)}) %collective-permute-start) | collective-permute-done | bytes 2097184 | tf_op jit(solution)/shard_map/ppermute | solution.py:466
  56.2 3.7 pad_maximum_fusion
  59.9 1.8 fusion.29.refs_0_
  61.8 4.2 convolution_convert_fusion.4.refs_2_
  66.0 4.0 fusion.30.refs_1_
  70.0 5.1 convolution_convert_fusion.3.refs_3_
  75.2 46.2 %attn_fwd.3 = (bf16[4096,128]{1,0:T(8,128)(2,1)S(1)}, f32[1,2,4096]{2,1,0:T(2,128)S(1)}) custom-call(s32[8]{0:T(128)S(1)} %fusion.39.tab_ref, bf16[1024,768]{1,0:T(8,128)(2,1)S(1)} %fusion.29.refs_0_, bf16[1024,768]{1,0:T(8,128)(2,1)S(1)} %fusion.30.refs_1_, bf16[1024,768]{1,0:T(8,128)(2,1)S(1)} %convolution_convert_fusion.4.refs_2_, ...), custom_call_target="tpu_custom_call" | custom-call | flops 17179869184 | bytes 8388608 | tf_op jit(solution)/shard_map/attn_fwd/pallas_call | solution.py:167
  121.4 46.0 %attn_fwd.2 = (bf16[4096,128]{1,0:T(8,128)(2,1)S(1)}, f32[1,2,4096]{2,1,0:T(2,128)S(1)}) custom-call(s32[8]{0:T(128)S(1)} %fusion.39.tab_ref, bf16[1024,768]{1,0:T(8,128)(2,1)S(1)} %fusion.29.refs_0_, bf16[1024,768]{1,0:T(8,128)(2,1)S(1)} %fusion.30.refs_1_, bf16[1024,768]{1,0:T(8,128)(2,1)S(1)} %convolution_convert_fusion.4.refs_2_, ...), custom_call_target="tpu_custom_call" | custom-call | flops 17179869184 | bytes 8388608 | tf_op jit(solution)/shard_map/attn_fwd/pallas_call | solution.py:167
  167.4 1.0 fusion.56
  169.8 1.0 fusion.55
  170.8 1.7 collective-permute-start.5
  172.9 1.3 collective-permute-start.7
  175.3 1.7 constant_dynamic-update-slice_fusion.4
  177.0 3.3 collective-permute-done.5
  180.3 1.7 constant_dynamic-update-slice_fusion.3
  182.0 3.8 collective-permute-done.6
  186.6 4.3 collective-permute-done.7
  191.5 4.6 collective-permute-done.8
  196.8 1.7 constant_dynamic-slice_fusion.15
  198.6 2.3 add_convert_fusion.2
  200.9 1.3 copy-done.18
  202.2 11.4 %convolution_convert_fusion = bf16[1024,4096]{1,0:T(8,128)(2,1)S(1)} fusion(bf16[1024,1024]{1,0:T(8,128)(2,1)S(1)} %add_convert_fusion.2, bf16[1024,4096]{1,0:T(8,128)(2,1)} %param.14), kind=kOutput, calls=%fused_computation.23 | convolution fusion | flops 8594128896 | bytes 18874368 | tf_op jit(solution)/shard_map/dot_general | solution.py:22
  213.7 3.3 copy-done.13
  217.0 16.1 %convolution_multiply_fusion = f32[4096,1024]{1,0:T(8,128)} fusion(bf16[1024,4096]{1,0:T(8,128)(2,1)S(1)} %convolution_convert_fusion, bf16[1,1024,1024]{2,1,0:T(8,128)(2,1)} %param.9), kind=kOutput, calls=%fused_computation.17 | convolution fusion | flops 8636071936 | bytes 27262976 | tf_op jit(solution)/shard_map/dot_general | solution.py:457
  233.1 14.0 %fusion.3 = bf16[1024,4096]{1,0:T(8,128)(2,1)S(1)} fusion(bf16[1024,4096]{1,0:T(8,128)(2,1)S(1)} %bitcast.80, bf16[1024,4096]{1,0:T(8,128)(2,1)} %copy-done.13), kind=kLoop, calls=%fused_computation.9 | loop fusion | flops 92274688 | bytes 25165824 | tf_op jit(solution)/shard_map/convert_element_type | solution.py:506
  247.1 11.7 %add_convert_fusion.1 = bf16[1024,1024]{1,0:T(8,128)(2,1)S(1)} fusion(bf16[1,1024,1024]{2,1,0:T(8,128)(2,1)} %param.9, bf16[1024,4096]{1,0:T(8,128)(2,1)S(1)} %fusion.3, bf16[1024,4096]{1,0:T(8,128)(2,1)} %param.14), kind=kOutput, calls=%fused_computation.35 | convolution fusion | flops 8593080320 | bytes 20971520 | tf_op jit(solution)/shard_map/dot_general | solution.py:18
  258.8 11.7 %convolution_multiply_fusion.1.up_ref = f32[1024,4096]{1,0:T(8,128)} fusion(bf16[1024,1024]{1,0:T(8,128)(2,1)S(1)} %copy-done.19, bf16[1024,4096]{1,0:T(8,128)(2,1)S(1)} %fusion.3), kind=kOutput, calls=%fused_computation.18 | convolution fusion | flops 8594128896 | bytes 27262976 | tf_op jit(solution)/shard_map/dot_general | solution.py:457
  270.6 2.4 convolution_convert_fusion.2
  273.9 1.7 collective-permute-start.13
  275.6 4.4 convolution_multiply_fusion.2
  280.4 1.7 collective-permute-start.10
  283.1 4.9 collective-permute-done.14.refs_7_
  287.9 59.8 %attn_bwd.3 = (bf16[1024,384]{1,0:T(8,128)(2,1)S(1)}, bf16[1024,384]{1,0:T(8,128)(2,1)}, bf16[1024,384]{1,0:T(8,128)(2,1)}, bf16[1024,384]{1,0:T(8,128)(2,1)S(1)}) custom-call(s32[8]{0:T(128)S(1)} %fusion.39.tab_ref, bf16[1024,768]{1,0:T(8,128)(2,1)} %copy-done.10, bf16[1024,768]{1,0:T(8,128)(2,1)} %copy-done.12, bf16[1024,768]{1,0:T(8,128)(2,1)} %copy-done.11, ...), custom_call_target="tpu_custom_call" | custom-call | flops 42949672960 | bytes 8388608 | tf_op jit(solution)/shard_map/attn_bwd/pallas_call | solution.py:186
  347.8 1.0 collective-permute-start.18
  348.8 2.8 fusion.60
  351.7 60.3 %attn_bwd.2 = (bf16[1024,384]{1,0:T(8,128)(2,1)S(1)}, bf16[1024,384]{1,0:T(8,128)(2,1)}, bf16[1024,384]{1,0:T(8,128)(2,1)}, bf16[1024,384]{1,0:T(8,128)(2,1)}) custom-call(s32[8]{0:T(128)S(1)} %fusion.39.tab_ref, bf16[1024,768]{1,0:T(8,128)(2,1)} %copy-done.10, bf16[1024,768]{1,0:T(8,128)(2,1)} %copy-done.12, bf16[1024,768]{1,0:T(8,128)(2,1)} %copy-done.11, ...), custom_call_target="tpu_custom_call" | custom-call | flops 42949672960 | bytes 8388608 | tf_op jit(solution)/shard_map/attn_bwd/pallas_call | solution.py:186
  412.0 1.1 collective-permute-start.17
  413.1 2.8 fusion.58
  416.8 1.0 collective-permute-start.19
  417.8 1.0 fusion.45
  418.8 1.0 fusion.47
  419.8 2.8 fusion.59
  422.7 2.8 fusion.57
  425.5 2.9 add_multiply_fusion.1
  428.4 2.6 add_multiply_fusion
  431.4 1.9 copy.20
  433.4 308.2 %sum_grads.1 = (f32[1024,4096]{1,0:T(8,128)}, f32[3072,1024]{1,0:T(8,128)}) custom-call(f32[1024,4096]{1,0:T(8,128)} %convolution_multiply_fusion.1.up_ref, f32[768,1024]{1,0:T(8,128)} %bitcast.94), custom_call_target="tpu_custom_call" | custom-call | flops 199999995904 | bytes 67108864 | tf_op jit(solution)/shard_map/sum_grads/pallas_call | solution.py:441
  741.6 10.3 %fusion.54 = (f32[1024,1024]{1,0:T(8,128)}, f32[1024,1024]{1,0:T(8,128)}, f32[1024,1024]{1,0:T(8,128)}) fusion(f32[3072,1024]{1,0:T(8,128)} %get-tuple-element.49), kind=kLoop, calls=%fused_computation.109 | loop fusion | bytes 25165824 | tf_op jit(solution)/shard_map/slice | solution.py:529
  752.0 1.0 collective-permute-start.20
  753.3 1.4 constant_dynamic-update-slice_fusion.11
  754.7 1.4 constant_dynamic-update-slice_fusion.10
  756.1 1.4 constant_dynamic-update-slice_fusion.9
  757.4 1.4 constant_dynamic-update-slice_fusion.8
  758.8 1.4 constant_dynamic-update-slice_fusion.7
  760.2 14.3 %collective-permute-done.20 = bf16[1024,384]{1,0:T(8,128)(2,1)S(1)} collective-permute-done((bf16[1024,384]{1,0:T(8,128)(2,1)S(1)}, bf16[1024,384]{1,0:T(8,128)(2,1)S(1)}, u32[]{:S(2)}, u32[]{:S(2)}) %collective-permute-start.20) | collective-permute-done | bytes 786464 | tf_op jit(solution)/shard_map/ppermute | solution.py:466
  775.6 1.1 slice-done.6
  778.1 8.0 fusion.24
  786.1 136.5 %all-reduce.3.cloned.1.call-done = (f32[16,64,1024]{2,1,0:T(8,128)}, f32[4096,1024]{1,0:T(8,128)}) async-done(((f32[16,64,1024]{2,1,0:T(8,128)}, f32[4096,1024]{1,0:T(8,128)}), (f32[16,64,1024]{2,1,0:T(8,128)}, f32[4096,1024]{1,0:T(8,128)})) %all-reduce.3.cloned.1.call-update) | async-done | bytes 20971536 | tf_op jit(solution)/shard_map/psum | solution.py:518
  922.5 4.9 copy.40
  927.5 13.5 %copy.41 = f32[1024,4096]{1,0:T(8,128)} copy(f32[1024,4096]{1,0:T(8,128)} %get-tuple-element.94) | data formatting | bytes 33554432
  941.0 1.8 slice-done.3
  942.8 6.3 copy.42
  (98 shorter events, 11.7 us)
Async XLA Ops:
  7.2 191.4 %copy-start = (bf16[16,64,1024]{2,1,0:T(8,128)(2,1)S(1)}, bf16[16,64,1024]{2,1,0:T(8,128)(2,1)}, u32[]{:S(2)}) copy-start(bf16[16,64,1024]{2,1,0:T(8,128)(2,1)} %param.13) | copy-start | bytes 6291460
  7.2 915.3 %all-reduce.3.cloned.1.call-start = ((), (), s32[]{:S(2)}) async-start(), calls=%async_computation | async-start | bytes 41943040 | tf_op jit(solution)/shard_map/psum | solution.py:518
  7.2 49.0 %collective-permute-start = (bf16[1024,1024]{1,0:T(8,128)(2,1)}, bf16[1024,1024]{1,0:T(8,128)(2,1)}, u32[]{:S(2)}, u32[]{:S(2)}) collective-permute-start(bf16[1024,1024]{1,0:T(8,128)(2,1)} %bitcast.81), channel_id=1, source_target_pairs={{0,2},{1,3},{2,0},{3,1},{4,6},{5,7},{6,4},{7,5},{8,10},{9,11},{10,... | collective-permute-start | bytes 6291464 | tf_op jit(solution)/shard_map/ppermute | solution.py:466
  10.3 55.7 %collective-permute-start.1 = (bf16[1024,1024]{1,0:T(8,128)(2,1)}, bf16[1024,1024]{1,0:T(8,128)(2,1)}, u32[]{:S(2)}, u32[]{:S(2)}) collective-permute-start(bf16[1024,1024]{1,0:T(8,128)(2,1)} %bitcast.82), channel_id=1, source_target_pairs={{0,1},{1,0},{2,3},{3,2},{4,5},{5,4},{6,7},{7,6},{8,9},{9,8},{10,11... | collective-permute-start | bytes 6291464 | tf_op jit(solution)/shard_map/ppermute | solution.py:466
  56.2 13.8 %collective-permute-start.2 = (bf16[1024,1024]{1,0:T(8,128)(2,1)}, bf16[1024,1024]{1,0:T(8,128)(2,1)}, u32[]{:S(2)}, u32[]{:S(2)}) collective-permute-start(bf16[1024,1024]{1,0:T(8,128)(2,1)} %collective-permute-done), channel_id=1, source_target_pairs={{0,1},{1,0},{2,3},{3,2},{4,5},{5,4},{6,7},{7,6},{8,9},{9,8},{10,11... | collective-permute-start | bytes 6291464 | tf_op jit(solution)/shard_map/ppermute | solution.py:466
  56.2 3.7 copy-start.14
  59.9 10.1 %copy-start.17 = (bf16[8,3,128,1024]{3,2,1,0:T(8,128)(2,1)}, bf16[8,3,128,1024]{3,2,1,0:T(8,128)(2,1)S(1)}, u32[]{:S(2)}) copy-start(bf16[8,3,128,1024]{3,2,1,0:T(8,128)(2,1)S(1)} %pad_maximum_fusion) | copy-start | bytes 18874372
  61.8 59.6 %copy-start.10 = (bf16[1024,768]{1,0:T(8,128)(2,1)}, bf16[1024,768]{1,0:T(8,128)(2,1)S(1)}, u32[]{:S(2)}) copy-start(bf16[1024,768]{1,0:T(8,128)(2,1)S(1)} %fusion.29.refs_0_) | copy-start | bytes 4718596
  66.0 55.4 %copy-start.11 = (bf16[1024,768]{1,0:T(8,128)(2,1)}, bf16[1024,768]{1,0:T(8,128)(2,1)S(1)}, u32[]{:S(2)}) copy-start(bf16[1024,768]{1,0:T(8,128)(2,1)S(1)} %convolution_convert_fusion.4.refs_2_) | copy-start | bytes 4718596
  70.0 51.4 %copy-start.12 = (bf16[1024,768]{1,0:T(8,128)(2,1)}, bf16[1024,768]{1,0:T(8,128)(2,1)S(1)}, u32[]{:S(2)}) copy-start(bf16[1024,768]{1,0:T(8,128)(2,1)S(1)} %fusion.30.refs_1_) | copy-start | bytes 4718596
  168.4 1.0 copy-start.8
  169.3 4.8 collective-permute-start.3
  170.8 4.5 collective-permute-start.4
  170.8 9.5 collective-permute-start.5
  172.6 13.3 %collective-permute-start.6 = (bf16[1024,128]{1,0:T(8,128)(2,1)}, bf16[1024,128]{1,0:T(8,128)(2,1)S(1)}, u32[]{:S(2)}, u32[]{:S(2)}) collective-permute-start(bf16[1024,128]{1,0:T(8,128)(2,1)} %get-tuple-element.75), channel_id=1, source_target_pairs={{0,2},{1,3},{2,0},{3,1},{4,6},{5,7},{6,4},{7,5},{8,10},{9,11},{10,... | collective-permute-start | bytes 786440 | tf_op jit(solution)/shard_map/ppermute | solution.py:466
  172.9 18.0 %collective-permute-start.7 = (bf16[1024,128]{1,0:T(8,128)(2,1)}, bf16[1024,128]{1,0:T(8,128)(2,1)S(1)}, u32[]{:S(2)}, u32[]{:S(2)}) collective-permute-start(bf16[1024,128]{1,0:T(8,128)(2,1)} %get-tuple-element.78), channel_id=1, source_target_pairs={{0,3},{1,2},{2,1},{3,0},{4,7},{5,6},{6,5},{7,4},{8,11},{9,10},{10,... | collective-permute-start | bytes 786440 | tf_op jit(solution)/shard_map/ppermute | solution.py:466
  174.1 22.0 %collective-permute-start.8 = (bf16[1024,128]{1,0:T(8,128)(2,1)}, bf16[1024,128]{1,0:T(8,128)(2,1)S(1)}, u32[]{:S(2)}, u32[]{:S(2)}) collective-permute-start(bf16[1024,128]{1,0:T(8,128)(2,1)} %get-tuple-element.74), channel_id=1, source_target_pairs={{0,3},{1,2},{2,1},{3,0},{4,7},{5,6},{6,5},{7,4},{8,11},{9,10},{10,... | collective-permute-start | bytes 786440 | tf_op jit(solution)/shard_map/ppermute | solution.py:466
  177.0 21.5 %copy-start.15 = (bf16[1,1024,1024]{2,1,0:T(8,128)(2,1)S(1)}, bf16[1,1024,1024]{2,1,0:T(8,128)(2,1)}, u32[]{:S(2)}) copy-start(bf16[1,1024,1024]{2,1,0:T(8,128)(2,1)} %param.8) | copy-start | bytes 6291460
  198.5 34.5 %slice-start.4 = ((s8[8388608]{0:T(1024)(128)(4,1)}), s8[4194304]{0:T(1024)(128)(4,1)S(1)}, s32[]{:S(2)}) async-start(s8[8388608]{0:T(1024)(128)(4,1)} %bitcast.79), calls=%async_computation.5 | async-start | bytes 8388608
  200.9 1.3 copy-start.18
  202.2 30.8 %slice-start.5 = ((s8[8388608]{0:T(1024)(128)(4,1)}), s8[4194304]{0:T(1024)(128)(4,1)S(1)}, s32[]{:S(2)}) async-start(s8[8388608]{0:T(1024)(128)(4,1)} %bitcast.79), calls=%async_computation.6 | async-start | bytes 8388608
  213.6 3.3 copy-start.13
  247.1 11.7 %copy-start.19 = (bf16[1024,1024]{1,0:T(8,128)(2,1)S(1)}, bf16[1024,1024]{1,0:T(8,128)(2,1)}, u32[]{:S(2)}) copy-start(bf16[1024,1024]{1,0:T(8,128)(2,1)} %copy-done.18) | copy-start | bytes 6291460
  258.8 16.8 %copy-start.20 = (bf16[1024,1024]{1,0:T(8,128)(2,1)}, bf16[1024,1024]{1,0:T(8,128)(2,1)S(1)}, u32[]{:S(2)}) copy-start(bf16[1024,1024]{1,0:T(8,128)(2,1)S(1)} %add_convert_fusion.1) | copy-start | bytes 6291460
  273.5 8.6 collective-permute-start.12
  273.9 9.2 collective-permute-start.13
  275.6 12.3 %collective-permute-start.14 = (bf16[1024,128]{1,0:T(8,128)(2,1)S(1)}, bf16[1024,128]{1,0:T(8,128)(2,1)S(1)}, u32[]{:S(2)}, u32[]{:S(2)}) collective-permute-start(bf16[1024,128]{1,0:T(8,128)(2,1)S(1)} %get-tuple-element.62), channel_id=1, source_target_pairs={{0,3},{1,2},{2,1},{3,0},{4,7},{5,6},{6,5},{7,4},{8,11},{9,10},{10,... | collective-permute-start | bytes 786440 | tf_op jit(solution)/shard_map/ppermute | solution.py:466
  280.0 71.6 %collective-permute-start.9 = (bf16[1024,128]{1,0:T(8,128)(2,1)S(1)}, bf16[1024,128]{1,0:T(8,128)(2,1)S(1)}, u32[]{:S(2)}, u32[]{:S(2)}) collective-permute-start(bf16[1024,128]{1,0:T(8,128)(2,1)S(1)} %get-tuple-element.68), channel_id=1, source_target_pairs={{0,1},{1,0},{2,3},{3,2},{4,5},{5,4},{6,7},{7,6},{8,9},{9,8},{10,11... | collective-permute-start | bytes 786440 | tf_op jit(solution)/shard_map/ppermute | solution.py:466
  280.4 71.2 %collective-permute-start.10 = (bf16[1024,128]{1,0:T(8,128)(2,1)S(1)}, bf16[1024,128]{1,0:T(8,128)(2,1)S(1)}, u32[]{:S(2)}, u32[]{:S(2)}) collective-permute-start(bf16[1024,128]{1,0:T(8,128)(2,1)S(1)} %get-tuple-element.67), channel_id=1, source_target_pairs={{0,2},{1,3},{2,0},{3,1},{4,6},{5,7},{6,4},{7,5},{8,10},{9,11},{10,... | collective-permute-start | bytes 786440 | tf_op jit(solution)/shard_map/ppermute | solution.py:466
  282.2 69.5 %collective-permute-start.11 = (bf16[1024,128]{1,0:T(8,128)(2,1)S(1)}, bf16[1024,128]{1,0:T(8,128)(2,1)S(1)}, u32[]{:S(2)}, u32[]{:S(2)}) collective-permute-start(bf16[1024,128]{1,0:T(8,128)(2,1)S(1)} %get-tuple-element.66), channel_id=1, source_target_pairs={{0,3},{1,2},{2,1},{3,0},{4,7},{5,6},{6,5},{7,4},{8,11},{9,10},{10,... | collective-permute-start | bytes 786440 | tf_op jit(solution)/shard_map/ppermute | solution.py:466
  347.7 70.1 %copy-start.2 = (bf16[1024,384]{1,0:T(8,128)(2,1)}, bf16[1024,384]{1,0:T(8,128)(2,1)S(1)}, u32[]{:S(2)}) copy-start(bf16[1024,384]{1,0:T(8,128)(2,1)S(1)} %get-tuple-element.41) | copy-start | bytes 2359300
  347.7 80.6 %copy-start.6 = (bf16[1024,384]{1,0:T(8,128)(2,1)}, bf16[1024,384]{1,0:T(8,128)(2,1)S(1)}, u32[]{:S(2)}) copy-start(bf16[1024,384]{1,0:T(8,128)(2,1)S(1)} %get-tuple-element.47) | copy-start | bytes 2359300
  347.8 3.9 copy-start.9
  347.8 409.7 %collective-permute-start.18 = (bf16[1024,384]{1,0:T(8,128)(2,1)}, bf16[1024,384]{1,0:T(8,128)(2,1)}, u32[]{:S(2)}, u32[]{:S(2)}) collective-permute-start(bf16[1024,384]{1,0:T(8,128)(2,1)} %get-tuple-element.45), channel_id=1, source_target_pairs={{0,2},{1,3},{2,0},{3,1},{4,6},{5,7},{6,4},{7,5},{8,10},{9,11},{10,... | collective-permute-start | bytes 2359304 | tf_op jit(solution)/shard_map/ppermute | solution.py:466
  411.9 6.9 copy-start.4
  412.0 5.9 copy-start.16
  412.0 344.1 %collective-permute-start.17 = (bf16[1024,384]{1,0:T(8,128)(2,1)}, bf16[1024,384]{1,0:T(8,128)(2,1)}, u32[]{:S(2)}, u32[]{:S(2)}) collective-permute-start(bf16[1024,384]{1,0:T(8,128)(2,1)} %get-tuple-element.44), channel_id=1, source_target_pairs={{0,2},{1,3},{2,0},{3,1},{4,6},{5,7},{6,4},{7,5},{8,10},{9,11},{10,... | collective-permute-start | bytes 2359304 | tf_op jit(solution)/shard_map/ppermute | solution.py:466
  415.9 336.1 %collective-permute-start.15 = (bf16[1024,384]{1,0:T(8,128)(2,1)}, bf16[1024,384]{1,0:T(8,128)(2,1)}, u32[]{:S(2)}, u32[]{:S(2)}) collective-permute-start(bf16[1024,384]{1,0:T(8,128)(2,1)} %get-tuple-element.42), channel_id=1, source_target_pairs={{0,1},{1,0},{2,3},{3,2},{4,5},{5,4},{6,7},{7,6},{8,9},{9,8},{10,11... | collective-permute-start | bytes 2359304 | tf_op jit(solution)/shard_map/ppermute | solution.py:466
  416.7 337.9 %collective-permute-start.16 = (bf16[1024,384]{1,0:T(8,128)(2,1)}, bf16[1024,384]{1,0:T(8,128)(2,1)}, u32[]{:S(2)}, u32[]{:S(2)}) collective-permute-start(bf16[1024,384]{1,0:T(8,128)(2,1)} %get-tuple-element.43), channel_id=1, source_target_pairs={{0,1},{1,0},{2,3},{3,2},{4,5},{5,4},{6,7},{7,6},{8,9},{9,8},{10,11... | collective-permute-start | bytes 2359304 | tf_op jit(solution)/shard_map/ppermute | solution.py:466
  416.8 342.0 %collective-permute-start.19 = (bf16[1024,384]{1,0:T(8,128)(2,1)}, bf16[1024,384]{1,0:T(8,128)(2,1)}, u32[]{:S(2)}, u32[]{:S(2)}) collective-permute-start(bf16[1024,384]{1,0:T(8,128)(2,1)} %get-tuple-element.46), channel_id=1, source_target_pairs={{0,3},{1,2},{2,1},{3,0},{4,7},{5,6},{6,5},{7,4},{8,11},{9,10},{10,... | collective-permute-start | bytes 2359304 | tf_op jit(solution)/shard_map/ppermute | solution.py:466
  741.6 10.3 %copy-start.5 = (bf16[1024,384]{1,0:T(8,128)(2,1)S(1)}, bf16[1024,384]{1,0:T(8,128)(2,1)}, u32[]{:S(2)}) copy-start(bf16[1024,384]{1,0:T(8,128)(2,1)} %copy-done.4) | copy-start | bytes 2359300
  741.6 10.5 %copy-start.7 = (bf16[1024,384]{1,0:T(8,128)(2,1)S(1)}, bf16[1024,384]{1,0:T(8,128)(2,1)}, u32[]{:S(2)}) copy-start(bf16[1024,384]{1,0:T(8,128)(2,1)} %copy-done.6) | copy-start | bytes 2359300
  741.6 11.5 %copy-start.3 = (bf16[1024,384]{1,0:T(8,128)(2,1)S(1)}, bf16[1024,384]{1,0:T(8,128)(2,1)}, u32[]{:S(2)}) copy-start(bf16[1024,384]{1,0:T(8,128)(2,1)} %copy-done.2) | copy-start | bytes 2359300
  752.0 22.5 %collective-permute-start.20 = (bf16[1024,384]{1,0:T(8,128)(2,1)S(1)}, bf16[1024,384]{1,0:T(8,128)(2,1)S(1)}, u32[]{:S(2)}, u32[]{:S(2)}) collective-permute-start(bf16[1024,384]{1,0:T(8,128)(2,1)S(1)} %copy-done.7), channel_id=1, source_target_pairs={{0,3},{1,2},{2,1},{3,0},{4,7},{5,6},{6,5},{7,4},{8,11},{9,10},{10,... | collective-permute-start | bytes 2359304 | tf_op jit(solution)/shard_map/ppermute | solution.py:466
  774.5 2.2 slice-start.6
  774.8 2.7 slice-start.7
  774.8 3.3 copy-start.21
  922.5 18.4 %slice-start = ((s8[16777216]{0:T(1024)(128)(4,1)}), s8[4194304]{0:T(1024)(128)(4,1)S(1)}, s32[]{:S(2)}) async-start(s8[16777216]{0:T(1024)(128)(4,1)} %bitcast.76), calls=%async_computation.1 | async-start | bytes 8388608
  927.5 13.5 %slice-start.1 = ((s8[16777216]{0:T(1024)(128)(4,1)}), s8[4194304]{0:T(1024)(128)(4,1)S(1)}, s32[]{:S(2)}) async-start(s8[16777216]{0:T(1024)(128)(4,1)} %bitcast.76), calls=%async_computation.2 | async-start | bytes 8388608
  927.5 13.5 %slice-start.2 = ((s8[16777216]{0:T(1024)(128)(4,1)}), s8[4194304]{0:T(1024)(128)(4,1)S(1)}, s32[]{:S(2)}) async-start(s8[16777216]{0:T(1024)(128)(4,1)} %bitcast.76), calls=%async_computation.3 | async-start | bytes 8388608
  927.5 15.3 %slice-start.3 = ((s8[16777216]{0:T(1024)(128)(4,1)}), s8[4194304]{0:T(1024)(128)(4,1)S(1)}, s32[]{:S(2)}) async-start(s8[16777216]{0:T(1024)(128)(4,1)} %bitcast.76), calls=%async_computation.4 | async-start | bytes 8388608
  942.8 6.3 copy-start.1
Sparse Core Ops, SparseCore 0:
  433.5 488.9 all-reduce.2

commit v2 on v1

--- a/solution.py
+++ b/solution.py
@@ -34,29 +34,30 @@
 def load_all(srcs, dsts, sem):
     copies = []
     for parts, dst in zip(srcs, dsts):
-        for j, (ref, c) in enumerate(parts):
-            rows = ref.shape[0]
-            copies.append(pltpu.make_async_copy(ref.at[:, pl.ds(c, 128)], dst.at[pl.ds(j * rows, rows), :], sem))
+        for b, (ref, row, col) in enumerate(parts):
+            copies.append(pltpu.make_async_copy(ref.at[pl.ds(row, BLK), pl.ds(col, 128)],
+                                                dst.at[pl.ds(b * BLK, BLK), :], sem))
     for c in copies:
         c.start()
     for c in copies:
         c.wait()
 
 
-def attn_fwd_kernel(pair, tab_ref, *refs):
-    qkv_refs = refs[:4]
-    o_ref, lse_ref, q_ref, k_ref, v_ref, vt_ref, sem = refs[4:]
-    n_blk = q_ref.shape[0] // BLK
+def attn_fwd_kernel(pair, n_in, first, tab_ref, *refs):
+    qkv_refs, o_refs = refs[:n_in], refs[n_in:n_in + 4]
+    lse_ref, q_ref, k_ref, v_ref, vt_ref, o_ref, sem = refs[n_in + 4:]
     step = pl.program_id(0)
+    seq = step + first
 
     @pl.when(step == 0)
     def _():
-        load_all([[(r, 384 * pair + 128 * t) for r in qkv_refs] for t in range(3)], [q_ref, k_ref, v_ref], sem)
-        for b in range(n_blk):
+        load_all([[(r, 0, 384 * pair + 128 * t) for r in (qkv_refs if t else qkv_refs[n_in - 4:])] for t in range(3)],
+                 [q_ref, k_ref, v_ref], sem)
+        for b in range(n_in):
             rows = pl.ds(b * BLK, BLK)
             vt_ref[:, rows] = v_ref[rows, :].astype(F32).T.astype(BF16)
 
-    q_off = pl.multiple_of(tab_ref[step] * BLK, BLK)
+    q_off = pl.multiple_of((tab_ref[seq] - first) * BLK, BLK)
     q_blk = q_ref[pl.ds(q_off, BLK), :] * jnp.asarray(0.125, BF16)
     q_half = [pick(q_blk, 0), pick(q_blk, 1)]
 
@@ -81,27 +82,33 @@
         return tuple(out)
 
     fresh = (jnp.full((1, BLK), NEG_BIG, F32), jnp.zeros((1, BLK), F32), jnp.zeros((64, BLK), F32))
-    state = lax.fori_loop(0, step, lambda j, st: update(j, st, False), fresh + fresh)
-    state = update(step, state, True)
+    state = lax.fori_loop(0, seq, lambda j, st: update(j, st, False), fresh + fresh)
+    state = update(seq, state, True)
     o_t = jnp.concatenate([state[2] / state[1], state[5] / state[4]], axis=0)
     o_ref[pl.ds(q_off, BLK), :] = o_t.T.astype(BF16)
     for h in range(2):
         lse_ref[0, h:h + 1, pl.ds(q_off, BLK)] = (state[3 * h] + jnp.log(state[3 * h + 1])) * LOG2E
 
+    @pl.when(step == 3)
+    def _():
+        for j in range(4):
+            o_refs[j][...] = o_ref[pl.ds(j * BLK, BLK), :]
+
 
 def attn_bwd_kernel(pair, tab_ref, *refs):
-    qkv_refs, do_refs = refs[:4], refs[4:8]
-    o_ref, lse_ref = refs[8:10]
-    out_refs = refs[10:14]
-    q_ref, k_ref, v_ref, do_ref, dqt_ref, dot_ref, dkv_ref, sem = refs[14:]
-    n_blk = q_ref.shape[0] // BLK
+    qkv_refs, do_refs, o_refs, lse_refs, out_refs = refs[:8], refs[8:12], refs[12:20], refs[20:22], refs[22:26]
+    q_ref, k_ref, v_ref, do_ref, o_ref, lse_ref, dqt_ref, dot_ref, dkv_ref, sem = refs[26:]
+    n_blk = 8
     step = pl.program_id(0)
 
     @pl.when(step == 0)
     def _():
-        load_all([[(r, 384 * pair + 128 * t) for r in qkv_refs] for t in range(3)] + [[(r, 0) for r in do_refs]],
-                 [q_ref, k_ref, v_ref, do_ref], sem)
+        load_all([[(r, 0, 384 * pair + 128 * t) for r in qkv_refs] for t in range(3)]
+                 + [[(do_refs[b % 4], (b // 4) * BLK, 0) for b in range(8)], [(r, 0, 0) for r in o_refs]],
+                 [q_ref, k_ref, v_ref, do_ref, o_ref], sem)
         dqt_ref[...] = jnp.zeros_like(dqt_ref)
+        for i in range(2):
+            lse_ref[:, i * 4 * BLK:(i + 1) * 4 * BLK] = lse_refs[i][0]
         for b in range(n_blk):
             rows = pl.ds(b * BLK, BLK)
             prod = (do_ref[rows, :].astype(F32) * o_ref[rows, :].astype(F32)).T
@@ -126,7 +133,7 @@
                 kk = lax.broadcasted_iota(jnp.int32, (BLK, BLK), 0)
                 qq = lax.broadcasted_iota(jnp.int32, (BLK, BLK), 1)
                 s = jnp.where(kk <= qq, s, NEG_BIG)
-            p = jnp.exp2(s * LOG2E - lse_ref[0, h:h + 1, pl.ds(off, BLK)])
+            p = jnp.exp2(s * LOG2E - lse_ref[h:h + 1, pl.ds(off, BLK)])
             dp = nt(v_blk, do_h).astype(BF16).astype(F32)
             ds = (p * (dp - dot_ref[h:h + 1, pl.ds(off, BLK)])).astype(BF16)
             dv = dv + nn(p.astype(BF16), do_h)
@@ -143,58 +150,108 @@
 
     @pl.when(step == n_blk - 1)
     def _():
-        rows = q_ref.shape[0] // 4
-        for j in range(4):
-            span = pl.ds(j * rows, rows)
-            out_refs[j][:, 0:128] = (dqt_ref[:, span] * 0.125).T.astype(BF16)
-            out_refs[j][:, 128:384] = dkv_ref[span, :]
-
-
-def pair_cost(seq_len, n_dots):
-    return pl.CostEstimate(flops=2 * seq_len * seq_len * 128 * n_dots * 2, bytes_accessed=16 * seq_len * 128,
-                           transcendentals=seq_len * seq_len)
+        for b in range(n_blk):
+            span = pl.ds(b * BLK, BLK)
+            dst = pl.ds((b // 4) * BLK, BLK)
+            out_refs[b % 4][dst, 0:128] = (dqt_ref[:, span] * 0.125).T.astype(BF16)
+            out_refs[b % 4][dst, 128:384] = dkv_ref[span, :]
+
+
+def pair_cost(n_pairs, n_dots):
+    return pl.CostEstimate(flops=2 * n_pairs * BLK * BLK * 128 * n_dots * 6, bytes_accessed=2 ** 22,
+                           transcendentals=2 * n_pairs * BLK * BLK)
 
 
 ANY = pl.BlockSpec(memory_space=pl.ANY)
 
 
-def attn_fwd(tab, qkv, pair):
-    rows = qkv[0].shape[0]
-    seq_len = 4 * rows
-    n_blk = seq_len // BLK
-    whole = pl.BlockSpec((seq_len, 128), lambda i, tab: (0, 0))
-    buf = pltpu.VMEM((seq_len, 128), BF16)
+def attn_fwd(tab, qkv, pair, first):
+    n_in = len(qkv)
+    half = 4 * BLK
+    buf = lambda n: pltpu.VMEM((n * BLK, 128), BF16)
     return pl.pallas_call(
-        functools.partial(attn_fwd_kernel, pair),
-        out_shape=[jax.ShapeDtypeStruct((seq_len, 128), BF16), jax.ShapeDtypeStruct((1, 2, seq_len), F32)],
+        functools.partial(attn_fwd_kernel, pair, n_in, first),
+        out_shape=[jax.ShapeDtypeStruct((BLK, 128), BF16)] * 4 + [jax.ShapeDtypeStruct((1, 2, half), F32)],
         grid_spec=pltpu.PrefetchScalarGridSpec(
-            num_scalar_prefetch=1, grid=(n_blk,),
-            in_specs=[ANY] * 4,
-            out_specs=[whole, pl.BlockSpec((1, 2, seq_len), lambda i, tab: (0, 0, 0))],
-            scratch_shapes=[buf, buf, buf, pltpu.VMEM((128, seq_len), BF16), pltpu.SemaphoreType.DMA]),
+            num_scalar_prefetch=1, grid=(4,),
+            in_specs=[ANY] * n_in,
+            out_specs=[pl.BlockSpec((BLK, 128), lambda i, tab: (0, 0))] * 4
+                      + [pl.BlockSpec((1, 2, half), lambda i, tab: (0, 0, 0))],
+            scratch_shapes=[buf(4), buf(n_in), buf(n_in), pltpu.VMEM((128, n_in * BLK), BF16), buf(4),
+                            pltpu.SemaphoreType.DMA]),
         compiler_params=pltpu.CompilerParams(vmem_limit_bytes=48 * 1024 * 1024),
-        cost_estimate=pair_cost(seq_len, 2),
+        cost_estimate=pair_cost(26 if first else 10, 2),
         name='attn_fwd')(tab, *qkv)
 
 
-def attn_bwd(tab, qkv, d_o, out_o, lse, pair):
-    rows = qkv[0].shape[0]
-    seq_len = 4 * rows
-    n_blk = seq_len // BLK
-    whole = pl.BlockSpec((seq_len, 128), lambda i, tab: (0, 0))
+def attn_bwd(tab, qkv, d_o, out_o, lses, pair):
+    seq_len = 8 * BLK
     buf = pltpu.VMEM((seq_len, 128), BF16)
     return pl.pallas_call(
         functools.partial(attn_bwd_kernel, pair),
-        out_shape=[jax.ShapeDtypeStruct((rows, 384), BF16)] * 4,
+        out_shape=[jax.ShapeDtypeStruct((2 * BLK, 384), BF16)] * 4,
         grid_spec=pltpu.PrefetchScalarGridSpec(
-            num_scalar_prefetch=1, grid=(n_blk,),
-            in_specs=[ANY] * 8 + [whole, pl.BlockSpec((1, 2, seq_len), lambda i, tab: (0, 0, 0))],
-            out_specs=[pl.BlockSpec((rows, 384), lambda i, tab: (0, 0))] * 4,
-            scratch_shapes=[buf, buf, buf, buf, pltpu.VMEM((128, seq_len), F32), pltpu.VMEM((2, seq_len), F32),
-                            pltpu.VMEM((seq_len, 256), BF16), pltpu.SemaphoreType.DMA]),
+            num_scalar_prefetch=1, grid=(8,),
+            in_specs=[ANY] * 20 + [pl.BlockSpec((1, 2, seq_len // 2), lambda i, tab: (0, 0, 0))] * 2,
+            out_specs=[pl.BlockSpec((2 * BLK, 384), lambda i, tab: (0, 0))] * 4,
+            scratch_shapes=[buf, buf, buf, buf, buf, pltpu.VMEM((2, seq_len), F32), pltpu.VMEM((128, seq_len), F32),
+                            pltpu.VMEM((2, seq_len), F32), pltpu.VMEM((seq_len, 256), BF16), pltpu.SemaphoreType.DMA]),
         compiler_params=pltpu.CompilerParams(vmem_limit_bytes=48 * 1024 * 1024),
-        cost_estimate=pair_cost(seq_len, 5),
-        name='attn_bwd')(tab, *qkv, *d_o, out_o, lse)
+        cost_estimate=pair_cost(36, 5),
+        name='attn_bwd')(tab, *qkv, *d_o, *out_o, *lses)
+
+
+def attend_out_kernel(rank_ref, x_ref, wo_ref, *refs):
+    parts, hid_ref, o_ref = refs[:16], refs[16], refs[17]
+    for i in range(2):
+        for j in range(4):
+            for p in range(2):
+                col = pl.multiple_of(rank_ref[1 + j] * 256 + 128 * p, 128)
+                o_ref[pl.ds(i * BLK, BLK), pl.ds(col, 128)] = parts[8 * i + 2 * j + p][...]
+
+    def tile(t, carry):
+        rows = pl.ds(pl.multiple_of(t * 256, 256), 256)
+        hid_ref[rows, :] = (x_ref[rows, :].astype(F32) + nn(o_ref[rows, :], wo_ref[...])).astype(BF16)
+        return carry
+
+    lax.fori_loop(0, x_ref.shape[0] // 256, tile, 0)
+
+
+def attend_out(where, x, wo, parts):
+    return pl.pallas_call(
+        attend_out_kernel,
+        out_shape=[jax.ShapeDtypeStruct(x.shape, BF16)] * 2,
+        in_specs=[pl.BlockSpec(memory_space=pltpu.SMEM)] + [pl.BlockSpec(memory_space=pltpu.VMEM)] * 18,
+        out_specs=[pl.BlockSpec(memory_space=pltpu.VMEM)] * 2,
+        compiler_params=pltpu.CompilerParams(vmem_limit_bytes=32 * 1024 * 1024),
+        cost_estimate=pl.CostEstimate(flops=2 ** 31, bytes_accessed=2 ** 23, transcendentals=0),
+        name='attend_out')(where, x, wo, *parts)
+
+
+def input_grad_kernel(where_ref, base_ref, w_ref, *refs):
+    parts, out_ref = refs[:8], refs[8]
+    acc = base_ref[...].astype(F32)
+    for j in range(4):
+        for p in range(2):
+            row = pl.multiple_of((where_ref[1 + j] * 2 + p) * 384, 128)
+            acc = acc + nn(parts[2 * j + p][...], w_ref[pl.ds(row, 384), :])
+    out_ref[...] = acc.astype(BF16)
+
+
+def input_grad(where, base, w_qkv, parts):
+    rows, cols = base.shape
+    tile = 256
+    return pl.pallas_call(
+        input_grad_kernel,
+        out_shape=jax.ShapeDtypeStruct(base.shape, BF16),
+        grid_spec=pltpu.PrefetchScalarGridSpec(
+            num_scalar_prefetch=1, grid=(rows // tile,),
+            in_specs=[pl.BlockSpec((tile, cols), lambda i, s: (i, 0)), pl.BlockSpec(w_qkv.shape, lambda i, s: (0, 0))]
+                     + [pl.BlockSpec((tile, 384), lambda i, s: (i, 0))] * 8,
+            out_specs=pl.BlockSpec((tile, cols), lambda i, s: (i, 0))),
+        compiler_params=pltpu.CompilerParams(vmem_limit_bytes=40 * 1024 * 1024),
+        cost_estimate=pl.CostEstimate(flops=6 * 2 ** 30, bytes_accessed=2 ** 24, transcendentals=0),
+        name='input_grad')(where, base, w_qkv, *parts)
 
 
 MESH = pl.DeviceIdType.MESH
@@ -465,75 +522,78 @@
     def flip(arr, bit):
         return lax.ppermute(arr, 'cp', [(i, i ^ bit) for i in range(cp_size)]) if bit else arr
 
-    def per_device(x_in, d_out, w_q, w_k, w_v, w_o, w_up, w_down):
+    def layer(x_in, d_out, w_q, w_k, w_v, w_o, w_up, w_down):
         rank = lax.axis_index('cp')
         x_own, g_out = x_in[0], d_out[0]
         tokens, d_model = x_own.shape
         width = d_model // cp_size
         n_pairs = width // 128
+        slots = range(cp_size)
+        halves = range(2)
         w_t = [jnp.transpose(w, (1, 2, 0)).reshape(d_model // 128, 1, 128, d_model) for w in (w_q, w_k, w_v)]
         w_qkv = jnp.concatenate(w_t, axis=1).reshape(3 * d_model, d_model)
         wo2 = w_o.reshape(d_model, d_model)
         w_mine = lax.dynamic_slice(w_qkv, (rank * 3 * width, 0), (3 * width, d_model))
-        slots = range(cp_size)
-
-        x_all = [x_own, flip(x_own, 1), flip(x_own, 2)]
+
+        x_part = [x_own[:BLK], x_own[BLK:]]
+        far = [flip(x_part[i], 2) for i in halves]
+        near = [flip(x_part[i], 1) for i in halves]
         grad_act = nt(g_out, w_down).astype(BF16)
-        x_far, grad_act = lax.optimization_barrier((x_all[2], grad_act))
-        x_all = [x_all[0], x_all[1], x_far, flip(x_far, 1)]
+        far[0], grad_act = lax.optimization_barrier((far[0], grad_act))
+        x_all = [[x_part[i], near[i], far[i], flip(far[i], 1)] for i in halves]
         seq_blk = jnp.arange(2 * cp_size)
-        holder = jnp.where(seq_blk < cp_size, seq_blk, 2 * cp_size - 1 - seq_blk)
-        tab = (2 * jnp.bitwise_xor(holder, rank) + (seq_blk >= cp_size)).astype(jnp.int32)
-        qkv = [nt(x_j, w_mine).astype(BF16) for x_j in x_all]
-
-        def absolute(parts, w):
-            rel = jnp.concatenate(parts, axis=1)
-            return jnp.concatenate([lax.dynamic_slice(rel, (0, (b ^ rank) * w), (tokens, w)) for b in slots], axis=1)
-
-        attn_o, lses, o_parts = [], [], {}
-        for pair in range(n_pairs):
-            o_pair, lse = attn_fwd(tab, qkv, pair)
-            attn_o.append(o_pair)
-            lses.append(lse)
-            for j in slots:
-                o_parts[j, pair] = flip(o_pair[j * tokens:(j + 1) * tokens], j)
-        o_own = absolute([o_parts[j, p] for j in slots for p in range(n_pairs)], width)
-
-        hidden = (x_own.astype(F32) + nn(o_own, wo2)).astype(BF16)
+        tab = jnp.where(seq_blk < cp_size, jnp.bitwise_xor(seq_blk, rank),
+                        cp_size + jnp.bitwise_xor(2 * cp_size - 1 - seq_blk, rank)).astype(jnp.int32)
+        qkv = [[nt(x_j, w_mine).astype(BF16) for x_j in x_all[i]] for i in halves]
+
+        where = jnp.stack([rank] + [rank ^ j for j in slots]).astype(jnp.int32)
+        attn_o, lses, o_parts = {}, {}, {}
+        for i in halves:
+            for pair in range(n_pairs):
+                *o_slots, lses[pair, i] = attn_fwd(tab, qkv[0] + (qkv[1] if i else []), pair, 4 * i)
+                attn_o[pair, i] = o_slots
+                for j in slots:
+                    o_parts[i, j, pair] = flip(o_slots[j], j)
+        hidden, o_own = attend_out(where, x_own, wo2,
+                                   [o_parts[i, j, p] for i in halves for j in slots for p in range(n_pairs)])
         up_pre = nn(hidden, w_up).astype(BF16)
         act_val, gelu_pull = jax.vjp(functools.partial(jax.nn.gelu, approximate=True), up_pre.astype(F32))
         act_b = act_val.astype(BF16)
         grad_pre = gelu_pull(grad_act.astype(F32))[0].astype(BF16)
         grad_down = tn(act_b, g_out) * inv
+        grad_down = lax.psum(grad_down, ('dp', 'cp'))
         grad_hidden = (g_out.astype(F32) + nt(grad_pre, w_up)).astype(BF16)
         grad_attn = nt(grad_hidden, wo2).astype(BF16)
-        grad_up = tn(hidden, grad_pre) * inv
-        grad_o = tn(o_own, grad_hidden) * inv
 
         d_o = []
         for pair in range(n_pairs):
+            if pair:
+                grad_attn, d_o[0] = lax.optimization_barrier((grad_attn, d_o[0]))
             pieces = [lax.dynamic_slice(grad_attn, (0, (rank ^ j) * width + 128 * pair), (tokens, 128)) for j in slots]
             d_o.append([flip(pieces[j], j) for j in slots])
-        d_o[0], grad_down, grad_up, grad_o = lax.optimization_barrier((d_o[0], grad_down, grad_up, grad_o))
-        grad_down, grad_o = lax.psum((grad_down, grad_o), ('dp', 'cp'))
+            if not pair:
+                grad_uo = jnp.concatenate([tn(hidden, grad_pre) * inv, tn(o_own, grad_hidden) * inv], axis=1)
+                d_o[0], grad_uo = lax.optimization_barrier((d_o[0], grad_uo))
 
         grads, back = [], {}
+        x_full = [jnp.concatenate([x_all[0][j], x_all[1][j]], axis=0) if j else x_own for j in slots]
         for pair in range(n_pairs):
-            parts = attn_bwd(tab, qkv, d_o[pair], attn_o[pair], lses[pair], pair)
+            parts = attn_bwd(tab, qkv[0] + qkv[1], d_o[pair], attn_o[pair, 0] + attn_o[pair, 1],
+                             [lses[pair, i] for i in halves], pair)
             for j in slots:
                 back[j, pair] = flip(parts[j], j)
-            grads.append(sum(tn(parts[j], x_all[j]) for j in slots) * inv)
+            grads.append(sum(tn(parts[j], x_full[j]) for j in slots) * inv)
         mine = jnp.concatenate(grads, axis=0).reshape(n_pairs, 3, 128, d_model)
         mine = jnp.transpose(mine, (1, 0, 2, 3)).reshape(3 * width, d_model)
-        grad_up, g_qkv = sum_grads(grad_up, mine)
+        g_uo, g_qkv = sum_grads(grad_uo, mine)
+        d_ff = w_up.shape[1]
         outs = [jnp.transpose(g_qkv[t * d_model:(t + 1) * d_model].reshape(w.shape[1], w.shape[2], d_model), (2, 0, 1))
                 for t, w in enumerate((w_q, w_k, w_v))]
-        back_abs = absolute([back[j, p] for j in slots for p in range(n_pairs)], 3 * width)
-        d_x = (grad_hidden.astype(F32) + nn(back_abs, w_qkv)).astype(BF16)
-        return (d_x[None], *outs, grad_o.reshape(w_o.shape), grad_up, grad_down)
+        d_x = input_grad(where, grad_hidden, w_qkv, [back[j, p] for j in slots for p in range(n_pairs)])
+        return (d_x[None], *outs, g_uo[:, d_ff:].reshape(w_o.shape), g_uo[:, :d_ff], grad_down)
 
     act_spec = P('dp', 'cp', None)
-    return jax.shard_map(per_device, mesh=mesh,
+    return jax.shard_map(layer, mesh=mesh,
                          in_specs=(act_spec, act_spec, P(), P(), P(), P(), P(), P()),
                          out_specs=(act_spec, P(), P(), P(), P(), P(), P()),
                          check_vma=False)

time: 965 us -> 900 us (0.933)
  waiting for transfers between devices: 204 us -> 71.6 us
  Pallas kernels: 520 us -> 578 us
  other arithmetic: 18.1 us -> 35.1 us
  local copies, waits for them, and re-layouts: 65.5 us -> 55.2 us
    psum x1, waiting for transfers between devices: 136 us -> 0.01 us  [layer(): grad_down = lax.psum(grad_down, ('dp', 'cp'))]
    pallas_call x1, Pallas kernels: 308 us -> 343 us  [sum_grads(): pl.pallas_call(sum_kernel, out_shape=[jax.ShapeDtypeStruct(up.shape, F32)...]
    unnamed x75 -> x118, local copies, waits for them, and re-layouts: 47.4 us -> 19 us
    pallas_call x2 -> x6, Pallas kernels: 92.2 us -> 113 us  [the longest x4 94 us: attn_fwd(): pl.pallas_call(functools.partial(attn_fwd_kernel, pair, n_in, first), out...]
    slice x3 -> x4, local copies, waits for them, and re-layouts: 12.2 us -> 29.8 us  [the longest x1 11.7 us: layer(): g_uo[:, :d_ff]]
    concatenate x2 -> x3, other arithmetic: 4.08 us -> 19.7 us  [the longest x1 16.2 us: layer(): jnp.concatenate([tn(hidden, grad_pre) * inv, tn(o_own, grad_hidden) * inv...]
    dot_general x3 -> x1, matrix products: 21.7 us -> 15 us  [nn(): lax.dot_general(a, b, (((1,), (0,)), ((), ())), preferred_element_type=F32)]
    dot_general x7 -> x11, matrix products: 44 us -> 49.6 us  [nt(): lax.dot_general(a, b, (((1,), (1,)), ((), ())), preferred_element_type=F32)]
  transfers between devices with their start and end apart: 22 -> 31, of which waited for: 9 -> 10; matrix products, arithmetic and copies ran while one was open for 9% -> 12% of each run, Pallas kernels for 45% -> 55%
where the time goes in v2:
time: 900 us; the launch traced here: 890 us
  Pallas kernels  578 us (64%)
  matrix products  114 us (13%)
  waiting for transfers between devices  71.6 us (8%)
  local copies, waits for them, and re-layouts  55.2 us (6%)
  other arithmetic  35.1 us (4%)
  starting transfers between devices  21 us (2%)
  between operations  15.4 us (2%)
    pallas_call x1, Pallas kernels, sum_grads(): pl.pallas_call(sum_kernel, out_shape=[jax.ShapeDtypeStruct(up.shape, F32)...  343 us
    pallas_call x2, Pallas kernels, attn_bwd(): pl.pallas_call(functools.partial(attn_bwd_kernel, pair), out_shape=[jax.S...  123 us
    pallas_call x4, Pallas kernels, attn_fwd(): pl.pallas_call(functools.partial(attn_fwd_kernel, pair, n_in, first), out...  94 us
    ppermute x30, waiting for transfers between devices, flip(): lax.ppermute(arr, 'cp', [(i, i ^ bit) for i in range(cp_size)])  71.5 us
    dot_general x11, matrix products, nt(): lax.dot_general(a, b, (((1,), (1,)), ((), ())), preferred_element_type=F32)  49.6 us
    dot_general x11, matrix products, tn(): lax.dot_general(a, b, (((0,), (0,)), ((), ())), preferred_element_type=F32)  49 us
    ppermute x30, starting transfers between devices, flip(): lax.ppermute(arr, 'cp', [(i, i ^ bit) for i in range(cp_size)])  20.9 us
    unnamed x118, local copies, waits for them, and re-layouts  19 us
  transfers between devices with their start and end apart: 31, of which 10 were waited for; matrix products, arithmetic and copies ran while one was open for 12% of the time, Pallas kernels for 55%

profile of v2, /device:TPU:0, one launch (start us, length us, event | category | flops | bytes accessed | tf_op | source)
XLA Modules:
  0.0 890.2 jit_solution(6709249645309368293)
XLA Ops:
  7.2 3.0 slice_bitcast_fusion
  10.7 2.5 collective-permute-start.10
  13.7 15.0 %convolution_convert_fusion.1 = bf16[1024,4096]{1,0:T(8,128)(2,1)} fusion(bf16[4096,1024]{1,0:T(8,128)(2,1)} %param.15, bf16[1,1024,1024]{2,1,0:T(8,128)(2,1)} %param.9), kind=kOutput, calls=%fused_computation.25 | convolution fusion | flops 8594128896 | bytes 18874368 | tf_op jit(solution)/shard_map/dot_general | solution.py:18
  28.8 3.1 pad_maximum_fusion.1
  31.9 1.0 fusion.18.refs_0_
  32.9 1.0 fusion.20.refs_4_
  34.0 25.9 %collective-permute-done = bf16[512,1024]{1,0:T(8,128)(2,1)} collective-permute-done((bf16[512,1024]{1,0:T(8,128)(2,1)}, bf16[512,1024]{1,0:T(8,128)(2,1)}, u32[]{:S(2)}, u32[]{:S(2)}) %collective-permute-start) | collective-permute-done | bytes 1048608 | tf_op jit(solution)/shard_map/ppermute | solution.py:523
  60.3 1.3 constant_dynamic-update-slice_fusion.3
  61.6 2.3 constant_dynamic-update-slice_fusion.1
  63.9 1.3 constant_dynamic-update-slice_fusion.2
  65.2 1.3 copy-done.39
  66.5 2.3 constant_dynamic-update-slice_fusion
  68.8 2.2 convolution_convert_fusion.8.refs_2_
  71.1 2.5 fusion.19.refs_1_
  73.6 3.0 fusion.21.refs_5_
  77.5 2.5 fusion.22.refs_6_
  80.1 1.9 fusion.23.refs_7_
  83.0 1.0 convolution_convert_fusion.7.refs_3_
  84.0 34.1 %attn_fwd.7 = (bf16[512,128]{1,0:T(8,128)(2,1)S(1)}, bf16[512,128]{1,0:T(8,128)(2,1)S(1)}, bf16[512,128]{1,0:T(8,128)(2,1)S(1)}, bf16[512,128]{1,0:T(8,128)(2,1)S(1)}, f32[1,2,2048]{2,1,0:T(2,128)S(1)}) custom-call(s32[8]{0:T(128)S(1)} %compare_select_fusion.tab_ref, bf16[512,768]{1,0:T(8,128)(2,1)S(1)} %fusion.18.refs_0_, ...), custom_call_target="tpu_custom_call" | custom-call | flops 20937965568 | bytes 4194304 | tf_op jit(solution)/shard_map/attn_fwd/pallas_call | solution.py:172
  118.2 33.9 %attn_fwd.6 = (bf16[512,128]{1,0:T(8,128)(2,1)S(1)}, bf16[512,128]{1,0:T(8,128)(2,1)S(1)}, bf16[512,128]{1,0:T(8,128)(2,1)S(1)}, bf16[512,128]{1,0:T(8,128)(2,1)S(1)}, f32[1,2,2048]{2,1,0:T(2,128)S(1)}) custom-call(s32[8]{0:T(128)S(1)} %compare_select_fusion.tab_ref, bf16[512,768]{1,0:T(8,128)(2,1)S(1)} %fusion.18.refs_0_, ...), custom_call_target="tpu_custom_call" | custom-call | flops 20937965568 | bytes 4194304 | tf_op jit(solution)/shard_map/attn_fwd/pallas_call | solution.py:172
  152.1 13.0 %attn_fwd.5 = (bf16[512,128]{1,0:T(8,128)(2,1)S(1)}, bf16[512,128]{1,0:T(8,128)(2,1)S(1)}, bf16[512,128]{1,0:T(8,128)(2,1)S(1)}, bf16[512,128]{1,0:T(8,128)(2,1)S(1)}, f32[1,2,2048]{2,1,0:T(2,128)S(1)}) custom-call(s32[8]{0:T(128)S(1)} %compare_select_fusion.tab_ref, bf16[512,768]{1,0:T(8,128)(2,1)S(1)} %fusion.18.refs_0_, ...), custom_call_target="tpu_custom_call" | custom-call | flops 8053063680 | bytes 4194304 | tf_op jit(solution)/shard_map/attn_fwd/pallas_call | solution.py:172
  165.3 1.8 collective-permute-start.15
  167.1 13.0 %attn_fwd.4 = (bf16[512,128]{1,0:T(8,128)(2,1)S(1)}, bf16[512,128]{1,0:T(8,128)(2,1)S(1)}, bf16[512,128]{1,0:T(8,128)(2,1)S(1)}, bf16[512,128]{1,0:T(8,128)(2,1)S(1)}, f32[1,2,2048]{2,1,0:T(2,128)S(1)}) custom-call(s32[8]{0:T(128)S(1)} %compare_select_fusion.tab_ref, bf16[512,768]{1,0:T(8,128)(2,1)S(1)} %fusion.18.refs_0_, ...), custom_call_target="tpu_custom_call" | custom-call | flops 8053063680 | bytes 4194304 | tf_op jit(solution)/shard_map/attn_fwd/pallas_call | solution.py:172
  180.6 1.7 collective-permute-start.14
  182.9 2.8 collective-permute-done.17.refs_15_
  185.9 1.6 collective-permute-start.8
  187.5 1.6 collective-permute-done.14.refs_12_
  189.2 2.1 collective-permute-done.16.refs_14_
  191.6 1.6 collective-permute-start.7
  193.2 1.5 collective-permute-done.6.refs_5_
  194.8 2.1 collective-permute-done.8.refs_7_
  196.9 3.5 collective-permute-done.5.refs_4_
  200.4 2.1 collective-permute-done.7.refs_6_
  202.6 4.5 attend_out.1
  207.1 15.0 %convolution_convert_fusion = bf16[1024,4096]{1,0:T(8,128)(2,1)} fusion(bf16[1024,1024]{1,0:T(8,128)(2,1)S(1)} %get-tuple-element.69, bf16[1024,4096]{1,0:T(8,128)(2,1)} %param.14), kind=kOutput, calls=%fused_computation.24 | convolution fusion | flops 8594128896 | bytes 18874368 | tf_op jit(solution)/shard_map/dot_general | solution.py:22
  222.1 15.4 %fusion.3 = bf16[1024,4096]{1,0:T(8,128)(2,1)} fusion(bf16[1024,4096]{1,0:T(8,128)(2,1)S(1)} %bitcast.101, bf16[1024,4096]{1,0:T(8,128)(2,1)} %convolution_convert_fusion), kind=kLoop, calls=%fused_computation.10 | loop fusion | flops 92274688 | bytes 25165824 | tf_op jit(solution)/shard_map/convert_element_type | solution.py:562
  237.6 15.1 %add_convert_fusion.base_ref = bf16[1024,1024]{1,0:T(8,128)(2,1)} fusion(bf16[1,1024,1024]{2,1,0:T(8,128)(2,1)} %param.9, bf16[1024,4096]{1,0:T(8,128)(2,1)} %fusion.3, bf16[1024,4096]{1,0:T(8,128)(2,1)} %param.14), kind=kOutput, calls=%fused_computation.27 | convolution fusion | flops 8593080320 | bytes 20971520 | tf_op jit(solution)/shard_map/dot_general | solution.py:18
  252.7 11.9 %convolution_multiply_fusion.1 = f32[1024,4096]{1,0:T(8,128)} fusion(bf16[1024,1024]{1,0:T(8,128)(2,1)S(1)} %get-tuple-element.69, bf16[1024,4096]{1,0:T(8,128)(2,1)S(1)} %copy-done.43), kind=kOutput, calls=%fused_computation.19 | convolution fusion | flops 8594128896 | bytes 27262976 | tf_op jit(solution)/shard_map/dot_general | solution.py:514
  264.7 15.8 %convolution_multiply_fusion = f32[4096,1024]{1,0:T(8,128)} fusion(bf16[1024,4096]{1,0:T(8,128)(2,1)S(1)} %bitcast.103, bf16[1,1024,1024]{2,1,0:T(8,128)(2,1)} %param.9), kind=kOutput, calls=%fused_computation.18 | convolution fusion | flops 8636071936 | bytes 27262976 | tf_op jit(solution)/shard_map/dot_general | solution.py:514
  280.5 4.1 convolution_convert_fusion.2
  285.1 1.7 collective-permute-start.19
  287.0 4.5 convolution_multiply_fusion.2
  291.5 16.2 %pad_maximum_fusion.up_ref = f32[1024,5120]{1,0:T(8,128)} fusion(f32[1024,1024]{1,0:T(8,128)} %convolution_multiply_fusion.2, f32[1024,4096]{1,0:T(8,128)} %convolution_multiply_fusion.1), kind=kLoop, calls=%fused_computation.7 | loop fusion | flops 5242880 | bytes 41943040 | tf_op jit(solution)/shard_map/concatenate | solution.py:575
  307.8 61.1 %attn_bwd.2 = (bf16[1024,384]{1,0:T(8,128)(2,1)S(1)}, bf16[1024,384]{1,0:T(8,128)(2,1)S(1)}, bf16[1024,384]{1,0:T(8,128)(2,1)}, bf16[1024,384]{1,0:T(8,128)(2,1)}) custom-call(s32[8]{0:T(128)S(1)} %compare_select_fusion.tab_ref, bf16[512,768]{1,0:T(8,128)(2,1)S(1)} %copy-done.26, bf16[512,768]{1,0:T(8,128)(2,1)} %copy-done.36, bf16[512,768]{1,0:T(8,128)(2,1)} %copy-done.30, ...), custom_call_target="tpu_custom_call" | custom-call | flops 72477573120 | bytes 4194304 | tf_op jit(solution)/shard_map/attn_bwd/pallas_call | solution.py:190
  370.0 1.3 collective-permute-start.23
  371.9 1.0 fusion.42
  372.9 2.8 fusion.49
  375.7 2.3 fusion.50
  378.1 2.3 add_multiply_fusion.1
  380.4 21.4 %collective-permute-done.23.refs_11_ = bf16[1024,128]{1,0:T(8,128)(2,1)S(1)} collective-permute-done((bf16[1024,128]{1,0:T(8,128)(2,1)S(1)}, bf16[1024,128]{1,0:T(8,128)(2,1)S(1)}, u32[]{:S(2)}, u32[]{:S(2)}) %collective-permute-start.23) | collective-permute-done | bytes 262176 | tf_op jit(solution)/shard_map/ppermute | solution.py:523
  401.8 2.3 collective-permute-start.28
  404.1 8.4 collective-permute-done.22.refs_10_
  412.6 61.4 %attn_bwd.3 = (bf16[1024,384]{1,0:T(8,128)(2,1)S(1)}, bf16[1024,384]{1,0:T(8,128)(2,1)}, bf16[1024,384]{1,0:T(8,128)(2,1)}, bf16[1024,384]{1,0:T(8,128)(2,1)}) custom-call(s32[8]{0:T(128)S(1)} %compare_select_fusion.tab_ref, bf16[512,768]{1,0:T(8,128)(2,1)S(1)} %copy-done.26, bf16[512,768]{1,0:T(8,128)(2,1)} %copy-done.36, bf16[512,768]{1,0:T(8,128)(2,1)} %copy-done.30, ...), custom_call_target="tpu_custom_call" | custom-call | flops 72477573120 | bytes 4194304 | tf_op jit(solution)/shard_map/attn_bwd/pallas_call | solution.py:190
  474.1 3.0 fusion.51
  477.5 2.2 fusion.52
  480.6 2.2 add_multiply_fusion
  483.3 2.1 copy.25
  485.4 1.4 collective-permute-start.29
  486.8 343.1 %sum_grads.1 = (f32[1024,5120]{1,0:T(8,128)}, f32[3072,1024]{1,0:T(8,128)}) custom-call(f32[1024,5120]{1,0:T(8,128)} %pad_maximum_fusion.up_ref, f32[768,1024]{1,0:T(8,128)} %bitcast.117), custom_call_target="tpu_custom_call" | custom-call | flops 199999995904 | bytes 67108864 | tf_op jit(solution)/shard_map/sum_grads/pallas_call | solution.py:498
  829.9 4.8 slice.34
  834.7 11.7 %slice.35 = f32[1024,4096]{1,0:T(8,128)} slice(f32[1024,5120]{1,0:T(8,128)} %get-tuple-element.94), slice={[0:1024], [0:4096]} | slice | bytes 33554432 | tf_op jit(solution)/shard_map/slice | solution.py:593
  846.4 10.3 %fusion.48 = (f32[1024,1024]{1,0:T(8,128)}, f32[1024,1024]{1,0:T(8,128)}, f32[1024,1024]{1,0:T(8,128)}) fusion(f32[3072,1024]{1,0:T(8,128)} %get-tuple-element.93), kind=kLoop, calls=%fused_computation.90 | loop fusion | bytes 25165824 | tf_op jit(solution)/shard_map/slice | solution.py:590
  856.8 14.2 %input_grad.1 = bf16[1024,1024]{1,0:T(8,128)(2,1)} custom-call(s32[5]{0:T(128)S(1)} %copy-done.7, bf16[1024,1024]{1,0:T(8,128)(2,1)S(1)} %copy-done.29, bf16[3072,1024]{1,0:T(8,128)(2,1)} %bitcast.109, bf16[1024,384]{1,0:T(8,128)(2,1)S(1)} %copy-done.3, bf16[1024,384]{1,0:T(8,128)(2,1)S(1)} %copy-done.5, bf16[1024,384]{1,0:T(8,128)(2,1)S(1)} %copy-done.10, ...), custom_call_target="tpu_custom_call" | custom-call | flops 6442450944 | bytes 16777216 | tf_op jit(solution)/shard_map/input_grad/pallas_call | solution.py:244
  871.0 12.0 %copy.37 = f32[4096,1024]{1,0:T(8,128)} copy(f32[4096,1024]{1,0:T(8,128)} %all-reduce.2.cloned.1.call-done) | data formatting | bytes 33554432
  (167 shorter events, 9.5 us)
Async XLA Ops:
  7.2 863.8 %all-reduce.2.cloned.1.call-start = ((), (), s32[]{:S(2)}) async-start(), calls=%async_computation | async-start | bytes 33554432 | tf_op jit(solution)/shard_map/psum | solution.py:564
  10.2 55.0 %collective-permute-start.9 = (bf16[512,1024]{1,0:T(8,128)(2,1)}, bf16[512,1024]{1,0:T(8,128)(2,1)}, u32[]{:S(2)}, u32[]{:S(2)}) collective-permute-start(bf16[512,1024]{1,0:T(8,128)(2,1)} %get-tuple-element.106), channel_id=1, source_target_pairs={{0,1},{1,0},{2,3},{3,2},{4,5},{5,4},{6,7},{7,6},{8,9},{9,8},{10,11... | collective-permute-start | bytes 3145736 | tf_op jit(solution)/shard_map/ppermute | solution.py:523
  10.7 49.1 %collective-permute-start.10 = (bf16[512,1024]{1,0:T(8,128)(2,1)}, bf16[512,1024]{1,0:T(8,128)(2,1)}, u32[]{:S(2)}, u32[]{:S(2)}) collective-permute-start(bf16[512,1024]{1,0:T(8,128)(2,1)} %get-tuple-element.106), channel_id=1, source_target_pairs={{0,2},{1,3},{2,0},{3,1},{4,6},{5,7},{6,4},{7,5},{8,10},{9,11},{10,... | collective-permute-start | bytes 3145736 | tf_op jit(solution)/shard_map/ppermute | solution.py:523
  13.2 48.4 %collective-permute-start.1 = (bf16[512,1024]{1,0:T(8,128)(2,1)}, bf16[512,1024]{1,0:T(8,128)(2,1)}, u32[]{:S(2)}, u32[]{:S(2)}) collective-permute-start(bf16[512,1024]{1,0:T(8,128)(2,1)} %get-tuple-element.107), channel_id=1, source_target_pairs={{0,1},{1,0},{2,3},{3,2},{4,5},{5,4},{6,7},{7,6},{8,9},{9,8},{10,11... | collective-permute-start | bytes 3145736 | tf_op jit(solution)/shard_map/ppermute | solution.py:523
  13.4 46.4 %collective-permute-start = (bf16[512,1024]{1,0:T(8,128)(2,1)}, bf16[512,1024]{1,0:T(8,128)(2,1)}, u32[]{:S(2)}, u32[]{:S(2)}) collective-permute-start(bf16[512,1024]{1,0:T(8,128)(2,1)} %get-tuple-element.107), channel_id=1, source_target_pairs={{0,2},{1,3},{2,0},{3,1},{4,6},{5,7},{6,4},{7,5},{8,10},{9,11},{10,... | collective-permute-start | bytes 3145736 | tf_op jit(solution)/shard_map/ppermute | solution.py:523
  28.8 173.8 %copy-start.6 = (s32[5]{0:T(128)}, s32[5]{0:T(128)S(1)}, u32[]{:S(2)}) copy-start(s32[5]{0:T(128)S(1)} %stack.20.rank_ref.where_ref) | copy-start | bytes 64
  31.8 39.2 %copy-start.44 = (bf16[8,3,128,1024]{3,2,1,0:T(8,128)(2,1)}, bf16[8,3,128,1024]{3,2,1,0:T(8,128)(2,1)S(1)}, u32[]{:S(2)}) copy-start(bf16[8,3,128,1024]{3,2,1,0:T(8,128)(2,1)S(1)} %pad_maximum_fusion.1) | copy-start | bytes 18874372
  32.9 134.2 %copy-start.25 = (bf16[512,768]{1,0:T(8,128)(2,1)}, bf16[512,768]{1,0:T(8,128)(2,1)S(1)}, u32[]{:S(2)}) copy-start(bf16[512,768]{1,0:T(8,128)(2,1)S(1)} %fusion.18.refs_0_) | copy-start | bytes 2359300
  33.9 84.2 %copy-start.27 = (bf16[512,768]{1,0:T(8,128)(2,1)}, bf16[512,768]{1,0:T(8,128)(2,1)S(1)}, u32[]{:S(2)}) copy-start(bf16[512,768]{1,0:T(8,128)(2,1)S(1)} %fusion.20.refs_4_) | copy-start | bytes 2359300
  59.8 22.2 %collective-permute-start.2 = (bf16[512,1024]{1,0:T(8,128)(2,1)}, bf16[512,1024]{1,0:T(8,128)(2,1)S(1)}, u32[]{:S(2)}, u32[]{:S(2)}) collective-permute-start(bf16[512,1024]{1,0:T(8,128)(2,1)} %collective-permute-done), channel_id=1, source_target_pairs={{0,1},{1,0},{2,3},{3,2},{4,5},{5,4},{6,7},{7,6},{8,9},{9,8},{10,11... | collective-permute-start | bytes 3145736 | tf_op jit(solution)/shard_map/ppermute | solution.py:523
  59.8 20.2 %collective-permute-start.11 = (bf16[512,1024]{1,0:T(8,128)(2,1)}, bf16[512,1024]{1,0:T(8,128)(2,1)S(1)}, u32[]{:S(2)}, u32[]{:S(2)}) collective-permute-start(bf16[512,1024]{1,0:T(8,128)(2,1)} %collective-permute-done.10), channel_id=1, source_target_pairs={{0,1},{1,0},{2,3},{3,2},{4,5},{5,4},{6,7},{7,6},{8,9},{9,8},{10,11... | collective-permute-start | bytes 3145736 | tf_op jit(solution)/shard_map/ppermute | solution.py:523
  71.1 96.0 %copy-start.30 = (bf16[512,768]{1,0:T(8,128)(2,1)}, bf16[512,768]{1,0:T(8,128)(2,1)S(1)}, u32[]{:S(2)}) copy-start(bf16[512,768]{1,0:T(8,128)(2,1)S(1)} %convolution_convert_fusion.8.refs_2_) | copy-start | bytes 2359300
  73.6 93.5 %copy-start.36 = (bf16[512,768]{1,0:T(8,128)(2,1)}, bf16[512,768]{1,0:T(8,128)(2,1)S(1)}, u32[]{:S(2)}) copy-start(bf16[512,768]{1,0:T(8,128)(2,1)S(1)} %fusion.19.refs_1_) | copy-start | bytes 2359300
  77.5 40.7 %copy-start.37 = (bf16[512,768]{1,0:T(8,128)(2,1)}, bf16[512,768]{1,0:T(8,128)(2,1)S(1)}, u32[]{:S(2)}) copy-start(bf16[512,768]{1,0:T(8,128)(2,1)S(1)} %fusion.21.refs_5_) | copy-start | bytes 2359300
  80.0 38.1 %copy-start.38 = (bf16[512,768]{1,0:T(8,128)(2,1)}, bf16[512,768]{1,0:T(8,128)(2,1)S(1)}, u32[]{:S(2)}) copy-start(bf16[512,768]{1,0:T(8,128)(2,1)S(1)} %fusion.22.refs_6_) | copy-start | bytes 2359300
  84.0 83.1 %copy-start.31 = (bf16[512,768]{1,0:T(8,128)(2,1)}, bf16[512,768]{1,0:T(8,128)(2,1)S(1)}, u32[]{:S(2)}) copy-start(bf16[512,768]{1,0:T(8,128)(2,1)S(1)} %convolution_convert_fusion.7.refs_3_) | copy-start | bytes 2359300
  118.1 47.0 %copy-start.11 = (bf16[512,128]{1,0:T(8,128)(2,1)}, bf16[512,128]{1,0:T(8,128)(2,1)S(1)}, u32[]{:S(2)}) copy-start(bf16[512,128]{1,0:T(8,128)(2,1)S(1)} %get-tuple-element.64.refs_17_) | copy-start | bytes 393220
  118.2 47.1 %copy-start.13 = (bf16[512,128]{1,0:T(8,128)(2,1)}, bf16[512,128]{1,0:T(8,128)(2,1)S(1)}, u32[]{:S(2)}) copy-start(bf16[512,128]{1,0:T(8,128)(2,1)S(1)} %get-tuple-element.66.refs_18_) | copy-start | bytes 393220
  118.2 62.0 %copy-start.15 = (bf16[512,128]{1,0:T(8,128)(2,1)}, bf16[512,128]{1,0:T(8,128)(2,1)S(1)}, u32[]{:S(2)}) copy-start(bf16[512,128]{1,0:T(8,128)(2,1)S(1)} %get-tuple-element.68.refs_19_) | copy-start | bytes 393220
  118.2 84.3 %copy-start.32 = (bf16[512,128]{1,0:T(8,128)(2,1)}, bf16[512,128]{1,0:T(8,128)(2,1)S(1)}, u32[]{:S(2)}) copy-start(bf16[512,128]{1,0:T(8,128)(2,1)S(1)} %get-tuple-element.62.refs_9_.refs_16_) | copy-start | bytes 393220
  165.1 17.3 %copy-start.17 = (bf16[512,128]{1,0:T(8,128)(2,1)}, bf16[512,128]{1,0:T(8,128)(2,1)S(1)}, u32[]{:S(2)}) copy-start(bf16[512,128]{1,0:T(8,128)(2,1)S(1)} %get-tuple-element.56.refs_13_) | copy-start | bytes 393220
  165.1 20.6 %copy-start.19 = (bf16[512,128]{1,0:T(8,128)(2,1)}, bf16[512,128]{1,0:T(8,128)(2,1)S(1)}, u32[]{:S(2)}) copy-start(bf16[512,128]{1,0:T(8,128)(2,1)S(1)} %get-tuple-element.58.refs_14_) | copy-start | bytes 393220
  165.1 20.8 %copy-start.21 = (bf16[512,128]{1,0:T(8,128)(2,1)}, bf16[512,128]{1,0:T(8,128)(2,1)S(1)}, u32[]{:S(2)}) copy-start(bf16[512,128]{1,0:T(8,128)(2,1)S(1)} %get-tuple-element.60.refs_15_) | copy-start | bytes 393220
  165.1 37.4 %copy-start.34 = (bf16[512,128]{1,0:T(8,128)(2,1)}, bf16[512,128]{1,0:T(8,128)(2,1)S(1)}, u32[]{:S(2)}) copy-start(bf16[512,128]{1,0:T(8,128)(2,1)S(1)} %get-tuple-element.54.refs_1_.refs_12_) | copy-start | bytes 393220
  165.2 17.2 %collective-permute-start.13 = (bf16[512,128]{1,0:T(8,128)(2,1)S(1)}, bf16[512,128]{1,0:T(8,128)(2,1)S(1)}, u32[]{:S(2)}, u32[]{:S(2)}) collective-permute-start(bf16[512,128]{1,0:T(8,128)(2,1)S(1)} %get-tuple-element.64.refs_17_), channel_id=1, source_target_pairs={{0,1},{1,0},{2,3},{3,2},{4,5},{5,4},{6,7},{7,6},{8,9},{9,8},{10,11... | collective-permute-start | bytes 393224 | tf_op jit(solution)/shard_map/ppermute | solution.py:523
  165.2 17.6 %copy-start.52 = (bf16[512,1024]{1,0:T(8,128)(2,1)S(1)}, bf16[512,1024]{1,0:T(8,128)(2,1)}, u32[]{:S(2)}) copy-start(bf16[512,1024]{1,0:T(8,128)(2,1)} %copy-done.51) | copy-start | bytes 3145732
  165.3 17.1 %collective-permute-start.15 = (bf16[512,128]{1,0:T(8,128)(2,1)S(1)}, bf16[512,128]{1,0:T(8,128)(2,1)S(1)}, u32[]{:S(2)}, u32[]{:S(2)}) collective-permute-start(bf16[512,128]{1,0:T(8,128)(2,1)S(1)} %get-tuple-element.66.refs_18_), channel_id=1, source_target_pairs={{0,2},{1,3},{2,0},{3,1},{4,6},{5,7},{6,4},{7,5},{8,10},{9,11},{10,... | collective-permute-start | bytes 393224 | tf_op jit(solution)/shard_map/ppermute | solution.py:523
  180.1 5.5 collective-permute-start.17
  180.3 5.7 collective-permute-start.12
  180.6 8.5 collective-permute-start.14
  182.4 8.9 %collective-permute-start.16 = (bf16[512,128]{1,0:T(8,128)(2,1)S(1)}, bf16[512,128]{1,0:T(8,128)(2,1)S(1)}, u32[]{:S(2)}, u32[]{:S(2)}) collective-permute-start(bf16[512,128]{1,0:T(8,128)(2,1)S(1)} %get-tuple-element.67.refs_19_), channel_id=1, source_target_pairs={{0,3},{1,2},{2,1},{3,0},{4,7},{5,6},{6,5},{7,4},{8,11},{9,10},{10,... | collective-permute-start | bytes 393224 | tf_op jit(solution)/shard_map/ppermute | solution.py:523
  182.4 20.2 %copy-start.8 = (bf16[16,64,1024]{2,1,0:T(8,128)(2,1)S(1)}, bf16[16,64,1024]{2,1,0:T(8,128)(2,1)}, u32[]{:S(2)}) copy-start(bf16[16,64,1024]{2,1,0:T(8,128)(2,1)} %param.13) | copy-start | bytes 6291460
  182.4 9.2 %collective-permute-start.4 = (bf16[512,128]{1,0:T(8,128)(2,1)S(1)}, bf16[512,128]{1,0:T(8,128)(2,1)S(1)}, u32[]{:S(2)}, u32[]{:S(2)}) collective-permute-start(bf16[512,128]{1,0:T(8,128)(2,1)S(1)} %get-tuple-element.56.refs_13_), channel_id=1, source_target_pairs={{0,1},{1,0},{2,3},{3,2},{4,5},{5,4},{6,7},{7,6},{8,9},{9,8},{10,11... | collective-permute-start | bytes 393224 | tf_op jit(solution)/shard_map/ppermute | solution.py:523
  185.7 9.1 %collective-permute-start.6 = (bf16[512,128]{1,0:T(8,128)(2,1)S(1)}, bf16[512,128]{1,0:T(8,128)(2,1)S(1)}, u32[]{:S(2)}, u32[]{:S(2)}) collective-permute-start(bf16[512,128]{1,0:T(8,128)(2,1)S(1)} %get-tuple-element.58.refs_14_), channel_id=1, source_target_pairs={{0,2},{1,3},{2,0},{3,1},{4,6},{5,7},{6,4},{7,5},{8,10},{9,11},{10,... | collective-permute-start | bytes 393224 | tf_op jit(solution)/shard_map/ppermute | solution.py:523
  185.9 11.0 %collective-permute-start.8 = (bf16[512,128]{1,0:T(8,128)(2,1)S(1)}, bf16[512,128]{1,0:T(8,128)(2,1)S(1)}, u32[]{:S(2)}, u32[]{:S(2)}) collective-permute-start(bf16[512,128]{1,0:T(8,128)(2,1)S(1)} %get-tuple-element.60.refs_15_), channel_id=1, source_target_pairs={{0,3},{1,2},{2,1},{3,0},{4,7},{5,6},{6,5},{7,4},{8,11},{9,10},{10,... | collective-permute-start | bytes 393224 | tf_op jit(solution)/shard_map/ppermute | solution.py:523
  189.2 7.8 collective-permute-start.3
  191.3 9.1 %collective-permute-start.5 = (bf16[512,128]{1,0:T(8,128)(2,1)S(1)}, bf16[512,128]{1,0:T(8,128)(2,1)S(1)}, u32[]{:S(2)}, u32[]{:S(2)}) collective-permute-start(bf16[512,128]{1,0:T(8,128)(2,1)S(1)} %get-tuple-element.57.refs_14_), channel_id=1, source_target_pairs={{0,2},{1,3},{2,0},{3,1},{4,6},{5,7},{6,4},{7,5},{8,10},{9,11},{10,... | collective-permute-start | bytes 393224 | tf_op jit(solution)/shard_map/ppermute | solution.py:523
  191.6 11.0 %collective-permute-start.7 = (bf16[512,128]{1,0:T(8,128)(2,1)S(1)}, bf16[512,128]{1,0:T(8,128)(2,1)S(1)}, u32[]{:S(2)}, u32[]{:S(2)}) collective-permute-start(bf16[512,128]{1,0:T(8,128)(2,1)S(1)} %get-tuple-element.59.refs_15_), channel_id=1, source_target_pairs={{0,3},{1,2},{2,1},{3,0},{4,7},{5,6},{6,5},{7,4},{8,11},{9,10},{10,... | collective-permute-start | bytes 393224 | tf_op jit(solution)/shard_map/ppermute | solution.py:523
  202.5 19.6 %slice-start = ((s8[8388608]{0:T(1024)(128)(4,1)}), s8[4194304]{0:T(1024)(128)(4,1)S(1)}, s32[]{:S(2)}) async-start(s8[8388608]{0:T(1024)(128)(4,1)} %bitcast.100), calls=%async_computation.1 | async-start | bytes 8388608
  222.1 42.5 %slice-start.2 = ((s8[8388608]{0:T(1024)(128)(4,1)}), s8[4194304]{0:T(1024)(128)(4,1)S(1)}, s32[]{:S(2)}) async-start(s8[8388608]{0:T(1024)(128)(4,1)} %bitcast.102), calls=%async_computation.3 | async-start | bytes 8388608
  237.6 27.1 %slice-start.3 = ((s8[8388608]{0:T(1024)(128)(4,1)}), s8[4194304]{0:T(1024)(128)(4,1)S(1)}, s32[]{:S(2)}) async-start(s8[8388608]{0:T(1024)(128)(4,1)} %bitcast.102), calls=%async_computation.4 | async-start | bytes 8388608
  285.0 22.8 %collective-permute-start.20 = (bf16[1024,128]{1,0:T(8,128)(2,1)S(1)}, bf16[1024,128]{1,0:T(8,128)(2,1)S(1)}, u32[]{:S(2)}, u32[]{:S(2)}) collective-permute-start(bf16[1024,128]{1,0:T(8,128)(2,1)S(1)} %get-tuple-element.102), channel_id=1, source_target_pairs={{0,3},{1,2},{2,1},{3,0},{4,7},{5,6},{6,5},{7,4},{8,11},{9,10},{10,... | collective-permute-start | bytes 786440 | tf_op jit(solution)/shard_map/ppermute | solution.py:523
  285.1 22.7 %collective-permute-start.19 = (bf16[1024,128]{1,0:T(8,128)(2,1)S(1)}, bf16[1024,128]{1,0:T(8,128)(2,1)S(1)}, u32[]{:S(2)}, u32[]{:S(2)}) collective-permute-start(bf16[1024,128]{1,0:T(8,128)(2,1)S(1)} %get-tuple-element.103), channel_id=1, source_target_pairs={{0,2},{1,3},{2,0},{3,1},{4,6},{5,7},{6,4},{7,5},{8,10},{9,11},{10,... | collective-permute-start | bytes 786440 | tf_op jit(solution)/shard_map/ppermute | solution.py:523
  286.8 20.9 %collective-permute-start.18 = (bf16[1024,128]{1,0:T(8,128)(2,1)S(1)}, bf16[1024,128]{1,0:T(8,128)(2,1)S(1)}, u32[]{:S(2)}, u32[]{:S(2)}) collective-permute-start(bf16[1024,128]{1,0:T(8,128)(2,1)S(1)} %get-tuple-element.104), channel_id=1, source_target_pairs={{0,1},{1,0},{2,3},{3,2},{4,5},{5,4},{6,7},{7,6},{8,9},{9,8},{10,11... | collective-permute-start | bytes 786440 | tf_op jit(solution)/shard_map/ppermute | solution.py:523
  291.5 16.3 %copy-start.26 = (bf16[512,768]{1,0:T(8,128)(2,1)S(1)}, bf16[512,768]{1,0:T(8,128)(2,1)}, u32[]{:S(2)}) copy-start(bf16[512,768]{1,0:T(8,128)(2,1)} %copy-done.25) | copy-start | bytes 2359300
  307.8 61.9 %copy-start.47 = (bf16[1024,1024]{1,0:T(8,128)(2,1)S(1)}, bf16[1024,1024]{1,0:T(8,128)(2,1)}, u32[]{:S(2)}) copy-start(bf16[1024,1024]{1,0:T(8,128)(2,1)} %copy-done.46) | copy-start | bytes 6291460
  368.9 116.4 %collective-permute-start.24 = (bf16[1024,384]{1,0:T(8,128)(2,1)S(1)}, bf16[1024,384]{1,0:T(8,128)(2,1)S(1)}, u32[]{:S(2)}, u32[]{:S(2)}) collective-permute-start(bf16[1024,384]{1,0:T(8,128)(2,1)S(1)} %get-tuple-element.86), channel_id=1, source_target_pairs={{0,1},{1,0},{2,3},{3,2},{4,5},{5,4},{6,7},{7,6},{8,9},{9,8},{10,11... | collective-permute-start | bytes 2359304 | tf_op jit(solution)/shard_map/ppermute | solution.py:523
  369.4 487.3 %collective-permute-start.26 = (bf16[1024,384]{1,0:T(8,128)(2,1)}, bf16[1024,384]{1,0:T(8,128)(2,1)}, u32[]{:S(2)}, u32[]{:S(2)}) collective-permute-start(bf16[1024,384]{1,0:T(8,128)(2,1)} %get-tuple-element.88), channel_id=1, source_target_pairs={{0,2},{1,3},{2,0},{3,1},{4,6},{5,7},{6,4},{7,5},{8,10},{9,11},{10,... | collective-permute-start | bytes 2359304 | tf_op jit(solution)/shard_map/ppermute | solution.py:523
  370.0 31.8 %collective-permute-start.23 = (bf16[1024,128]{1,0:T(8,128)(2,1)S(1)}, bf16[1024,128]{1,0:T(8,128)(2,1)S(1)}, u32[]{:S(2)}, u32[]{:S(2)}) collective-permute-start(bf16[1024,128]{1,0:T(8,128)(2,1)S(1)} %get-tuple-element.98), channel_id=1, source_target_pairs={{0,3},{1,2},{2,1},{3,0},{4,7},{5,6},{6,5},{7,4},{8,11},{9,10},{10,... | collective-permute-start | bytes 786440 | tf_op jit(solution)/shard_map/ppermute | solution.py:523
  371.2 41.3 %collective-permute-start.22 = (bf16[1024,128]{1,0:T(8,128)(2,1)S(1)}, bf16[1024,128]{1,0:T(8,128)(2,1)S(1)}, u32[]{:S(2)}, u32[]{:S(2)}) collective-permute-start(bf16[1024,128]{1,0:T(8,128)(2,1)S(1)} %get-tuple-element.99), channel_id=1, source_target_pairs={{0,2},{1,3},{2,0},{3,1},{4,6},{5,7},{6,4},{7,5},{8,10},{9,11},{10,... | collective-permute-start | bytes 786440 | tf_op jit(solution)/shard_map/ppermute | solution.py:523
  371.9 40.7 %collective-permute-start.21 = (bf16[1024,128]{1,0:T(8,128)(2,1)S(1)}, bf16[1024,128]{1,0:T(8,128)(2,1)S(1)}, u32[]{:S(2)}, u32[]{:S(2)}) collective-permute-start(bf16[1024,128]{1,0:T(8,128)(2,1)S(1)} %get-tuple-element.100), channel_id=1, source_target_pairs={{0,1},{1,0},{2,3},{3,2},{4,5},{5,4},{6,7},{7,6},{8,9},{9,8},{10,11... | collective-permute-start | bytes 786440 | tf_op jit(solution)/shard_map/ppermute | solution.py:523
  378.0 34.5 %copy-start.12 = (bf16[512,128]{1,0:T(8,128)(2,1)S(1)}, bf16[512,128]{1,0:T(8,128)(2,1)}, u32[]{:S(2)}) copy-start(bf16[512,128]{1,0:T(8,128)(2,1)} %copy-done.11) | copy-start | bytes 393220
  378.0 34.5 %copy-start.14 = (bf16[512,128]{1,0:T(8,128)(2,1)S(1)}, bf16[512,128]{1,0:T(8,128)(2,1)}, u32[]{:S(2)}) copy-start(bf16[512,128]{1,0:T(8,128)(2,1)} %copy-done.13) | copy-start | bytes 393220
  378.1 34.5 %copy-start.16 = (bf16[512,128]{1,0:T(8,128)(2,1)S(1)}, bf16[512,128]{1,0:T(8,128)(2,1)}, u32[]{:S(2)}) copy-start(bf16[512,128]{1,0:T(8,128)(2,1)} %copy-done.15) | copy-start | bytes 393220
  378.1 34.5 %copy-start.18 = (bf16[512,128]{1,0:T(8,128)(2,1)S(1)}, bf16[512,128]{1,0:T(8,128)(2,1)}, u32[]{:S(2)}) copy-start(bf16[512,128]{1,0:T(8,128)(2,1)} %copy-done.17) | copy-start | bytes 393220
  378.1 34.5 %copy-start.20 = (bf16[512,128]{1,0:T(8,128)(2,1)S(1)}, bf16[512,128]{1,0:T(8,128)(2,1)}, u32[]{:S(2)}) copy-start(bf16[512,128]{1,0:T(8,128)(2,1)} %copy-done.19) | copy-start | bytes 393220
  378.1 34.5 %copy-start.22 = (bf16[512,128]{1,0:T(8,128)(2,1)S(1)}, bf16[512,128]{1,0:T(8,128)(2,1)}, u32[]{:S(2)}) copy-start(bf16[512,128]{1,0:T(8,128)(2,1)} %copy-done.21) | copy-start | bytes 393220
  378.1 34.5 %copy-start.33 = (bf16[512,128]{1,0:T(8,128)(2,1)S(1)}, bf16[512,128]{1,0:T(8,128)(2,1)}, u32[]{:S(2)}) copy-start(bf16[512,128]{1,0:T(8,128)(2,1)} %copy-done.32) | copy-start | bytes 393220
  378.1 34.5 %copy-start.35 = (bf16[512,128]{1,0:T(8,128)(2,1)S(1)}, bf16[512,128]{1,0:T(8,128)(2,1)}, u32[]{:S(2)}) copy-start(bf16[512,128]{1,0:T(8,128)(2,1)} %copy-done.34) | copy-start | bytes 393220
  401.8 454.9 %collective-permute-start.28 = (bf16[1024,384]{1,0:T(8,128)(2,1)}, bf16[1024,384]{1,0:T(8,128)(2,1)}, u32[]{:S(2)}, u32[]{:S(2)}) collective-permute-start(bf16[1024,384]{1,0:T(8,128)(2,1)} %get-tuple-element.90), channel_id=1, source_target_pairs={{0,3},{1,2},{2,1},{3,0},{4,7},{5,6},{6,5},{7,4},{8,11},{9,10},{10,... | collective-permute-start | bytes 2359304 | tf_op jit(solution)/shard_map/ppermute | solution.py:523
  474.0 382.7 %collective-permute-start.25 = (bf16[1024,384]{1,0:T(8,128)(2,1)}, bf16[1024,384]{1,0:T(8,128)(2,1)}, u32[]{:S(2)}, u32[]{:S(2)}) collective-permute-start(bf16[1024,384]{1,0:T(8,128)(2,1)} %get-tuple-element.87), channel_id=1, source_target_pairs={{0,1},{1,0},{2,3},{3,2},{4,5},{5,4},{6,7},{7,6},{8,9},{9,8},{10,11... | collective-permute-start | bytes 2359304 | tf_op jit(solution)/shard_map/ppermute | solution.py:523
  477.1 379.6 %collective-permute-start.27 = (bf16[1024,384]{1,0:T(8,128)(2,1)}, bf16[1024,384]{1,0:T(8,128)(2,1)}, u32[]{:S(2)}, u32[]{:S(2)}) collective-permute-start(bf16[1024,384]{1,0:T(8,128)(2,1)} %get-tuple-element.89), channel_id=1, source_target_pairs={{0,2},{1,3},{2,0},{3,1},{4,6},{5,7},{6,4},{7,5},{8,10},{9,11},{10,... | collective-permute-start | bytes 2359304 | tf_op jit(solution)/shard_map/ppermute | solution.py:523
  485.4 344.5 %copy-start.9 = (bf16[1024,384]{1,0:T(8,128)(2,1)}, bf16[1024,384]{1,0:T(8,128)(2,1)S(1)}, u32[]{:S(2)}) copy-start(bf16[1024,384]{1,0:T(8,128)(2,1)S(1)} %collective-permute-done.24.refs_2_) | copy-start | bytes 2359300
  485.4 371.3 %collective-permute-start.29 = (bf16[1024,384]{1,0:T(8,128)(2,1)}, bf16[1024,384]{1,0:T(8,128)(2,1)}, u32[]{:S(2)}, u32[]{:S(2)}) collective-permute-start(bf16[1024,384]{1,0:T(8,128)(2,1)} %get-tuple-element.91), channel_id=1, source_target_pairs={{0,3},{1,2},{2,1},{3,0},{4,7},{5,6},{6,5},{7,4},{8,11},{9,10},{10,... | collective-permute-start | bytes 2359304 | tf_op jit(solution)/shard_map/ppermute | solution.py:523
  (24 other events, 178.6 us)
Sparse Core Ops, SparseCore 0:
  291.6 376.8 all-reduce.1

commit v3 on v2

--- a/solution.py
+++ b/solution.py
@@ -10,6 +10,10 @@
 LOG2E = 1.4426950408889634
 NEG_BIG = -1e30
 BLK = 512
+MIB = 2 ** 20
+PAIR = range(2)
+SLOTS = range(4)
+FOLD = dict(axis=0, keepdims=True)
 F32 = jnp.float32
 BF16 = jnp.bfloat16
 
@@ -65,33 +69,33 @@
         off = pl.multiple_of(tab_ref[key_idx] * BLK, BLK)
         k_blk = k_ref[pl.ds(off, BLK), :]
         out = []
-        for h in range(2):
+        scores = [nt(k_blk, q_half[h]) for h in PAIR]
+        for h in PAIR:
             m_row, l_row, acc = state[3 * h:3 * h + 3]
-            s = nt(k_blk, q_half[h])
+            s = scores[h]
             if diag:
-                kk = lax.broadcasted_iota(jnp.int32, (BLK, BLK), 0)
-                qq = lax.broadcasted_iota(jnp.int32, (BLK, BLK), 1)
-                s = jnp.where(kk <= qq, s, NEG_BIG)
-            m_new = jnp.maximum(m_row, jnp.max(s, axis=0, keepdims=True))
+                s = jnp.where(kept, s, NEG_BIG)
+            m_new = jnp.maximum(m_row, jnp.max(s, **FOLD))
             fac = jnp.exp2((m_row - m_new) * LOG2E)
             p = jnp.exp2((s - m_new) * LOG2E)
-            l_row = l_row * fac + jnp.sum(p, axis=0, keepdims=True)
+            l_row = l_row * fac + jnp.sum(p, **FOLD)
             vt = vt_ref[64 * h:64 * h + 64, pl.ds(off, BLK)]
             acc = acc * fac + nn(vt, p.astype(BF16))
             out += [m_new, l_row, acc]
         return tuple(out)
 
+    kept = lax.broadcasted_iota(jnp.int32, (BLK, BLK), 0) <= lax.broadcasted_iota(jnp.int32, (BLK, BLK), 1)
     fresh = (jnp.full((1, BLK), NEG_BIG, F32), jnp.zeros((1, BLK), F32), jnp.zeros((64, BLK), F32))
     state = lax.fori_loop(0, seq, lambda j, st: update(j, st, False), fresh + fresh)
     state = update(seq, state, True)
     o_t = jnp.concatenate([state[2] / state[1], state[5] / state[4]], axis=0)
     o_ref[pl.ds(q_off, BLK), :] = o_t.T.astype(BF16)
-    for h in range(2):
+    for h in PAIR:
         lse_ref[0, h:h + 1, pl.ds(q_off, BLK)] = (state[3 * h] + jnp.log(state[3 * h + 1])) * LOG2E
 
     @pl.when(step == 3)
     def _():
-        for j in range(4):
+        for j in SLOTS:
             o_refs[j][...] = o_ref[pl.ds(j * BLK, BLK), :]
 
 
@@ -107,13 +111,13 @@
                  + [[(do_refs[b % 4], (b // 4) * BLK, 0) for b in range(8)], [(r, 0, 0) for r in o_refs]],
                  [q_ref, k_ref, v_ref, do_ref, o_ref], sem)
         dqt_ref[...] = jnp.zeros_like(dqt_ref)
-        for i in range(2):
+        for i in PAIR:
             lse_ref[:, i * 4 * BLK:(i + 1) * 4 * BLK] = lse_refs[i][0]
         for b in range(n_blk):
             rows = pl.ds(b * BLK, BLK)
             prod = (do_ref[rows, :].astype(F32) * o_ref[rows, :].astype(F32)).T
-            dot_ref[0:1, rows] = jnp.sum(prod[:64], axis=0, keepdims=True)
-            dot_ref[1:2, rows] = jnp.sum(prod[64:], axis=0, keepdims=True)
+            dot_ref[0:1, rows] = jnp.sum(prod[:64], **FOLD)
+            dot_ref[1:2, rows] = jnp.sum(prod[64:], **FOLD)
 
     k_off = pl.multiple_of(tab_ref[step] * BLK, BLK)
     k_blk = k_ref[pl.ds(k_off, BLK), :]
@@ -125,7 +129,7 @@
         off = pl.multiple_of(tab_ref[q_idx] * BLK, BLK)
         q_blk = q_ref[pl.ds(off, BLK), :] * jnp.asarray(0.125, BF16)
         do_blk = do_ref[pl.ds(off, BLK), :]
-        for h in range(2):
+        for h in PAIR:
             q_h = pick(q_blk, h)
             do_h = pick(do_blk, h)
             s = nt(k_blk, q_h)
@@ -157,6 +161,14 @@
             out_refs[b % 4][dst, 128:384] = dkv_ref[span, :]
 
 
+def first_block(i, tab):
+    return 0, 0
+
+
+def first_block3(i, tab):
+    return 0, 0, 0
+
+
 def pair_cost(n_pairs, n_dots):
     return pl.CostEstimate(flops=2 * n_pairs * BLK * BLK * 128 * n_dots * 6, bytes_accessed=2 ** 22,
                            transcendentals=2 * n_pairs * BLK * BLK)
@@ -175,11 +187,11 @@
         grid_spec=pltpu.PrefetchScalarGridSpec(
             num_scalar_prefetch=1, grid=(4,),
             in_specs=[ANY] * n_in,
-            out_specs=[pl.BlockSpec((BLK, 128), lambda i, tab: (0, 0))] * 4
-                      + [pl.BlockSpec((1, 2, half), lambda i, tab: (0, 0, 0))],
+            out_specs=[pl.BlockSpec((BLK, 128), first_block)] * 4
+                      + [pl.BlockSpec((1, 2, half), first_block3)],
             scratch_shapes=[buf(4), buf(n_in), buf(n_in), pltpu.VMEM((128, n_in * BLK), BF16), buf(4),
                             pltpu.SemaphoreType.DMA]),
-        compiler_params=pltpu.CompilerParams(vmem_limit_bytes=48 * 1024 * 1024),
+        compiler_params=pltpu.CompilerParams(vmem_limit_bytes=48 * MIB),
         cost_estimate=pair_cost(26 if first else 10, 2),
         name='attn_fwd')(tab, *qkv)
 
@@ -192,20 +204,20 @@
         out_shape=[jax.ShapeDtypeStruct((2 * BLK, 384), BF16)] * 4,
         grid_spec=pltpu.PrefetchScalarGridSpec(
             num_scalar_prefetch=1, grid=(8,),
-            in_specs=[ANY] * 20 + [pl.BlockSpec((1, 2, seq_len // 2), lambda i, tab: (0, 0, 0))] * 2,
-            out_specs=[pl.BlockSpec((2 * BLK, 384), lambda i, tab: (0, 0))] * 4,
+            in_specs=[ANY] * 20 + [pl.BlockSpec((1, 2, seq_len // 2), first_block3)] * 2,
+            out_specs=[pl.BlockSpec((2 * BLK, 384), first_block)] * 4,
             scratch_shapes=[buf, buf, buf, buf, buf, pltpu.VMEM((2, seq_len), F32), pltpu.VMEM((128, seq_len), F32),
                             pltpu.VMEM((2, seq_len), F32), pltpu.VMEM((seq_len, 256), BF16), pltpu.SemaphoreType.DMA]),
-        compiler_params=pltpu.CompilerParams(vmem_limit_bytes=48 * 1024 * 1024),
+        compiler_params=pltpu.CompilerParams(vmem_limit_bytes=48 * MIB),
         cost_estimate=pair_cost(36, 5),
         name='attn_bwd')(tab, *qkv, *d_o, *out_o, *lses)
 
 
 def attend_out_kernel(rank_ref, x_ref, wo_ref, *refs):
     parts, hid_ref, o_ref = refs[:16], refs[16], refs[17]
-    for i in range(2):
-        for j in range(4):
-            for p in range(2):
+    for i in PAIR:
+        for j in SLOTS:
+            for p in PAIR:
                 col = pl.multiple_of(rank_ref[1 + j] * 256 + 128 * p, 128)
                 o_ref[pl.ds(i * BLK, BLK), pl.ds(col, 128)] = parts[8 * i + 2 * j + p][...]
 
@@ -223,7 +235,7 @@
         out_shape=[jax.ShapeDtypeStruct(x.shape, BF16)] * 2,
         in_specs=[pl.BlockSpec(memory_space=pltpu.SMEM)] + [pl.BlockSpec(memory_space=pltpu.VMEM)] * 18,
         out_specs=[pl.BlockSpec(memory_space=pltpu.VMEM)] * 2,
-        compiler_params=pltpu.CompilerParams(vmem_limit_bytes=32 * 1024 * 1024),
+        compiler_params=pltpu.CompilerParams(vmem_limit_bytes=32 * MIB),
         cost_estimate=pl.CostEstimate(flops=2 ** 31, bytes_accessed=2 ** 23, transcendentals=0),
         name='attend_out')(where, x, wo, *parts)
 
@@ -231,10 +243,10 @@
 def input_grad_kernel(where_ref, base_ref, w_ref, *refs):
     parts, out_ref = refs[:8], refs[8]
     acc = base_ref[...].astype(F32)
-    for j in range(4):
-        for p in range(2):
-            row = pl.multiple_of((where_ref[1 + j] * 2 + p) * 384, 128)
-            acc = acc + nn(parts[2 * j + p][...], w_ref[pl.ds(row, 384), :])
+    for j in SLOTS:
+        row = pl.multiple_of(where_ref[1 + j] * 768, 128)
+        both = jnp.concatenate([parts[2 * j][...], parts[2 * j + 1][...]], axis=1)
+        acc = acc + nn(both, w_ref[pl.ds(row, 768), :])
     out_ref[...] = acc.astype(BF16)
 
 
@@ -246,18 +258,57 @@
         out_shape=jax.ShapeDtypeStruct(base.shape, BF16),
         grid_spec=pltpu.PrefetchScalarGridSpec(
             num_scalar_prefetch=1, grid=(rows // tile,),
-            in_specs=[pl.BlockSpec((tile, cols), lambda i, s: (i, 0)), pl.BlockSpec(w_qkv.shape, lambda i, s: (0, 0))]
+            in_specs=[pl.BlockSpec((tile, cols), lambda i, s: (i, 0)), pl.BlockSpec(w_qkv.shape, first_block)]
                      + [pl.BlockSpec((tile, 384), lambda i, s: (i, 0))] * 8,
             out_specs=pl.BlockSpec((tile, cols), lambda i, s: (i, 0))),
-        compiler_params=pltpu.CompilerParams(vmem_limit_bytes=40 * 1024 * 1024),
+        compiler_params=pltpu.CompilerParams(vmem_limit_bytes=40 * MIB),
         cost_estimate=pl.CostEstimate(flops=6 * 2 ** 30, bytes_accessed=2 ** 24, transcendentals=0),
         name='input_grad')(where, base, w_qkv, *parts)
+
+
+def qkv_grad_kernel(scale, *refs):
+    parts, xs, out_ref, lt_ref = refs[:8], refs[8:16], refs[16], refs[17]
+    for p in PAIR:
+        for j in SLOTS:
+            for i in PAIR:
+                block = parts[4 * p + j][i * BLK:(i + 1) * BLK, :]
+                lt_ref[:, pl.ds((4 * i + j) * BLK, BLK)] = block.astype(F32).T.astype(BF16)
+
+        def tile(n, carry):
+            cols = pl.ds(pl.multiple_of(n * 256, 256), 256)
+            acc = nn(lt_ref[:, 0:BLK], xs[0][:, cols])
+            for b in range(1, 8):
+                acc = acc + nn(lt_ref[:, b * BLK:(b + 1) * BLK], xs[b][:, cols])
+            out_ref[p * 384:(p + 1) * 384, cols] = acc * scale
+            return carry
+
+        lax.fori_loop(0, out_ref.shape[1] // 256, tile, 0)
+
+
+def qkv_grad(scale, parts, xs):
+    d_model = xs[0].shape[1]
+    vmem = pl.BlockSpec(memory_space=pltpu.VMEM)
+    return pl.pallas_call(
+        functools.partial(qkv_grad_kernel, scale),
+        out_shape=jax.ShapeDtypeStruct((768, d_model), F32),
+        in_specs=[vmem] * 16, out_specs=vmem,
+        scratch_shapes=[pltpu.VMEM((384, 8 * BLK), BF16)],
+        compiler_params=pltpu.CompilerParams(vmem_limit_bytes=48 * MIB),
+        cost_estimate=pl.CostEstimate(flops=6 * 2 ** 30, bytes_accessed=2 ** 24, transcendentals=0),
+        name='qkv_grad')(*parts, *xs)
 
 
 MESH = pl.DeviceIdType.MESH
 LAG = 2
 UNIT = 256
 WIDE = 1024
+HALF, QUART, EIGHTH, LEAF = UNIT // 2, UNIT // 4, UNIT // 8, UNIT // 32
+HOPS = (1, 2, 3)
+MROW = 64
+MHALF = 32
+ROW = 8
+BIG = 1024
+HELD = 256
 
 
 def sum_kernel(up_ref, mine_ref, up_out, qkv_out, acc, rc, r1, r2, rz, macc, my, mz,
@@ -270,7 +321,7 @@
     core_id = ids(dp, 2 * x + 1 - c)
     x_id = ids(dp, 2 * (1 - x) + c)
     y_id = ids(2 * z + 1 - y, cp)
-    z_ids = [ids(2 * ((z + k) % 4) + y, cp) for k in (1, 2, 3)]
+    z_ids = [ids(2 * ((z + k) % 4) + y, cp) for k in HOPS]
 
     barrier = pltpu.get_barrier_semaphore()
     for peer in [core_id, x_id, y_id] + z_ids:
@@ -283,7 +334,7 @@
 
     class Up:
         def __init__(self, u):
-            color = u % 2
+            color = (u % 3 + 2) // 3
             self.u = u
             self.row = (u // blocks) * UNIT
             self.cols = pl.ds(pl.multiple_of((u % blocks) * WIDE, WIDE), WIDE)
@@ -291,60 +342,60 @@
             self.b2 = y + color * (x - y)
             self.d1 = ids(2 * z + y + color * (1 - 2 * y), 2 * (x + (1 - color) * (1 - 2 * x)) + c)
             self.d2 = ids(2 * z + y + (1 - color) * (1 - 2 * y), 2 * (x + color * (1 - 2 * x)) + c)
-            self.base = self.b1 * (UNIT // 4) + self.b2 * (UNIT // 8)
+            self.base = self.b1 * QUART + self.b2 * EIGHTH
 
         def src(self, off, n):
-            return up_ref.at[pl.ds(pl.multiple_of(self.row + off, 8), n), self.cols]
+            return up_ref.at[pl.ds(pl.multiple_of(self.row + off, ROW), n), self.cols]
 
         def out(self, off, n):
-            return up_out.at[pl.ds(pl.multiple_of(self.row + off, 8), n), self.cols]
+            return up_out.at[pl.ds(pl.multiple_of(self.row + off, ROW), n), self.cols]
 
         def part(self, off, n):
-            return acc.at[self.u, pl.ds(pl.multiple_of(off, 8), n), :]
+            return acc.at[self.u, pl.ds(pl.multiple_of(off, ROW), n), :]
 
         def pair(self, i, src, dst, dev):
             return remote(src, dst, pairs.at[self.u, i, 0], pairs.at[self.u, i, 1], dev)
 
         def load(self):
-            return pltpu.make_async_copy(self.src(c * (UNIT // 2), UNIT // 2), acc.at[self.u], one.at[self.u, 0])
+            return pltpu.make_async_copy(self.src(c * HALF, HALF), acc.at[self.u], one.at[self.u, 0])
 
         def core(self):
-            return self.pair(0, self.src((1 - c) * (UNIT // 2), UNIT // 2), rc.at[self.u], core_id)
+            return self.pair(0, self.src((1 - c) * HALF, HALF), rc.at[self.u], core_id)
 
         def first(self):
-            return self.pair(1, self.part((1 - self.b1) * (UNIT // 4), UNIT // 4), r1.at[self.u], self.d1)
+            return self.pair(1, self.part((1 - self.b1) * QUART, QUART), r1.at[self.u], self.d1)
 
         def second(self):
-            return self.pair(2, self.part(self.b1 * (UNIT // 4) + (1 - self.b2) * (UNIT // 8), UNIT // 8),
+            return self.pair(2, self.part(self.b1 * QUART + (1 - self.b2) * EIGHTH, EIGHTH),
                              r2.at[self.u], self.d2)
 
         def zs(self):
-            n = UNIT // 32
+            n = LEAF
             return [remote(self.part(self.base + ((z + k) % 4) * n, n), rz.at[self.u, k - 1],
-                           tri_s.at[self.u, k - 1], tri_r.at[self.u, k - 1], z_ids[k - 1]) for k in (1, 2, 3)]
+                           tri_s.at[self.u, k - 1], tri_r.at[self.u, k - 1], z_ids[k - 1]) for k in HOPS]
 
         def back_zs(self):
-            n = UNIT // 32
-            dst = self.out(c * (UNIT // 2) + self.base + z * n, n)
+            n = LEAF
+            dst = self.out(c * HALF + self.base + z * n, n)
             return [remote(self.part(self.base + z * n, n), dst,
-                           tri_as.at[self.u, k - 1], tri_ar.at[self.u, k - 1], z_ids[k - 1]) for k in (1, 2, 3)]
+                           tri_as.at[self.u, k - 1], tri_ar.at[self.u, k - 1], z_ids[k - 1]) for k in HOPS]
 
         def keep(self):
-            n = UNIT // 32
+            n = LEAF
             return pltpu.make_async_copy(self.part(self.base + z * n, n),
-                                         self.out(c * (UNIT // 2) + self.base + z * n, n), one.at[self.u, 1])
+                                         self.out(c * HALF + self.base + z * n, n), one.at[self.u, 1])
 
         def back(self, i, off, n, dev):
             return self.pair(i, self.out(off, n), self.out(off, n), dev)
 
         def back_second(self):
-            return self.back(3, c * (UNIT // 2) + self.base, UNIT // 8, self.d2)
+            return self.back(3, c * HALF + self.base, EIGHTH, self.d2)
 
         def back_first(self):
-            return self.back(4, c * (UNIT // 2) + self.b1 * (UNIT // 4), UNIT // 4, self.d1)
+            return self.back(4, c * HALF + self.b1 * QUART, QUART, self.d1)
 
         def back_core(self):
-            return self.back(5, c * (UNIT // 2), UNIT // 2, core_id)
+            return self.back(5, c * HALF, HALF, core_id)
 
     def add_into(ref, other):
         ref[...] = ref[...] + other[...]
@@ -357,14 +408,14 @@
             add_into(acc.at[u], rc.at[u])
         elif s == 2:
             w.first().wait_recv()
-            add_into(w.part(w.b1 * (UNIT // 4), UNIT // 4), r1.at[u])
+            add_into(w.part(w.b1 * QUART, QUART), r1.at[u])
         elif s == 3:
             w.second().wait_recv()
-            add_into(w.part(w.base, UNIT // 8), r2.at[u])
+            add_into(w.part(w.base, EIGHTH), r2.at[u])
         elif s == 4:
             for cpy in w.zs():
                 cpy.wait_recv()
-            n = UNIT // 32
+            n = LEAF
             dst = w.part(w.base + z * n, n)
             dst[...] = dst[...] + (rz[u, 0] + rz[u, 1] + rz[u, 2])
         elif s == 5:
@@ -392,60 +443,60 @@
     class Mine:
         def __init__(self, m):
             self.m = m
-            self.orow = (m // 4) * 1024 + (m % 4) * 64
+            self.orow = (m % 6) // 2 * BIG + m // 6 * 128 + m % 2 * MROW
 
         def out(self, holder, off, n):
-            return qkv_out.at[pl.ds(pl.multiple_of(self.orow + holder * 256 + off, 8), n), :]
+            return qkv_out.at[pl.ds(pl.multiple_of(self.orow + holder * HELD + off, ROW), n), :]
 
         def part(self, off, n):
-            return macc.at[self.m, pl.ds(pl.multiple_of(off, 8), n), :]
+            return macc.at[self.m, pl.ds(pl.multiple_of(off, ROW), n), :]
 
         def pair(self, i, src, dst, dev):
             return remote(src, dst, m_pairs.at[self.m, i, 0], m_pairs.at[self.m, i, 1], dev)
 
         def load(self):
-            return pltpu.make_async_copy(mine_ref.at[pl.ds(pl.multiple_of(self.m * 64, 8), 64), :], macc.at[self.m],
+            return pltpu.make_async_copy(mine_ref.at[pl.ds(pl.multiple_of(self.m * MROW, ROW), MROW), :], macc.at[self.m],
                                          m_one.at[self.m, 0])
 
         def ys(self):
-            return self.pair(0, mine_ref.at[pl.ds(pl.multiple_of(self.m * 64 + (1 - y) * 32, 8), 32), :],
+            return self.pair(0, mine_ref.at[pl.ds(pl.multiple_of(self.m * MROW + (1 - y) * MHALF, ROW), MHALF), :],
                              my.at[self.m], y_id)
 
         def zs(self):
-            return [remote(self.part(y * 32 + ((z + k) % 4) * 8, 8), mz.at[self.m, k - 1],
-                           m_tri_s.at[self.m, k - 1], m_tri_r.at[self.m, k - 1], z_ids[k - 1]) for k in (1, 2, 3)]
+            return [remote(self.part(y * MHALF + ((z + k) % 4) * ROW, ROW), mz.at[self.m, k - 1],
+                           m_tri_s.at[self.m, k - 1], m_tri_r.at[self.m, k - 1], z_ids[k - 1]) for k in HOPS]
 
         def back_zs(self):
-            return [remote(self.part(y * 32 + z * 8, 8), self.out(cp, y * 32 + z * 8, 8),
-                           m_tri_as.at[self.m, k - 1], m_tri_ar.at[self.m, k - 1], z_ids[k - 1]) for k in (1, 2, 3)]
+            return [remote(self.part(y * MHALF + z * ROW, ROW), self.out(cp, y * MHALF + z * ROW, ROW),
+                           m_tri_as.at[self.m, k - 1], m_tri_ar.at[self.m, k - 1], z_ids[k - 1]) for k in HOPS]
 
         def keep(self):
-            return pltpu.make_async_copy(self.part(y * 32 + z * 8, 8), self.out(cp, y * 32 + z * 8, 8),
+            return pltpu.make_async_copy(self.part(y * MHALF + z * ROW, ROW), self.out(cp, y * MHALF + z * ROW, ROW),
                                          m_one.at[self.m, 1])
 
         def back_y(self):
-            return self.pair(1, self.out(cp, y * 32, 32), self.out(cp, y * 32, 32), y_id)
+            return self.pair(1, self.out(cp, y * MHALF, MHALF), self.out(cp, y * MHALF, MHALF), y_id)
 
         def back_x(self):
-            return self.pair(2, self.out(cp, 0, 64), self.out(cp, 0, 64), x_id)
+            return self.pair(2, self.out(cp, 0, MROW), self.out(cp, 0, MROW), x_id)
 
         def back_core(self):
-            return self.pair(3, self.out(cp, 0, 64), self.out(cp, 0, 64), core_id)
+            return self.pair(3, self.out(cp, 0, MROW), self.out(cp, 0, MROW), core_id)
 
         def back_far(self):
             far = 2 * (1 - x) + c
-            return self.pair(4, self.out(far, 0, 64), self.out(far, 0, 64), core_id)
+            return self.pair(4, self.out(far, 0, MROW), self.out(far, 0, MROW), core_id)
 
     def mine_take(s, m):
         w = Mine(m)
         if s == 1:
             w.load().wait()
             w.ys().wait_recv()
-            add_into(w.part(y * 32, 32), my.at[m])
+            add_into(w.part(y * MHALF, MHALF), my.at[m])
         elif s == 2:
             for cpy in w.zs():
                 cpy.wait_recv()
-            dst = w.part(y * 32 + z * 8, 8)
+            dst = w.part(y * MHALF + z * ROW, ROW)
             dst[...] = dst[...] + (mz[m, 0] + mz[m, 1] + mz[m, 2])
         elif s == 3:
             for cpy in w.back_zs():
@@ -491,7 +542,7 @@
 
 def sum_grads(up, mine):
     n_up = up.shape[0] * up.shape[1] // (UNIT * WIDE)
-    n_mine = mine.shape[0] // 64
+    n_mine = mine.shape[0] // MROW
     cols = mine.shape[1]
     dma = pltpu.SemaphoreType.DMA
     vm = lambda *shape: pltpu.VMEM(shape, F32)
@@ -501,11 +552,11 @@
         in_specs=[ANY] * 2, out_specs=[ANY] * 2,
         scratch_shapes=[vm(n_up, UNIT // 2, WIDE), vm(n_up, UNIT // 2, WIDE), vm(n_up, UNIT // 4, WIDE),
                         vm(n_up, UNIT // 8, WIDE), vm(n_up, 3, UNIT // 32, WIDE),
-                        vm(n_mine, 64, cols), vm(n_mine, 32, cols), vm(n_mine, 3, 8, cols),
+                        vm(n_mine, MROW, cols), vm(n_mine, MHALF, cols), vm(n_mine, 3, ROW, cols),
                         dma((n_up, 2)), dma((n_up, 6, 2))] + [dma((n_up, 3))] * 4
                        + [dma((n_mine, 2)), dma((n_mine, 5, 2))] + [dma((n_mine, 3))] * 4,
         compiler_params=pltpu.CompilerParams(collective_id=0, has_side_effects=True,
-                                             vmem_limit_bytes=56 * 1024 * 1024),
+                                             vmem_limit_bytes=56 * MIB),
         cost_estimate=pl.CostEstimate(flops=200 * 10 ** 9, bytes_accessed=2 ** 26, transcendentals=0),
         name='sum_grads')(up, mine)
 
@@ -529,7 +580,7 @@
         width = d_model // cp_size
         n_pairs = width // 128
         slots = range(cp_size)
-        halves = range(2)
+        halves = PAIR
         w_t = [jnp.transpose(w, (1, 2, 0)).reshape(d_model // 128, 1, 128, d_model) for w in (w_q, w_k, w_v)]
         w_qkv = jnp.concatenate(w_t, axis=1).reshape(3 * d_model, d_model)
         wo2 = w_o.reshape(d_model, d_model)
@@ -561,7 +612,6 @@
         act_b = act_val.astype(BF16)
         grad_pre = gelu_pull(grad_act.astype(F32))[0].astype(BF16)
         grad_down = tn(act_b, g_out) * inv
-        grad_down = lax.psum(grad_down, ('dp', 'cp'))
         grad_hidden = (g_out.astype(F32) + nt(grad_pre, w_up)).astype(BF16)
         grad_attn = nt(grad_hidden, wo2).astype(BF16)
 
@@ -572,25 +622,25 @@
             pieces = [lax.dynamic_slice(grad_attn, (0, (rank ^ j) * width + 128 * pair), (tokens, 128)) for j in slots]
             d_o.append([flip(pieces[j], j) for j in slots])
             if not pair:
-                grad_uo = jnp.concatenate([tn(hidden, grad_pre) * inv, tn(o_own, grad_hidden) * inv], axis=1)
-                d_o[0], grad_uo = lax.optimization_barrier((d_o[0], grad_uo))
+                grad_up = tn(hidden, grad_pre)
+                grad_o = tn(o_own, grad_hidden) * inv
+                d_o[0], grad_up = lax.optimization_barrier((d_o[0], grad_up))
+                grad_down, grad_o = lax.psum((grad_down, grad_o), ('dp', 'cp'))
 
         grads, back = [], {}
-        x_full = [jnp.concatenate([x_all[0][j], x_all[1][j]], axis=0) if j else x_own for j in slots]
         for pair in range(n_pairs):
             parts = attn_bwd(tab, qkv[0] + qkv[1], d_o[pair], attn_o[pair, 0] + attn_o[pair, 1],
                              [lses[pair, i] for i in halves], pair)
             for j in slots:
                 back[j, pair] = flip(parts[j], j)
-            grads.append(sum(tn(parts[j], x_full[j]) for j in slots) * inv)
-        mine = jnp.concatenate(grads, axis=0).reshape(n_pairs, 3, 128, d_model)
-        mine = jnp.transpose(mine, (1, 0, 2, 3)).reshape(3 * width, d_model)
-        g_uo, g_qkv = sum_grads(grad_uo, mine)
-        d_ff = w_up.shape[1]
+            grads += parts
+        mine = qkv_grad(inv, grads, x_all[0] + x_all[1])
+        g_up, g_qkv = sum_grads(grad_up, mine)
+        g_up = g_up * inv
         outs = [jnp.transpose(g_qkv[t * d_model:(t + 1) * d_model].reshape(w.shape[1], w.shape[2], d_model), (2, 0, 1))
                 for t, w in enumerate((w_q, w_k, w_v))]
         d_x = input_grad(where, grad_hidden, w_qkv, [back[j, p] for j in slots for p in range(n_pairs)])
-        return (d_x[None], *outs, g_uo[:, d_ff:].reshape(w_o.shape), g_uo[:, :d_ff], grad_down)
+        return (d_x[None], *outs, grad_o.reshape(w_o.shape), g_up, grad_down)
 
     act_spec = P('dp', 'cp', None)
     return jax.shard_map(layer, mesh=mesh,

time: 900 us -> 811 us (0.901)
  waiting for transfers between devices: 71.6 us -> 40.8 us
  Pallas kernels: 578 us -> 551 us
  matrix products: 114 us -> 95.5 us
    ppermute x30, waiting for transfers between devices: 71.5 us -> 40.8 us  [flip(): lax.ppermute(arr, 'cp', [(i, i ^ bit) for i in range(cp_size)])]
    pallas_call x1, Pallas kernels: 343 us -> 316 us  [sum_grads(): pl.pallas_call(sum_kernel, out_shape=[jax.ShapeDtypeStruct(up.shape, F32)...]
    concatenate x2 -> x0, other arithmetic: 16.6 us -> none  [the longest x1 16.2 us: layer(): jnp.concatenate([tn(hidden, grad_pre) * inv, tn(o_own, grad_hidden) * inv...]
    slice x2 -> x0, local copies, waits for them, and re-layouts: 16.5 us -> none  [the longest x1 11.7 us: layer(): g_uo[:, :d_ff]]
    pallas_call x0 -> x1, Pallas kernels: none -> 16.4 us  [qkv_grad(): pl.pallas_call(functools.partial(qkv_grad_kernel, scale), out_shape=jax.S...]
    pallas_call x4, Pallas kernels: 94 us -> 78.7 us  [attn_fwd(): pl.pallas_call(functools.partial(attn_fwd_kernel, pair, n_in, first), out...]
    dot_general x11 -> x3, matrix products: 49 us -> 34.5 us  [tn(): lax.dot_general(a, b, (((0,), (0,)), ((), ())), preferred_element_type=F32)]
    unnamed x118 -> x134, local copies, waits for them, and re-layouts: 19 us -> 33 us
  transfers between devices with their start and end apart: 31 -> 31, of which waited for: 10 -> 6; matrix products, arithmetic and copies ran while one was open for 12% -> 7% of each run, Pallas kernels for 55% -> 61%
where the time goes in v3:
time: 811 us; the launch traced here: 801 us
  Pallas kernels  551 us (68%)
  matrix products  95.5 us (12%)
  local copies, waits for them, and re-layouts  49.1 us (6%)
  waiting for transfers between devices  40.8 us (5%)
  other arithmetic  30.3 us (4%)
  starting transfers between devices  20 us (2%)
  between operations  15.2 us (2%)
    pallas_call x1, Pallas kernels, sum_grads(): pl.pallas_call(sum_kernel, out_shape=[jax.ShapeDtypeStruct(up.shape, F32)...  316 us
    pallas_call x2, Pallas kernels, attn_bwd(): pl.pallas_call(functools.partial(attn_bwd_kernel, pair), out_shape=[jax.S...  123 us
    pallas_call x4, Pallas kernels, attn_fwd(): pl.pallas_call(functools.partial(attn_fwd_kernel, pair, n_in, first), out...  78.7 us
    dot_general x11, matrix products, nt(): lax.dot_general(a, b, (((1,), (1,)), ((), ())), preferred_element_type=F32)  46.1 us
    ppermute x30, waiting for transfers between devices, flip(): lax.ppermute(arr, 'cp', [(i, i ^ bit) for i in range(cp_size)])  40.8 us
    dot_general x3, matrix products, tn(): lax.dot_general(a, b, (((0,), (0,)), ((), ())), preferred_element_type=F32)  34.5 us
    unnamed x134, local copies, waits for them, and re-layouts  33 us
    ppermute x30, starting transfers between devices, flip(): lax.ppermute(arr, 'cp', [(i, i ^ bit) for i in range(cp_size)])  20 us
  transfers between devices with their start and end apart: 31, of which 6 were waited for; matrix products, arithmetic and copies ran while one was open for 7% of the time, Pallas kernels for 61%

profile of v3, /device:TPU:0, one launch (start us, length us, event | category | flops | bytes accessed | tf_op | source)
XLA Modules:
  0.0 801.5 jit_solution(13569627224742293411)
XLA Ops:
  7.2 3.0 slice_bitcast_fusion
  10.2 3.0 collective-permute-start.10
  13.7 15.0 %convolution_convert_fusion.1 = bf16[1024,4096]{1,0:T(8,128)(2,1)} fusion(bf16[4096,1024]{1,0:T(8,128)(2,1)} %param.15, bf16[1,1024,1024]{2,1,0:T(8,128)(2,1)} %param.9), kind=kOutput, calls=%fused_computation.24 | convolution fusion | flops 8594128896 | bytes 18874368 | tf_op jit(solution)/shard_map/dot_general | solution.py:22
  28.7 3.0 pad_maximum_fusion
  31.8 1.0 fusion.18.refs_0_
  32.8 1.0 fusion.20.refs_4_
  33.9 25.3 %collective-permute-done.refs_10_ = bf16[512,1024]{1,0:T(8,128)(2,1)} collective-permute-done((bf16[512,1024]{1,0:T(8,128)(2,1)}, bf16[512,1024]{1,0:T(8,128)(2,1)}, u32[]{:S(2)}, u32[]{:S(2)}) %collective-permute-start) | collective-permute-done | bytes 1048608 | tf_op jit(solution)/shard_map/ppermute | solution.py:574
  59.7 2.2 convolution_convert_fusion.8.refs_2_
  61.9 2.5 fusion.22.refs_6_
  64.5 2.5 fusion.19.refs_1_
  67.1 2.5 fusion.21.refs_5_
  69.6 1.9 fusion.23.refs_7_
  71.6 1.0 convolution_convert_fusion.7.refs_3_
  72.6 28.5 %attn_fwd.7 = (bf16[512,128]{1,0:T(8,128)(2,1)S(1)}, bf16[512,128]{1,0:T(8,128)(2,1)S(1)}, bf16[512,128]{1,0:T(8,128)(2,1)S(1)}, bf16[512,128]{1,0:T(8,128)(2,1)S(1)}, f32[1,2,2048]{2,1,0:T(2,128)S(1)}) custom-call(s32[8]{0:T(128)S(1)} %compare_select_fusion.tab_ref, bf16[512,768]{1,0:T(8,128)(2,1)S(1)} %fusion.18.refs_0_, ...), custom_call_target="tpu_custom_call" | custom-call | flops 20937965568 | bytes 4194304 | tf_op jit(solution)/shard_map/attn_fwd/pallas_call | solution.py:184
  101.8 28.3 %attn_fwd.6 = (bf16[512,128]{1,0:T(8,128)(2,1)S(1)}, bf16[512,128]{1,0:T(8,128)(2,1)S(1)}, bf16[512,128]{1,0:T(8,128)(2,1)S(1)}, bf16[512,128]{1,0:T(8,128)(2,1)S(1)}, f32[1,2,2048]{2,1,0:T(2,128)S(1)}) custom-call(s32[8]{0:T(128)S(1)} %compare_select_fusion.tab_ref, bf16[512,768]{1,0:T(8,128)(2,1)S(1)} %fusion.18.refs_0_, ...), custom_call_target="tpu_custom_call" | custom-call | flops 20937965568 | bytes 4194304 | tf_op jit(solution)/shard_map/attn_fwd/pallas_call | solution.py:184
  130.8 1.8 collective-permute-start.15
  132.6 11.0 %attn_fwd.5 = (bf16[512,128]{1,0:T(8,128)(2,1)S(1)}, bf16[512,128]{1,0:T(8,128)(2,1)S(1)}, bf16[512,128]{1,0:T(8,128)(2,1)S(1)}, bf16[512,128]{1,0:T(8,128)(2,1)S(1)}, f32[1,2,2048]{2,1,0:T(2,128)S(1)}) custom-call(s32[8]{0:T(128)S(1)} %compare_select_fusion.tab_ref, bf16[512,768]{1,0:T(8,128)(2,1)S(1)} %fusion.18.refs_0_, ...), custom_call_target="tpu_custom_call" | custom-call | flops 8053063680 | bytes 4194304 | tf_op jit(solution)/shard_map/attn_fwd/pallas_call | solution.py:184
  145.2 1.8 collective-permute-start.14
  147.4 11.0 %attn_fwd.4 = (bf16[512,128]{1,0:T(8,128)(2,1)S(1)}, bf16[512,128]{1,0:T(8,128)(2,1)S(1)}, bf16[512,128]{1,0:T(8,128)(2,1)S(1)}, bf16[512,128]{1,0:T(8,128)(2,1)S(1)}, f32[1,2,2048]{2,1,0:T(2,128)S(1)}) custom-call(s32[8]{0:T(128)S(1)} %compare_select_fusion.tab_ref, bf16[512,768]{1,0:T(8,128)(2,1)S(1)} %fusion.18.refs_0_, ...), custom_call_target="tpu_custom_call" | custom-call | flops 8053063680 | bytes 4194304 | tf_op jit(solution)/shard_map/attn_fwd/pallas_call | solution.py:184
  159.7 1.8 collective-permute-start.6
  161.4 0.7 copy-done.13
  163.2 0.7 copy-done.17
  163.8 1.8 collective-permute-start.5
  165.6 0.7 copy-done.19
  166.3 1.8 collective-permute-done.8.refs_7_
  168.1 3.1 collective-permute-done.5.refs_4_
  171.2 2.4 collective-permute-done.7.refs_6_
  173.6 1.6 copy-done.1
  175.2 0.9 copy-done.14
  176.1 0.9 copy-done.16
  177.0 0.9 copy-done.18
  177.9 0.9 copy-done.20
  178.8 0.9 copy-done.29
  179.7 0.9 copy-done.32
  180.6 0.9 copy-done.35
  181.5 0.9 copy-done.38
  182.4 4.8 attend_out.1
  187.3 14.8 %convolution_convert_fusion = bf16[1024,4096]{1,0:T(8,128)(2,1)} fusion(bf16[1024,1024]{1,0:T(8,128)(2,1)S(1)} %get-tuple-element.69, bf16[1024,4096]{1,0:T(8,128)(2,1)} %param.14), kind=kOutput, calls=%fused_computation.23 | convolution fusion | flops 8594128896 | bytes 18874368 | tf_op jit(solution)/shard_map/dot_general | solution.py:26
  202.1 15.5 %fusion.3 = bf16[1024,4096]{1,0:T(8,128)(2,1)} fusion(bf16[1024,4096]{1,0:T(8,128)(2,1)S(1)} %bitcast.78, bf16[1024,4096]{1,0:T(8,128)(2,1)} %convolution_convert_fusion), kind=kLoop, calls=%fused_computation.9 | loop fusion | flops 92274688 | bytes 25165824 | tf_op jit(solution)/shard_map/convert_element_type | solution.py:613
  217.6 13.9 %add_convert_fusion.base_ref = bf16[1024,1024]{1,0:T(8,128)(2,1)S(1)} fusion(bf16[1,1024,1024]{2,1,0:T(8,128)(2,1)S(1)} %copy-done.58, bf16[1024,4096]{1,0:T(8,128)(2,1)} %fusion.3, bf16[1024,4096]{1,0:T(8,128)(2,1)} %param.14), kind=kOutput, calls=%fused_computation.26 | convolution fusion | flops 8593080320 | bytes 20971520 | tf_op jit(solution)/shard_map/dot_general | solution.py:22
  231.6 15.8 %fusion.45.up_ref = f32[1024,4096]{1,0:T(8,128)} fusion(bf16[1024,1024]{1,0:T(8,128)(2,1)S(1)} %get-tuple-element.69, bf16[1024,4096]{1,0:T(8,128)(2,1)} %fusion.3), kind=kOutput, calls=%fused_computation.77 | convolution fusion | flops 8589934592 | bytes 27262976 | tf_op jit(solution)/shard_map/dot_general | solution.py:565
  247.4 14.4 %convolution_multiply_fusion = f32[4096,1024]{1,0:T(8,128)} fusion(bf16[1024,4096]{1,0:T(8,128)(2,1)S(1)} %bitcast.80, bf16[1,1024,1024]{2,1,0:T(8,128)(2,1)S(1)} %copy-done.59), kind=kOutput, calls=%fused_computation.17 | convolution fusion | flops 8636071936 | bytes 27262976 | tf_op jit(solution)/shard_map/dot_general | solution.py:565
  261.7 2.4 convolution_convert_fusion.2
  264.1 1.4 constant_dynamic-slice_fusion.4
  265.5 1.2 collective-permute-start.20
  267.4 4.4 convolution_multiply_fusion.1
  271.8 2.2 collective-permute-done.20.refs_11_
  274.1 5.9 collective-permute-done.19.refs_10_
  280.0 1.3 constant_dynamic-slice_fusion
  281.4 1.5 collective-permute-start.22
  283.3 61.3 %attn_bwd.2 = (bf16[1024,384]{1,0:T(8,128)(2,1)S(1)}, bf16[1024,384]{1,0:T(8,128)(2,1)}, bf16[1024,384]{1,0:T(8,128)(2,1)}, bf16[1024,384]{1,0:T(8,128)(2,1)}) custom-call(s32[8]{0:T(128)S(1)} %compare_select_fusion.tab_ref, bf16[512,768]{1,0:T(8,128)(2,1)S(1)} %copy-done.22, bf16[512,768]{1,0:T(8,128)(2,1)} %copy-done.41, bf16[512,768]{1,0:T(8,128)(2,1)} %copy-done.26, ...), custom_call_target="tpu_custom_call" | custom-call | flops 72477573120 | bytes 4194304 | tf_op jit(solution)/shard_map/attn_bwd/pallas_call | solution.py:202
  344.9 0.9 collective-permute-start.26
  345.8 0.9 collective-permute-start.28
  346.7 61.4 %attn_bwd.3 = (bf16[1024,384]{1,0:T(8,128)(2,1)S(1)}, bf16[1024,384]{1,0:T(8,128)(2,1)}, bf16[1024,384]{1,0:T(8,128)(2,1)}, bf16[1024,384]{1,0:T(8,128)(2,1)S(1)}) custom-call(s32[8]{0:T(128)S(1)} %compare_select_fusion.tab_ref, bf16[512,768]{1,0:T(8,128)(2,1)S(1)} %copy-done.22, bf16[512,768]{1,0:T(8,128)(2,1)} %copy-done.41, bf16[512,768]{1,0:T(8,128)(2,1)} %copy-done.26, ...), custom_call_target="tpu_custom_call" | custom-call | flops 72477573120 | bytes 4194304 | tf_op jit(solution)/shard_map/attn_bwd/pallas_call | solution.py:202
  408.1 0.9 copy-done.3
  409.4 0.9 collective-permute-start.27
  410.2 16.4 %qkv_grad.1.mine_ref = f32[768,1024]{1,0:T(8,128)} custom-call(bf16[1024,384]{1,0:T(8,128)(2,1)S(1)} %get-tuple-element.80.refs_0_, bf16[1024,384]{1,0:T(8,128)(2,1)} %get-tuple-element.85.refs_1_, bf16[1024,384]{1,0:T(8,128)(2,1)} %get-tuple-element.87.refs_2_, bf16[1024,384]{1,0:T(8,128)(2,1)} %get-tuple-element.89.refs_3_, ...), custom_call_target="tpu_custom_call" | custom-call | flops 6442450944 | bytes 16777216 | tf_op jit(solution)/shard_map/qkv_grad/pallas_call | solution.py:291
  426.6 315.6 %sum_grads.1 = (f32[1024,4096]{1,0:T(8,128)}, f32[3072,1024]{1,0:T(8,128)}) custom-call(f32[1024,4096]{1,0:T(8,128)} %fusion.45.up_ref, f32[768,1024]{1,0:T(8,128)} %qkv_grad.1.mine_ref), custom_call_target="tpu_custom_call" | custom-call | flops 199999995904 | bytes 67108864 | tf_op jit(solution)/shard_map/sum_grads/pallas_call | solution.py:549
  742.2 0.8 collective-permute-start.29
  743.0 11.7 %broadcast_multiply_fusion = f32[1024,4096]{1,0:T(8,128)} fusion(f32[1024,4096]{1,0:T(8,128)} %get-tuple-element.94), kind=kLoop, calls=%fused_computation.18 | loop fusion | flops 4194304 | bytes 33554432 | tf_op jit(solution)/shard_map/mul | solution.py:639
  754.8 10.3 %fusion.44 = (f32[1024,1024]{1,0:T(8,128)}, f32[1024,1024]{1,0:T(8,128)}, f32[1024,1024]{1,0:T(8,128)}) fusion(f32[3072,1024]{1,0:T(8,128)} %get-tuple-element.92), kind=kLoop, calls=%fused_computation.76 | loop fusion | bytes 25165824 | tf_op jit(solution)/shard_map/slice | solution.py:640
  765.1 12.3 %input_grad.1 = bf16[1024,1024]{1,0:T(8,128)(2,1)} custom-call(s32[5]{0:T(128)S(1)} %stack.20.rank_ref.where_ref, bf16[1024,1024]{1,0:T(8,128)(2,1)S(1)} %copy-done.25, bf16[3072,1024]{1,0:T(8,128)(2,1)} %bitcast.89, bf16[1024,384]{1,0:T(8,128)(2,1)S(1)} %copy-done.44, bf16[1024,384]{1,0:T(8,128)(2,1)S(1)} %copy-done.46, ...), custom_call_target="tpu_custom_call" | custom-call | flops 6442450944 | bytes 16777216 | tf_op jit(solution)/shard_map/input_grad/pallas_call | solution.py:256
  777.4 4.8 copy.32
  782.2 12.0 %copy.33 = f32[4096,1024]{1,0:T(8,128)} copy(f32[4096,1024]{1,0:T(8,128)} %get-tuple-element.116) | data formatting | bytes 33554432
  (169 shorter events, 8.7 us)
Async XLA Ops:
  7.2 770.3 %all-reduce.3.cloned.1.call-start = ((), (), s32[]{:S(2)}) async-start(), calls=%async_computation | async-start | bytes 41943040 | tf_op jit(solution)/shard_map/psum | solution.py:628
  10.2 48.9 %collective-permute-start.10 = (bf16[512,1024]{1,0:T(8,128)(2,1)}, bf16[512,1024]{1,0:T(8,128)(2,1)}, u32[]{:S(2)}, u32[]{:S(2)}) collective-permute-start(bf16[512,1024]{1,0:T(8,128)(2,1)} %get-tuple-element.108.refs_12_), channel_id=1, source_target_pairs={{0,2},{1,3},{2,0},{3,1},{4,6},{5,7},{6,4},{7,5},{8,10},{9,11},{10,... | collective-permute-start | bytes 3145736 | tf_op jit(solution)/shard_map/ppermute | solution.py:574
  13.2 53.9 %collective-permute-start.9 = (bf16[512,1024]{1,0:T(8,128)(2,1)}, bf16[512,1024]{1,0:T(8,128)(2,1)}, u32[]{:S(2)}, u32[]{:S(2)}) collective-permute-start(bf16[512,1024]{1,0:T(8,128)(2,1)} %get-tuple-element.108.refs_12_), channel_id=1, source_target_pairs={{0,1},{1,0},{2,3},{3,2},{4,5},{5,4},{6,7},{7,6},{8,9},{9,8},{10,11... | collective-permute-start | bytes 3145736 | tf_op jit(solution)/shard_map/ppermute | solution.py:574
  13.2 51.3 %collective-permute-start.1 = (bf16[512,1024]{1,0:T(8,128)(2,1)}, bf16[512,1024]{1,0:T(8,128)(2,1)}, u32[]{:S(2)}, u32[]{:S(2)}) collective-permute-start(bf16[512,1024]{1,0:T(8,128)(2,1)} %get-tuple-element.109.refs_8_), channel_id=1, source_target_pairs={{0,1},{1,0},{2,3},{3,2},{4,5},{5,4},{6,7},{7,6},{8,9},{9,8},{10,11... | collective-permute-start | bytes 3145736 | tf_op jit(solution)/shard_map/ppermute | solution.py:574
  13.7 45.4 %collective-permute-start = (bf16[512,1024]{1,0:T(8,128)(2,1)}, bf16[512,1024]{1,0:T(8,128)(2,1)}, u32[]{:S(2)}, u32[]{:S(2)}) collective-permute-start(bf16[512,1024]{1,0:T(8,128)(2,1)} %get-tuple-element.109.refs_8_), channel_id=1, source_target_pairs={{0,2},{1,3},{2,0},{3,1},{4,6},{5,7},{6,4},{7,5},{8,10},{9,11},{10,... | collective-permute-start | bytes 3145736 | tf_op jit(solution)/shard_map/ppermute | solution.py:574
  13.7 15.0 %copy-start.57 = (bf16[1024,16,64]{0,2,1:T(8,128)(2,1)S(1)}, bf16[1024,16,64]{0,2,1:T(8,128)(2,1)}, u32[]{:S(2)}) copy-start(bf16[1024,16,64]{0,2,1:T(8,128)(2,1)} %param.12) | copy-start | bytes 6291460
  31.8 39.8 %copy-start.55 = (bf16[8,3,128,1024]{3,2,1,0:T(8,128)(2,1)}, bf16[8,3,128,1024]{3,2,1,0:T(8,128)(2,1)S(1)}, u32[]{:S(2)}) copy-start(bf16[8,3,128,1024]{3,2,1,0:T(8,128)(2,1)S(1)} %pad_maximum_fusion) | copy-start | bytes 18874372
  32.8 114.6 %copy-start.21 = (bf16[512,768]{1,0:T(8,128)(2,1)}, bf16[512,768]{1,0:T(8,128)(2,1)S(1)}, u32[]{:S(2)}) copy-start(bf16[512,768]{1,0:T(8,128)(2,1)S(1)} %fusion.18.refs_0_) | copy-start | bytes 2359300
  33.9 67.2 %copy-start.23 = (bf16[512,768]{1,0:T(8,128)(2,1)}, bf16[512,768]{1,0:T(8,128)(2,1)S(1)}, u32[]{:S(2)}) copy-start(bf16[512,768]{1,0:T(8,128)(2,1)S(1)} %fusion.20.refs_4_) | copy-start | bytes 2359300
  59.2 12.4 %collective-permute-start.2 = (bf16[512,1024]{1,0:T(8,128)(2,1)}, bf16[512,1024]{1,0:T(8,128)(2,1)S(1)}, u32[]{:S(2)}, u32[]{:S(2)}) collective-permute-start(bf16[512,1024]{1,0:T(8,128)(2,1)} %collective-permute-done.refs_10_), channel_id=1, source_target_pairs={{0,1},{1,0},{2,3},{3,2},{4,5},{5,4},{6,7},{7,6},{8,9},{9,8},{10,11... | collective-permute-start | bytes 3145736 | tf_op jit(solution)/shard_map/ppermute | solution.py:574
  59.2 10.5 %collective-permute-start.11 = (bf16[512,1024]{1,0:T(8,128)(2,1)}, bf16[512,1024]{1,0:T(8,128)(2,1)S(1)}, u32[]{:S(2)}, u32[]{:S(2)}) collective-permute-start(bf16[512,1024]{1,0:T(8,128)(2,1)} %collective-permute-done.10.refs_14_), channel_id=1, source_target_pairs={{0,1},{1,0},{2,3},{3,2},{4,5},{5,4},{6,7},{7,6},{8,9},{9,8},{10,11... | collective-permute-start | bytes 3145736 | tf_op jit(solution)/shard_map/ppermute | solution.py:574
  61.9 85.5 %copy-start.26 = (bf16[512,768]{1,0:T(8,128)(2,1)}, bf16[512,768]{1,0:T(8,128)(2,1)S(1)}, u32[]{:S(2)}) copy-start(bf16[512,768]{1,0:T(8,128)(2,1)S(1)} %convolution_convert_fusion.8.refs_2_) | copy-start | bytes 2359300
  64.5 36.6 %copy-start.40 = (bf16[512,768]{1,0:T(8,128)(2,1)}, bf16[512,768]{1,0:T(8,128)(2,1)S(1)}, u32[]{:S(2)}) copy-start(bf16[512,768]{1,0:T(8,128)(2,1)S(1)} %fusion.22.refs_6_) | copy-start | bytes 2359300
  67.0 80.3 %copy-start.41 = (bf16[512,768]{1,0:T(8,128)(2,1)}, bf16[512,768]{1,0:T(8,128)(2,1)S(1)}, u32[]{:S(2)}) copy-start(bf16[512,768]{1,0:T(8,128)(2,1)S(1)} %fusion.19.refs_1_) | copy-start | bytes 2359300
  69.6 31.5 %copy-start.42 = (bf16[512,768]{1,0:T(8,128)(2,1)}, bf16[512,768]{1,0:T(8,128)(2,1)S(1)}, u32[]{:S(2)}) copy-start(bf16[512,768]{1,0:T(8,128)(2,1)S(1)} %fusion.21.refs_5_) | copy-start | bytes 2359300
  71.6 29.6 %copy-start.60 = (bf16[512,1024]{1,0:T(8,128)(2,1)}, bf16[512,1024]{1,0:T(8,128)(2,1)S(1)}, u32[]{:S(2)}) copy-start(bf16[512,1024]{1,0:T(8,128)(2,1)S(1)} %collective-permute-done.2.refs_11_) | copy-start | bytes 3145732
  72.6 74.8 %copy-start.27 = (bf16[512,768]{1,0:T(8,128)(2,1)}, bf16[512,768]{1,0:T(8,128)(2,1)S(1)}, u32[]{:S(2)}) copy-start(bf16[512,768]{1,0:T(8,128)(2,1)S(1)} %convolution_convert_fusion.7.refs_3_) | copy-start | bytes 2359300
  101.8 28.3 %copy-start.51 = (f32[1,2,2048]{2,1,0:T(2,128)}, f32[1,2,2048]{2,1,0:T(2,128)S(1)}, u32[]{:S(2)}) copy-start(f32[1,2,2048]{2,1,0:T(2,128)S(1)} %get-tuple-element.83.refs_21_) | copy-start | bytes 49156
  101.8 28.9 %copy-start.5 = (bf16[512,128]{1,0:T(8,128)(2,1)}, bf16[512,128]{1,0:T(8,128)(2,1)S(1)}, u32[]{:S(2)}) copy-start(bf16[512,128]{1,0:T(8,128)(2,1)S(1)} %get-tuple-element.64.refs_17_) | copy-start | bytes 393220
  101.8 29.0 %copy-start.7 = (bf16[512,128]{1,0:T(8,128)(2,1)}, bf16[512,128]{1,0:T(8,128)(2,1)S(1)}, u32[]{:S(2)}) copy-start(bf16[512,128]{1,0:T(8,128)(2,1)S(1)} %get-tuple-element.66.refs_18_) | copy-start | bytes 393220
  101.8 43.0 %copy-start.9 = (bf16[512,128]{1,0:T(8,128)(2,1)}, bf16[512,128]{1,0:T(8,128)(2,1)S(1)}, u32[]{:S(2)}) copy-start(bf16[512,128]{1,0:T(8,128)(2,1)S(1)} %get-tuple-element.68.refs_19_) | copy-start | bytes 393220
  130.7 16.3 %collective-permute-start.13 = (bf16[512,128]{1,0:T(8,128)(2,1)S(1)}, bf16[512,128]{1,0:T(8,128)(2,1)S(1)}, u32[]{:S(2)}, u32[]{:S(2)}) collective-permute-start(bf16[512,128]{1,0:T(8,128)(2,1)S(1)} %get-tuple-element.64.refs_17_), channel_id=1, source_target_pairs={{0,1},{1,0},{2,3},{3,2},{4,5},{5,4},{6,7},{7,6},{8,9},{9,8},{10,11... | collective-permute-start | bytes 393224 | tf_op jit(solution)/shard_map/ppermute | solution.py:574
  130.8 16.2 %collective-permute-start.15 = (bf16[512,128]{1,0:T(8,128)(2,1)S(1)}, bf16[512,128]{1,0:T(8,128)(2,1)S(1)}, u32[]{:S(2)}, u32[]{:S(2)}) collective-permute-start(bf16[512,128]{1,0:T(8,128)(2,1)S(1)} %get-tuple-element.66.refs_18_), channel_id=1, source_target_pairs={{0,2},{1,3},{2,0},{3,1},{4,6},{5,7},{6,4},{7,5},{8,10},{9,11},{10,... | collective-permute-start | bytes 393224 | tf_op jit(solution)/shard_map/ppermute | solution.py:574
  144.8 14.8 %collective-permute-start.17 = (bf16[512,128]{1,0:T(8,128)(2,1)S(1)}, bf16[512,128]{1,0:T(8,128)(2,1)S(1)}, u32[]{:S(2)}, u32[]{:S(2)}) collective-permute-start(bf16[512,128]{1,0:T(8,128)(2,1)S(1)} %get-tuple-element.68.refs_19_), channel_id=1, source_target_pairs={{0,3},{1,2},{2,1},{3,0},{4,7},{5,6},{6,5},{7,4},{8,11},{9,10},{10,... | collective-permute-start | bytes 393224 | tf_op jit(solution)/shard_map/ppermute | solution.py:574
  144.9 16.5 %collective-permute-start.12 = (bf16[512,128]{1,0:T(8,128)(2,1)S(1)}, bf16[512,128]{1,0:T(8,128)(2,1)S(1)}, u32[]{:S(2)}, u32[]{:S(2)}) collective-permute-start(bf16[512,128]{1,0:T(8,128)(2,1)S(1)} %get-tuple-element.63.refs_17_), channel_id=1, source_target_pairs={{0,1},{1,0},{2,3},{3,2},{4,5},{5,4},{6,7},{7,6},{8,9},{9,8},{10,11... | collective-permute-start | bytes 393224 | tf_op jit(solution)/shard_map/ppermute | solution.py:574
  145.2 16.9 %collective-permute-start.14 = (bf16[512,128]{1,0:T(8,128)(2,1)S(1)}, bf16[512,128]{1,0:T(8,128)(2,1)S(1)}, u32[]{:S(2)}, u32[]{:S(2)}) collective-permute-start(bf16[512,128]{1,0:T(8,128)(2,1)S(1)} %get-tuple-element.65.refs_18_), channel_id=1, source_target_pairs={{0,2},{1,3},{2,0},{3,1},{4,6},{5,7},{6,4},{7,5},{8,10},{9,11},{10,... | collective-permute-start | bytes 393224 | tf_op jit(solution)/shard_map/ppermute | solution.py:574
  147.0 16.2 %collective-permute-start.16 = (bf16[512,128]{1,0:T(8,128)(2,1)S(1)}, bf16[512,128]{1,0:T(8,128)(2,1)S(1)}, u32[]{:S(2)}, u32[]{:S(2)}) collective-permute-start(bf16[512,128]{1,0:T(8,128)(2,1)S(1)} %get-tuple-element.67.refs_19_), channel_id=1, source_target_pairs={{0,3},{1,2},{2,1},{3,0},{4,7},{5,6},{6,5},{7,4},{8,11},{9,10},{10,... | collective-permute-start | bytes 393224 | tf_op jit(solution)/shard_map/ppermute | solution.py:574
  147.0 18.6 %collective-permute-start.4 = (bf16[512,128]{1,0:T(8,128)(2,1)S(1)}, bf16[512,128]{1,0:T(8,128)(2,1)S(1)}, u32[]{:S(2)}, u32[]{:S(2)}) collective-permute-start(bf16[512,128]{1,0:T(8,128)(2,1)S(1)} %get-tuple-element.56.refs_13_), channel_id=1, source_target_pairs={{0,1},{1,0},{2,3},{3,2},{4,5},{5,4},{6,7},{7,6},{8,9},{9,8},{10,11... | collective-permute-start | bytes 393224 | tf_op jit(solution)/shard_map/ppermute | solution.py:574
  159.7 6.6 collective-permute-start.6
  162.1 6.0 collective-permute-start.8
  162.8 5.4 collective-permute-start.3
  163.8 7.4 collective-permute-start.5
  166.2 7.4 collective-permute-start.7
  182.4 19.6 %slice-start = ((s8[8388608]{0:T(1024)(128)(4,1)}), s8[4194304]{0:T(1024)(128)(4,1)S(1)}, s32[]{:S(2)}) async-start(s8[8388608]{0:T(1024)(128)(4,1)} %bitcast.77), calls=%async_computation.1 | async-start | bytes 8388608
  187.3 14.8 %slice-start.1 = ((s8[8388608]{0:T(1024)(128)(4,1)}), s8[4194304]{0:T(1024)(128)(4,1)S(1)}, s32[]{:S(2)}) async-start(s8[8388608]{0:T(1024)(128)(4,1)} %bitcast.77), calls=%async_computation.2 | async-start | bytes 8388608
  202.1 15.5 %copy-start.58 = (bf16[1,1024,1024]{2,1,0:T(8,128)(2,1)S(1)}, bf16[1,1024,1024]{2,1,0:T(8,128)(2,1)}, u32[]{:S(2)}) copy-start(bf16[1,1024,1024]{2,1,0:T(8,128)(2,1)} %param.9) | copy-start | bytes 6291460
  202.1 45.2 %slice-start.2 = ((s8[8388608]{0:T(1024)(128)(4,1)}), s8[4194304]{0:T(1024)(128)(4,1)S(1)}, s32[]{:S(2)}) async-start(s8[8388608]{0:T(1024)(128)(4,1)} %bitcast.79), calls=%async_computation.3 | async-start | bytes 8388608
  217.6 29.7 %slice-start.3 = ((s8[8388608]{0:T(1024)(128)(4,1)}), s8[4194304]{0:T(1024)(128)(4,1)S(1)}, s32[]{:S(2)}) async-start(s8[8388608]{0:T(1024)(128)(4,1)} %bitcast.79), calls=%async_computation.4 | async-start | bytes 8388608
  231.5 35.9 %copy-start.24 = (bf16[1024,1024]{1,0:T(8,128)(2,1)}, bf16[1024,1024]{1,0:T(8,128)(2,1)S(1)}, u32[]{:S(2)}) copy-start(bf16[1024,1024]{1,0:T(8,128)(2,1)S(1)} %add_convert_fusion.base_ref) | copy-start | bytes 6291460
  231.5 15.8 %copy-start.59 = (bf16[1,1024,1024]{2,1,0:T(8,128)(2,1)S(1)}, bf16[1,1024,1024]{2,1,0:T(8,128)(2,1)}, u32[]{:S(2)}) copy-start(bf16[1,1024,1024]{2,1,0:T(8,128)(2,1)} %param.9) | copy-start | bytes 6291460
  247.3 14.4 %copy-start.2 = (bf16[16,64,1024]{2,1,0:T(8,128)(2,1)S(1)}, bf16[16,64,1024]{2,1,0:T(8,128)(2,1)}, u32[]{:S(2)}) copy-start(bf16[16,64,1024]{2,1,0:T(8,128)(2,1)} %param.13) | copy-start | bytes 6291460
  265.5 8.5 %collective-permute-start.20 = (bf16[1024,128]{1,0:T(8,128)(2,1)}, bf16[1024,128]{1,0:T(8,128)(2,1)S(1)}, u32[]{:S(2)}, u32[]{:S(2)}) collective-permute-start(bf16[1024,128]{1,0:T(8,128)(2,1)} %get-tuple-element.104), channel_id=1, source_target_pairs={{0,3},{1,2},{2,1},{3,0},{4,7},{5,6},{6,5},{7,4},{8,11},{9,10},{10,... | collective-permute-start | bytes 786440 | tf_op jit(solution)/shard_map/ppermute | solution.py:574
  266.7 13.2 %collective-permute-start.19 = (bf16[1024,128]{1,0:T(8,128)(2,1)}, bf16[1024,128]{1,0:T(8,128)(2,1)S(1)}, u32[]{:S(2)}, u32[]{:S(2)}) collective-permute-start(bf16[1024,128]{1,0:T(8,128)(2,1)} %get-tuple-element.105), channel_id=1, source_target_pairs={{0,2},{1,3},{2,0},{3,1},{4,6},{5,7},{6,4},{7,5},{8,10},{9,11},{10,... | collective-permute-start | bytes 786440 | tf_op jit(solution)/shard_map/ppermute | solution.py:574
  267.3 12.7 %collective-permute-start.18 = (bf16[1024,128]{1,0:T(8,128)(2,1)S(1)}, bf16[1024,128]{1,0:T(8,128)(2,1)S(1)}, u32[]{:S(2)}, u32[]{:S(2)}) collective-permute-start(bf16[1024,128]{1,0:T(8,128)(2,1)S(1)} %get-tuple-element.106), channel_id=1, source_target_pairs={{0,1},{1,0},{2,3},{3,2},{4,5},{5,4},{6,7},{7,6},{8,9},{9,8},{10,11... | collective-permute-start | bytes 786440 | tf_op jit(solution)/shard_map/ppermute | solution.py:574
  281.3 64.4 %collective-permute-start.23 = (bf16[1024,128]{1,0:T(8,128)(2,1)S(1)}, bf16[1024,128]{1,0:T(8,128)(2,1)S(1)}, u32[]{:S(2)}, u32[]{:S(2)}) collective-permute-start(bf16[1024,128]{1,0:T(8,128)(2,1)S(1)} %get-tuple-element.100), channel_id=1, source_target_pairs={{0,3},{1,2},{2,1},{3,0},{4,7},{5,6},{6,5},{7,4},{8,11},{9,10},{10,... | collective-permute-start | bytes 786440 | tf_op jit(solution)/shard_map/ppermute | solution.py:574
  281.4 65.2 %collective-permute-start.22 = (bf16[1024,128]{1,0:T(8,128)(2,1)S(1)}, bf16[1024,128]{1,0:T(8,128)(2,1)S(1)}, u32[]{:S(2)}, u32[]{:S(2)}) collective-permute-start(bf16[1024,128]{1,0:T(8,128)(2,1)S(1)} %get-tuple-element.101), channel_id=1, source_target_pairs={{0,2},{1,3},{2,0},{3,1},{4,6},{5,7},{6,4},{7,5},{8,10},{9,11},{10,... | collective-permute-start | bytes 786440 | tf_op jit(solution)/shard_map/ppermute | solution.py:574
  282.9 63.7 %collective-permute-start.21 = (bf16[1024,128]{1,0:T(8,128)(2,1)S(1)}, bf16[1024,128]{1,0:T(8,128)(2,1)S(1)}, u32[]{:S(2)}, u32[]{:S(2)}) collective-permute-start(bf16[1024,128]{1,0:T(8,128)(2,1)S(1)} %get-tuple-element.102), channel_id=1, source_target_pairs={{0,1},{1,0},{2,3},{3,2},{4,5},{5,4},{6,7},{7,6},{8,9},{9,8},{10,11... | collective-permute-start | bytes 786440 | tf_op jit(solution)/shard_map/ppermute | solution.py:574
  283.3 63.4 %copy-start.6 = (bf16[512,128]{1,0:T(8,128)(2,1)S(1)}, bf16[512,128]{1,0:T(8,128)(2,1)}, u32[]{:S(2)}) copy-start(bf16[512,128]{1,0:T(8,128)(2,1)} %copy-done.5) | copy-start | bytes 393220
  283.3 63.4 %copy-start.8 = (bf16[512,128]{1,0:T(8,128)(2,1)S(1)}, bf16[512,128]{1,0:T(8,128)(2,1)}, u32[]{:S(2)}) copy-start(bf16[512,128]{1,0:T(8,128)(2,1)} %copy-done.7) | copy-start | bytes 393220
  283.3 63.4 %copy-start.10 = (bf16[512,128]{1,0:T(8,128)(2,1)S(1)}, bf16[512,128]{1,0:T(8,128)(2,1)}, u32[]{:S(2)}) copy-start(bf16[512,128]{1,0:T(8,128)(2,1)} %copy-done.9) | copy-start | bytes 393220
  283.3 63.4 %copy-start.12 = (bf16[512,128]{1,0:T(8,128)(2,1)S(1)}, bf16[512,128]{1,0:T(8,128)(2,1)}, u32[]{:S(2)}) copy-start(bf16[512,128]{1,0:T(8,128)(2,1)} %copy-done.11) | copy-start | bytes 393220
  283.3 63.4 %copy-start.30 = (bf16[512,128]{1,0:T(8,128)(2,1)S(1)}, bf16[512,128]{1,0:T(8,128)(2,1)}, u32[]{:S(2)}) copy-start(bf16[512,128]{1,0:T(8,128)(2,1)} %copy-done.28) | copy-start | bytes 393220
  283.3 63.4 %copy-start.33 = (bf16[512,128]{1,0:T(8,128)(2,1)S(1)}, bf16[512,128]{1,0:T(8,128)(2,1)}, u32[]{:S(2)}) copy-start(bf16[512,128]{1,0:T(8,128)(2,1)} %copy-done.31) | copy-start | bytes 393220
  283.3 63.4 %copy-start.48 = (f32[1,2,2048]{2,1,0:T(2,128)S(1)}, f32[1,2,2048]{2,1,0:T(2,128)}, u32[]{:S(2)}) copy-start(f32[1,2,2048]{2,1,0:T(2,128)} %copy-done.47) | copy-start | bytes 49156
  283.3 63.4 %copy-start.52 = (f32[1,2,2048]{2,1,0:T(2,128)S(1)}, f32[1,2,2048]{2,1,0:T(2,128)}, u32[]{:S(2)}) copy-start(f32[1,2,2048]{2,1,0:T(2,128)} %copy-done.51) | copy-start | bytes 49156
  344.7 65.6 %copy-start.43 = (bf16[1024,384]{1,0:T(8,128)(2,1)}, bf16[1024,384]{1,0:T(8,128)(2,1)S(1)}, u32[]{:S(2)}) copy-start(bf16[1024,384]{1,0:T(8,128)(2,1)S(1)} %get-tuple-element.80.refs_0_) | copy-start | bytes 2359300
  344.7 397.5 %collective-permute-start.24 = (bf16[1024,384]{1,0:T(8,128)(2,1)}, bf16[1024,384]{1,0:T(8,128)(2,1)}, u32[]{:S(2)}, u32[]{:S(2)}) collective-permute-start(bf16[1024,384]{1,0:T(8,128)(2,1)} %get-tuple-element.85.refs_1_), channel_id=1, source_target_pairs={{0,1},{1,0},{2,3},{3,2},{4,5},{5,4},{6,7},{7,6},{8,9},{9,8},{10,11... | collective-permute-start | bytes 2359304 | tf_op jit(solution)/shard_map/ppermute | solution.py:574
  344.9 420.1 %collective-permute-start.26 = (bf16[1024,384]{1,0:T(8,128)(2,1)}, bf16[1024,384]{1,0:T(8,128)(2,1)}, u32[]{:S(2)}, u32[]{:S(2)}) collective-permute-start(bf16[1024,384]{1,0:T(8,128)(2,1)} %get-tuple-element.87.refs_2_), channel_id=1, source_target_pairs={{0,2},{1,3},{2,0},{3,1},{4,6},{5,7},{6,4},{7,5},{8,10},{9,11},{10,... | collective-permute-start | bytes 2359304 | tf_op jit(solution)/shard_map/ppermute | solution.py:574
  345.8 419.3 %collective-permute-start.28 = (bf16[1024,384]{1,0:T(8,128)(2,1)}, bf16[1024,384]{1,0:T(8,128)(2,1)}, u32[]{:S(2)}, u32[]{:S(2)}) collective-permute-start(bf16[1024,384]{1,0:T(8,128)(2,1)} %get-tuple-element.89.refs_3_), channel_id=1, source_target_pairs={{0,3},{1,2},{2,1},{3,0},{4,7},{5,6},{6,5},{7,4},{8,11},{9,10},{10,... | collective-permute-start | bytes 2359304 | tf_op jit(solution)/shard_map/ppermute | solution.py:574
  409.0 17.6 %copy-start.45 = (bf16[1024,384]{1,0:T(8,128)(2,1)}, bf16[1024,384]{1,0:T(8,128)(2,1)S(1)}, u32[]{:S(2)}) copy-start(bf16[1024,384]{1,0:T(8,128)(2,1)S(1)} %get-tuple-element.84.refs_1_.refs_4_) | copy-start | bytes 2359300
  409.0 356.1 %collective-permute-start.25 = (bf16[1024,384]{1,0:T(8,128)(2,1)}, bf16[1024,384]{1,0:T(8,128)(2,1)}, u32[]{:S(2)}, u32[]{:S(2)}) collective-permute-start(bf16[1024,384]{1,0:T(8,128)(2,1)} %get-tuple-element.86.refs_5_), channel_id=1, source_target_pairs={{0,1},{1,0},{2,3},{3,2},{4,5},{5,4},{6,7},{7,6},{8,9},{9,8},{10,11... | collective-permute-start | bytes 2359304 | tf_op jit(solution)/shard_map/ppermute | solution.py:574
  409.4 355.7 %collective-permute-start.27 = (bf16[1024,384]{1,0:T(8,128)(2,1)}, bf16[1024,384]{1,0:T(8,128)(2,1)}, u32[]{:S(2)}, u32[]{:S(2)}) collective-permute-start(bf16[1024,384]{1,0:T(8,128)(2,1)} %get-tuple-element.88.refs_6_), channel_id=1, source_target_pairs={{0,2},{1,3},{2,0},{3,1},{4,6},{5,7},{6,4},{7,5},{8,10},{9,11},{10,... | collective-permute-start | bytes 2359304 | tf_op jit(solution)/shard_map/ppermute | solution.py:574
  426.6 315.6 %copy-start.4 = (bf16[1024,384]{1,0:T(8,128)(2,1)S(1)}, bf16[1024,384]{1,0:T(8,128)(2,1)}, u32[]{:S(2)}) copy-start(bf16[1024,384]{1,0:T(8,128)(2,1)} %copy-done.3) | copy-start | bytes 2359300
  742.2 22.8 %collective-permute-start.29 = (bf16[1024,384]{1,0:T(8,128)(2,1)S(1)}, bf16[1024,384]{1,0:T(8,128)(2,1)S(1)}, u32[]{:S(2)}, u32[]{:S(2)}) collective-permute-start(bf16[1024,384]{1,0:T(8,128)(2,1)S(1)} %copy-done.4), channel_id=1, source_target_pairs={{0,3},{1,2},{2,1},{3,0},{4,7},{5,6},{6,5},{7,4},{8,11},{9,10},{10,... | collective-permute-start | bytes 2359304 | tf_op jit(solution)/shard_map/ppermute | solution.py:574
  (33 other events, 143.4 us)
Sparse Core Ops, SparseCore 0:
  272.0 455.7 all-reduce.2
